TPU v7x, 512 devices: a whole 4x4x16 slice. The times are simulated.
512 devices in a mesh: rows: 128 (over z, y, core), cols: 4 (over x).
Axes of the slice: x: 4, y: 4, z: 16, core: 2. Of those that a mesh axis runs over, the one named last changes fastest.
Arguments:
- blocks: bfloat16 [512, 4, 3, 128, 128], P('rows', 'cols'), may hold values from -1.1953125 to 1.1953125
- block_cols: int32 [512, 4, 3], P('rows', 'cols'), may hold values from 0 to 511, as said below
Outputs:
- square_blocks: bfloat16 [512, 4, 36, 128, 128], P('rows', 'cols')
- square_cols: int32 [512, 4, 36], P('rows', 'cols')
- square_start: int32 [512, 4], P('rows', 'cols')
Inputs may be any that keep to these rules, and one draw needn't show every extreme that they name: Block-row i lies in panel p = i // 4; every block_cols[i, g, s] is a block-column congruent to g modulo 4 among block-rows 4 * (p - 4) to 4 * (p + 4) - 1, taken modulo 512; the three entries of one group differ; the block-columns i - 1, i and i + 1 (modulo 512) are always among a row's entries.
All inputs are finite; a program needn't handle non-finite values.
Results may differ from a plain program's by a relative error of at most 0.001.
Values may be sent and summed in bfloat16 or wider, within the bound.
No kernel may reach another device: no remote copies, remote signals or barrier semaphores. Data moves between devices by JAX's collectives and lax.ppermute only.
A program may use at most 64 MiB of HBM per device.

v0:
```python
import jax
import jax.numpy as jnp
from jax import lax
from jax.sharding import Mesh
from jax.sharding import PartitionSpec as P

HP = 4
ROWS = ("rows_0", "rows_1", "rows_2")


def sent_to_all(shard, axis):
    size = lax.axis_size(axis)
    return lax.all_to_all(
        jnp.broadcast_to(shard[None], (size, *shard.shape)), axis, 0, 0, tiled=True
    )


def in_order(parts, dim):
    lengths = list(parts.shape[1:])
    lengths[dim] *= parts.shape[0]
    return jnp.moveaxis(parts, 0, dim).reshape(lengths)


def collect(shard, axis, dim):
    parts = sent_to_all(shard, axis)
    return in_order(parts, dim)


def shifted(block, axis, distance):
    devices = range(lax.axis_size(axis))
    route = [((i - distance) % len(devices), i) for i in devices]
    return lax.ppermute(block, axis, route)


def stacked_from(shard, axes, sequence):
    parts = shard[None]
    for k in sequence:
        parts = lax.all_gather(parts, axes[k], axis=0, tiled=True)
    current = [lax.axis_size(axes[k]) for k in reversed(sequence)]
    parts = parts.reshape(*current, *shard.shape)
    turned = sorted(range(len(sequence)), key=lambda place: sequence[len(sequence) - 1 - place])
    return parts.transpose(*turned, *range(len(sequence), parts.ndim)).reshape(-1, *shard.shape)


def whole_of(shard, axes, sequence, dim):
    return in_order(stacked_from(shard, axes, sequence), dim)


def unique_slots(candidates):
    width = candidates.shape[-1]
    ordered = jnp.sort(candidates, axis=-1)
    firsts = jnp.concatenate(
        [jnp.ones(ordered.shape[:-1] + (1,), dtype=bool), ordered[..., 1:] != ordered[..., :-1]],
        axis=-1,
    )
    marks = firsts.astype(jnp.int32)
    totals = jnp.sum(marks, axis=-1)
    ranking = jnp.sum(
        marks[..., None, :] * (ordered[..., None, :] < candidates[..., :, None]).astype(jnp.int32),
        axis=-1,
    )
    places = jnp.cumsum(marks, axis=-1) - 1
    slot_ids = jnp.arange(width, dtype=jnp.int32)
    chosen = (places[..., None, :] == slot_ids[:, None]) & firsts[..., None, :]
    columns = jnp.sum(jnp.where(chosen, ordered[..., None, :], 0), axis=-1).astype(jnp.int32)
    columns = jnp.where(slot_ids < totals[..., None], columns, -1)
    onehot = (ranking[..., None, :] == slot_ids[:, None]).astype(jnp.float32)
    return (columns, onehot, totals)


def on_device(blocks, block_cols):
    panel_rows = block_cols.shape[0]
    per_group = block_cols.shape[2]
    block_size = blocks.shape[-1]
    cycle_size = lax.axis_size(ROWS)
    block_rows = panel_rows * cycle_size
    panel_id = lax.axis_index(ROWS)
    left_vals, left_cols = (collect(blocks, "cols", 1), collect(block_cols, "cols", 1))
    groups = left_cols.shape[1]
    row_slots = groups * per_group
    left_vals = left_vals.reshape(panel_rows, row_slots, block_size, block_size)
    left_cols = left_cols.reshape(panel_rows, row_slots)
    own_panel = (blocks[:, 0], block_cols[:, 0])
    pieces = []
    for offset in range(-HP, HP):
        if offset == 0:
            pieces.append(own_panel)
        else:
            pieces.append(shifted((own_panel[0], own_panel[1]), ROWS, -offset))
    win_vals = jnp.concatenate([piece[0] for piece in pieces], axis=0)
    win_cols = jnp.concatenate([piece[1] for piece in pieces], axis=0)
    window_base = (panel_id - HP) * panel_rows % block_rows
    local_index = ((left_cols - window_base) % block_rows).astype(jnp.int32)
    right_vals = win_vals[local_index]
    right_cols = win_cols[local_index]
    products = jnp.einsum(
        "ptab,ptsbc->ptsac", left_vals, right_vals, preferred_element_type=jnp.float32
    )
    candidates = right_cols.reshape(panel_rows, row_slots * per_group)
    columns, onehot, totals = unique_slots(candidates)
    merged = jnp.einsum(
        "poq,pqac->poac",
        onehot,
        products.reshape(panel_rows, row_slots * per_group, block_size, block_size),
        precision=lax.Precision.HIGHEST,
    )
    merged_blocks = merged.astype(jnp.bfloat16)
    panel_total = jnp.sum(totals)
    all_totals = whole_of(panel_total.reshape(1), (("rows_0", "rows_1"), "rows_2"), (0, 1), 0)
    earlier = jnp.sum(jnp.where(jnp.arange(cycle_size, dtype=jnp.int32) < panel_id, all_totals, 0))
    starts = earlier + jnp.cumsum(totals) - totals
    return (merged_blocks[:, None], columns[:, None], starts[:, None])


def solution(mesh):
    split = Mesh(
        mesh.devices.reshape(16, 4, 2, mesh.shape["cols"]), ("rows_0", "rows_1", "rows_2", "cols")
    )
    return jax.shard_map(
        on_device,
        mesh=split,
        in_specs=(P(ROWS, "cols", None, None, None), P(ROWS, "cols", None)),
        out_specs=(P(ROWS, "cols", None, None, None), P(ROWS, "cols", None), P(ROWS, "cols")),
        check_vma=False,
    )
```

profile of v0, /device:TPU:1, one launch (start us, length us, event | category | flops | bytes accessed | tf_op | source)
XLA Modules:
  0.0 164.1 jit_solution(924323540875775555)
XLA Ops:
  1.5 14.9 %collective-permute-start.6 = (s32[4,3]{1,0:T(4,128)S(1)}, s32[4,3]{1,0:T(4,128)S(1)}, u32[]{:S(2)}, u32[]{:S(2)}) collective-permute-start(s32[4,3]{1,0:T(4,128)S(1)} %bitcast.52), channel_id=1, source_target_pairs={{12,0},{16,4},{20,8},{24,12},{28,16},{32,20},{36,24},{40,28},{44,3... | collective-permute-start | bytes 152 | tf_op jit(solution)/shard_map/ppermute | solution.py:32
  16.4 2.4 %collective-permute-start.5 = (s32[4,3]{1,0:T(4,128)S(1)}, s32[4,3]{1,0:T(4,128)S(1)}, u32[]{:S(2)}, u32[]{:S(2)}) collective-permute-start(s32[4,3]{1,0:T(4,128)S(1)} %bitcast.53), channel_id=1, source_target_pairs={{8,0},{12,4},{16,8},{20,12},{24,16},{28,20},{32,24},{36,28},{40,32... | collective-permute-start | bytes 152 | tf_op jit(solution)/shard_map/ppermute | solution.py:32
  18.8 2.5 %collective-permute-start.4 = (s32[4,3]{1,0:T(4,128)S(1)}, s32[4,3]{1,0:T(4,128)S(1)}, u32[]{:S(2)}, u32[]{:S(2)}) collective-permute-start(s32[4,3]{1,0:T(4,128)S(1)} %bitcast.54), channel_id=1, source_target_pairs={{4,0},{8,4},{12,8},{16,12},{20,16},{24,20},{28,24},{32,28},{36,32}... | collective-permute-start | bytes 152 | tf_op jit(solution)/shard_map/ppermute | solution.py:32
  21.3 3.0 %collective-permute-start.3 = (s32[4,3]{1,0:T(4,128)S(1)}, s32[4,3]{1,0:T(4,128)S(1)}, u32[]{:S(2)}, u32[]{:S(2)}) collective-permute-start(s32[4,3]{1,0:T(4,128)S(1)} %bitcast.55), channel_id=1, source_target_pairs={{508,0},{0,4},{4,8},{8,12},{12,16},{16,20},{20,24},{24,28},{28,32}... | collective-permute-start | bytes 152 | tf_op jit(solution)/shard_map/ppermute | solution.py:32
  24.4 2.9 %collective-permute-start.2 = (s32[4,3]{1,0:T(4,128)S(1)}, s32[4,3]{1,0:T(4,128)S(1)}, u32[]{:S(2)}, u32[]{:S(2)}) collective-permute-start(s32[4,3]{1,0:T(4,128)S(1)} %bitcast.56), channel_id=1, source_target_pairs={{504,0},{508,4},{0,8},{4,12},{8,16},{12,20},{16,24},{20,28},{24,32... | collective-permute-start | bytes 152 | tf_op jit(solution)/shard_map/ppermute | solution.py:32
  28.6 4.0 %all-to-all-start = ((s32[4,4,1,3]{1,2,3,0:T(1,128)}), s32[4,4,1,3]{1,2,3,0:T(1,128)S(1)}, u32[]{:S(2)}, u32[]{:S(2)}) async-start(s32[4,4,1,3]{1,2,3,0:T(1,128)} %broadcast_in_dim.14), calls=%async_computation | async-start | bytes 12288 | tf_op jit(solution)/shard_map/all_to_all | solution.py:13
  32.6 1.3 dynamic-slice.1
  33.8 1.3 dynamic-slice
  35.8 2.5 %collective-permute-start.1 = (s32[4,3]{1,0:T(4,128)S(1)}, s32[4,3]{1,0:T(4,128)S(1)}, u32[]{:S(2)}, u32[]{:S(2)}) collective-permute-start(s32[4,3]{1,0:T(4,128)S(1)} %bitcast.57), channel_id=1, source_target_pairs={{500,0},{504,4},{508,8},{0,12},{4,16},{8,20},{12,24},{16,28},{20,3... | collective-permute-start | bytes 152 | tf_op jit(solution)/shard_map/ppermute | solution.py:32
  38.3 1.9 %collective-permute-start = (s32[4,3]{1,0:T(4,128)S(1)}, s32[4,3]{1,0:T(4,128)S(1)}, u32[]{:S(2)}, u32[]{:S(2)}) collective-permute-start(s32[4,3]{1,0:T(4,128)S(1)} %bitcast.58), channel_id=1, source_target_pairs={{496,0},{500,4},{504,8},{508,12},{0,16},{4,20},{8,24},{12,28},{16,... | collective-permute-start | bytes 152 | tf_op jit(solution)/shard_map/ppermute | solution.py:32
  40.3 6.6 %collective-permute-start.13 = (bf16[4,3,128,128]{3,2,1,0:T(8,128)(2,1)}, bf16[4,3,128,128]{3,2,1,0:T(8,128)(2,1)}, u32[]{:S(2)}, u32[]{:S(2)}) collective-permute-start(bf16[4,3,128,128]{3,2,1,0:T(8,128)(2,1)} %bitcast.44), channel_id=1, source_target_pairs={{12,0},{16,4},{20,8},{24,12},{28,16},{32,20},{36,24},{40,28},{44,3... | collective-permute-start | bytes 1179656 | tf_op jit(solution)/shard_map/ppermute | solution.py:32
  46.9 2.5 %collective-permute-start.10 = (bf16[4,3,128,128]{3,2,1,0:T(8,128)(2,1)}, bf16[4,3,128,128]{3,2,1,0:T(8,128)(2,1)}, u32[]{:S(2)}, u32[]{:S(2)}) collective-permute-start(bf16[4,3,128,128]{3,2,1,0:T(8,128)(2,1)} %bitcast.45), channel_id=1, source_target_pairs={{508,0},{0,4},{4,8},{8,12},{12,16},{16,20},{20,24},{24,28},{28,32}... | collective-permute-start | bytes 1179656 | tf_op jit(solution)/shard_map/ppermute | solution.py:32
  49.4 1.9 %collective-permute-start.9 = (bf16[4,3,128,128]{3,2,1,0:T(8,128)(2,1)}, bf16[4,3,128,128]{3,2,1,0:T(8,128)(2,1)}, u32[]{:S(2)}, u32[]{:S(2)}) collective-permute-start(bf16[4,3,128,128]{3,2,1,0:T(8,128)(2,1)} %bitcast.46), channel_id=1, source_target_pairs={{504,0},{508,4},{0,8},{4,12},{8,16},{12,20},{16,24},{20,28},{24,32... | collective-permute-start | bytes 1179656 | tf_op jit(solution)/shard_map/ppermute | solution.py:32
  51.4 1.9 %collective-permute-start.8 = (bf16[4,3,128,128]{3,2,1,0:T(8,128)(2,1)}, bf16[4,3,128,128]{3,2,1,0:T(8,128)(2,1)}, u32[]{:S(2)}, u32[]{:S(2)}) collective-permute-start(bf16[4,3,128,128]{3,2,1,0:T(8,128)(2,1)} %bitcast.47), channel_id=1, source_target_pairs={{500,0},{504,4},{508,8},{0,12},{4,16},{8,20},{12,24},{16,28},{20,3... | collective-permute-start | bytes 1179656 | tf_op jit(solution)/shard_map/ppermute | solution.py:32
  53.3 1.9 %collective-permute-start.7 = (bf16[4,3,128,128]{3,2,1,0:T(8,128)(2,1)}, bf16[4,3,128,128]{3,2,1,0:T(8,128)(2,1)S(1)}, u32[]{:S(2)}, u32[]{:S(2)}) collective-permute-start(bf16[4,3,128,128]{3,2,1,0:T(8,128)(2,1)} %bitcast.48), channel_id=1, source_target_pairs={{496,0},{500,4},{504,8},{508,12},{0,16},{4,20},{8,24},{12,28},{16,... | collective-permute-start | bytes 1179656 | tf_op jit(solution)/shard_map/ppermute | solution.py:32
  55.3 2.5 %broadcast_in_dim.15 = bf16[4,4,1,3,128,128]{5,4,3,1,2,0:T(8,128)(2,1)} broadcast(bf16[4,3,128,128]{3,2,1,0:T(8,128)(2,1)} %bitcast.49), dimensions={1,3,4,5} | broadcast | bytes 1966080 | tf_op jit(solution)/shard_map/broadcast_in_dim | solution.py:14
  57.9 4.5 %all-to-all-start.1 = ((bf16[4,4,1,3,128,128]{5,4,3,1,2,0:T(8,128)(2,1)}), bf16[4,4,1,3,128,128]{5,4,3,1,2,0:T(8,128)(2,1)}, u32[]{:S(2)}, u32[]{:S(2)}) async-start(bf16[4,4,1,3,128,128]{5,4,3,1,2,0:T(8,128)(2,1)} %broadcast_in_dim.15), calls=%async_computation.1 | async-start | bytes 3145728 | tf_op jit(solution)/shard_map/all_to_all | solution.py:13
  65.6 1.3 select_reduce_fusion
  67.0 1.4 dynamic-update-slice
  68.4 29.0 %all-reduce.1 = s32[64]{0:T(128)S(1)} all-reduce(s32[64]{0:T(128)S(1)} %dynamic-update-slice), channel_id=1, replica_groups=mesh['rows_0'=16,'rows_1'=4,'rows_2'=2,'cols'=4] {'rows_0','rows_1'}, use_global_device_ids=true, to_apply=%add.1 | all-reduce | flops 64 | bytes 512
  97.6 5.8 %all-reduce.2 = s32[128]{0:T(128)S(1)} all-reduce(s32[128]{0:T(128)S(1)} %dynamic-update-slice.1), channel_id=1, replica_groups=mesh['rows_0'=16,'rows_1'=4,'rows_2'=2,'cols'=4] {'rows_2'}, use_global_device_ids=true, to_apply=%add.2 | all-reduce | flops 128 | bytes 1024
  104.3 1.2 add_subtract_fusion
  106.9 5.9 %collective-permute-start.12 = (bf16[4,3,128,128]{3,2,1,0:T(8,128)(2,1)S(1)}, bf16[4,3,128,128]{3,2,1,0:T(8,128)(2,1)S(1)}, u32[]{:S(2)}, u32[]{:S(2)}) collective-permute-start(bf16[4,3,128,128]{3,2,1,0:T(8,128)(2,1)S(1)} %bitcast.50), channel_id=1, source_target_pairs={{8,0},{12,4},{16,8},{20,12},{24,16},{28,20},{32,24},{36,28},{40,32... | collective-permute-start | bytes 1179656 | tf_op jit(solution)/shard_map/ppermute | solution.py:32
  113.9 2.7 %collective-permute-start.11 = (bf16[4,3,128,128]{3,2,1,0:T(8,128)(2,1)S(1)}, bf16[4,3,128,128]{3,2,1,0:T(8,128)(2,1)S(1)}, u32[]{:S(2)}, u32[]{:S(2)}) collective-permute-start(bf16[4,3,128,128]{3,2,1,0:T(8,128)(2,1)S(1)} %bitcast.51), channel_id=1, source_target_pairs={{4,0},{8,4},{12,8},{16,12},{20,16},{24,20},{28,24},{32,28},{36,32}... | collective-permute-start | bytes 1179656 | tf_op jit(solution)/shard_map/ppermute | solution.py:32
  119.8 5.6 %collective-permute-done.11 = bf16[4,3,128,128]{3,2,1,0:T(8,128)(2,1)S(1)} collective-permute-done((bf16[4,3,128,128]{3,2,1,0:T(8,128)(2,1)S(1)}, bf16[4,3,128,128]{3,2,1,0:T(8,128)(2,1)S(1)}, u32[]{:S(2)}, u32[]{:S(2)}) %collective-permute-start.11) | collective-permute-done | bytes 393248 | tf_op jit(solution)/shard_map/ppermute | solution.py:32
  125.6 1.0 constant_dynamic-update-slice_fusion
  126.6 3.5 %gather_fusion.1 = bf16[48,3,128,128]{3,2,1,0:T(8,128)(2,1)} fusion(bf16[32,3,128,128]{3,2,1,0:T(8,128)(2,1)S(1)} %constant_dynamic-update-slice_fusion, s32[1024]{0:T(1024)S(1)} %pad_clamp_fusion), kind=kCustom, calls=%fused_computation.1 | custom fusion | bytes 9437376 | tf_op jit(solution)/shard_map/gather | solution.py:94
  130.1 1.6 copy.47
  131.7 7.4 %fusion.6 = f32[4,12,3,128,128]{4,3,2,1,0:T(8,128)} fusion(bf16[4,12,3,128,128]{4,3,2,1,0:T(8,128)(2,1)} %bitcast.42, bf16[4,12,128,128,1]{3,2,4,1,0:T(8,128)(2,1)S(1)} %bitcast.43), kind=kOutput, calls=%fused_computation.36 | convolution fusion | flops 603979776 | bytes 15728640 | tf_op jit(solution)/shard_map/ptab,ptsbc->ptsac/dot_general | solution.py:96
  139.1 12.0 %copy.49 = f32[4,36,128,128]{3,1,2,0:T(8,128)} copy(f32[4,36,128,128]{2,3,1,0:T(8,128)} %bitcast.41) | data formatting | bytes 18874368 | tf_op jit(solution)/shard_map/reshape | solution.py:104
  151.1 9.6 %convert_bitcast_fusion = bf16[4,1,36,128,128]{4,2,3,0,1:T(8,128)(2,1)S(1)} fusion(f32[4,36,128,128]{3,1,2,0:T(8,128)} %copy.49, s32[4,36]{1,0:T(4,128)S(1)} %copy.46), kind=kOutput, calls=%fused_computation.2 | convolution fusion | flops 1021580352 | bytes 14156352 | tf_op jit(solution)/shard_map/poq,pqac->poac/dot_general | solution.py:101
  160.7 3.4 %copy.52 = bf16[4,1,36,128,128]{4,3,2,1,0:T(8,128)(2,1)} copy(bf16[4,1,36,128,128]{4,2,3,0,1:T(8,128)(2,1)S(1)} %convert_bitcast_fusion) | data formatting | bytes 9437184
  (59 shorter events, 12.4 us)
Async XLA Ops:
  0.6 106.3 %copy-start = (bf16[4,1,3,128,128]{4,3,2,1,0:T(8,128)(2,1)S(1)}, bf16[4,1,3,128,128]{4,3,2,1,0:T(8,128)(2,1)}, u32[]{:S(2)}) copy-start(bf16[4,1,3,128,128]{4,3,2,1,0:T(8,128)(2,1)} %param.2) | copy-start | bytes 1179652
  1.5 34.3 %collective-permute-start.6 = (s32[4,3]{1,0:T(4,128)S(1)}, s32[4,3]{1,0:T(4,128)S(1)}, u32[]{:S(2)}, u32[]{:S(2)}) collective-permute-start(s32[4,3]{1,0:T(4,128)S(1)} %bitcast.52), channel_id=1, source_target_pairs={{12,0},{16,4},{20,8},{24,12},{28,16},{32,20},{36,24},{40,28},{44,3... | collective-permute-start | bytes 152 | tf_op jit(solution)/shard_map/ppermute | solution.py:32
  16.4 21.9 %collective-permute-start.5 = (s32[4,3]{1,0:T(4,128)S(1)}, s32[4,3]{1,0:T(4,128)S(1)}, u32[]{:S(2)}, u32[]{:S(2)}) collective-permute-start(s32[4,3]{1,0:T(4,128)S(1)} %bitcast.53), channel_id=1, source_target_pairs={{8,0},{12,4},{16,8},{20,12},{24,16},{28,20},{32,24},{36,28},{40,32... | collective-permute-start | bytes 152 | tf_op jit(solution)/shard_map/ppermute | solution.py:32
  18.8 21.5 %collective-permute-start.4 = (s32[4,3]{1,0:T(4,128)S(1)}, s32[4,3]{1,0:T(4,128)S(1)}, u32[]{:S(2)}, u32[]{:S(2)}) collective-permute-start(s32[4,3]{1,0:T(4,128)S(1)} %bitcast.54), channel_id=1, source_target_pairs={{4,0},{8,4},{12,8},{16,12},{20,16},{24,20},{28,24},{32,28},{36,32}... | collective-permute-start | bytes 152 | tf_op jit(solution)/shard_map/ppermute | solution.py:32
  21.3 25.6 %collective-permute-start.3 = (s32[4,3]{1,0:T(4,128)S(1)}, s32[4,3]{1,0:T(4,128)S(1)}, u32[]{:S(2)}, u32[]{:S(2)}) collective-permute-start(s32[4,3]{1,0:T(4,128)S(1)} %bitcast.55), channel_id=1, source_target_pairs={{508,0},{0,4},{4,8},{8,12},{12,16},{16,20},{20,24},{24,28},{28,32}... | collective-permute-start | bytes 152 | tf_op jit(solution)/shard_map/ppermute | solution.py:32
  24.4 25.1 %collective-permute-start.2 = (s32[4,3]{1,0:T(4,128)S(1)}, s32[4,3]{1,0:T(4,128)S(1)}, u32[]{:S(2)}, u32[]{:S(2)}) collective-permute-start(s32[4,3]{1,0:T(4,128)S(1)} %bitcast.56), channel_id=1, source_target_pairs={{504,0},{508,4},{0,8},{4,12},{8,16},{12,20},{16,24},{20,28},{24,32... | collective-permute-start | bytes 152 | tf_op jit(solution)/shard_map/ppermute | solution.py:32
  28.6 26.8 %all-to-all-start = ((s32[4,4,1,3]{1,2,3,0:T(1,128)}), s32[4,4,1,3]{1,2,3,0:T(1,128)S(1)}, u32[]{:S(2)}, u32[]{:S(2)}) async-start(s32[4,4,1,3]{1,2,3,0:T(1,128)} %broadcast_in_dim.14), calls=%async_computation | async-start | bytes 12288 | tf_op jit(solution)/shard_map/all_to_all | solution.py:13
  35.8 15.6 %collective-permute-start.1 = (s32[4,3]{1,0:T(4,128)S(1)}, s32[4,3]{1,0:T(4,128)S(1)}, u32[]{:S(2)}, u32[]{:S(2)}) collective-permute-start(s32[4,3]{1,0:T(4,128)S(1)} %bitcast.57), channel_id=1, source_target_pairs={{500,0},{504,4},{508,8},{0,12},{4,16},{8,20},{12,24},{16,28},{20,3... | collective-permute-start | bytes 152 | tf_op jit(solution)/shard_map/ppermute | solution.py:32
  38.3 15.0 %collective-permute-start = (s32[4,3]{1,0:T(4,128)S(1)}, s32[4,3]{1,0:T(4,128)S(1)}, u32[]{:S(2)}, u32[]{:S(2)}) collective-permute-start(s32[4,3]{1,0:T(4,128)S(1)} %bitcast.58), channel_id=1, source_target_pairs={{496,0},{500,4},{504,8},{508,12},{0,16},{4,20},{8,24},{12,28},{16,... | collective-permute-start | bytes 152 | tf_op jit(solution)/shard_map/ppermute | solution.py:32
  40.3 85.3 %collective-permute-start.13 = (bf16[4,3,128,128]{3,2,1,0:T(8,128)(2,1)}, bf16[4,3,128,128]{3,2,1,0:T(8,128)(2,1)}, u32[]{:S(2)}, u32[]{:S(2)}) collective-permute-start(bf16[4,3,128,128]{3,2,1,0:T(8,128)(2,1)} %bitcast.44), channel_id=1, source_target_pairs={{12,0},{16,4},{20,8},{24,12},{28,16},{32,20},{36,24},{40,28},{44,3... | collective-permute-start | bytes 1179656 | tf_op jit(solution)/shard_map/ppermute | solution.py:32
  46.9 71.8 %collective-permute-start.10 = (bf16[4,3,128,128]{3,2,1,0:T(8,128)(2,1)}, bf16[4,3,128,128]{3,2,1,0:T(8,128)(2,1)}, u32[]{:S(2)}, u32[]{:S(2)}) collective-permute-start(bf16[4,3,128,128]{3,2,1,0:T(8,128)(2,1)} %bitcast.45), channel_id=1, source_target_pairs={{508,0},{0,4},{4,8},{8,12},{12,16},{16,20},{20,24},{24,28},{28,32}... | collective-permute-start | bytes 1179656 | tf_op jit(solution)/shard_map/ppermute | solution.py:32
  49.4 68.2 %collective-permute-start.9 = (bf16[4,3,128,128]{3,2,1,0:T(8,128)(2,1)}, bf16[4,3,128,128]{3,2,1,0:T(8,128)(2,1)}, u32[]{:S(2)}, u32[]{:S(2)}) collective-permute-start(bf16[4,3,128,128]{3,2,1,0:T(8,128)(2,1)} %bitcast.46), channel_id=1, source_target_pairs={{504,0},{508,4},{0,8},{4,12},{8,16},{12,20},{16,24},{20,28},{24,32... | collective-permute-start | bytes 1179656 | tf_op jit(solution)/shard_map/ppermute | solution.py:32
  51.4 62.5 %collective-permute-start.8 = (bf16[4,3,128,128]{3,2,1,0:T(8,128)(2,1)}, bf16[4,3,128,128]{3,2,1,0:T(8,128)(2,1)}, u32[]{:S(2)}, u32[]{:S(2)}) collective-permute-start(bf16[4,3,128,128]{3,2,1,0:T(8,128)(2,1)} %bitcast.47), channel_id=1, source_target_pairs={{500,0},{504,4},{508,8},{0,12},{4,16},{8,20},{12,24},{16,28},{20,3... | collective-permute-start | bytes 1179656 | tf_op jit(solution)/shard_map/ppermute | solution.py:32
  53.3 52.9 %collective-permute-start.7 = (bf16[4,3,128,128]{3,2,1,0:T(8,128)(2,1)}, bf16[4,3,128,128]{3,2,1,0:T(8,128)(2,1)S(1)}, u32[]{:S(2)}, u32[]{:S(2)}) collective-permute-start(bf16[4,3,128,128]{3,2,1,0:T(8,128)(2,1)} %bitcast.48), channel_id=1, source_target_pairs={{496,0},{500,4},{504,8},{508,12},{0,16},{4,20},{8,24},{12,28},{16,... | collective-permute-start | bytes 1179656 | tf_op jit(solution)/shard_map/ppermute | solution.py:32
  57.9 72.3 %all-to-all-start.1 = ((bf16[4,4,1,3,128,128]{5,4,3,1,2,0:T(8,128)(2,1)}), bf16[4,4,1,3,128,128]{5,4,3,1,2,0:T(8,128)(2,1)}, u32[]{:S(2)}, u32[]{:S(2)}) async-start(bf16[4,4,1,3,128,128]{5,4,3,1,2,0:T(8,128)(2,1)} %broadcast_in_dim.15), calls=%async_computation.1 | async-start | bytes 3145728 | tf_op jit(solution)/shard_map/all_to_all | solution.py:13
  106.2 0.7 copy-start.1
  106.9 18.6 %collective-permute-start.12 = (bf16[4,3,128,128]{3,2,1,0:T(8,128)(2,1)S(1)}, bf16[4,3,128,128]{3,2,1,0:T(8,128)(2,1)S(1)}, u32[]{:S(2)}, u32[]{:S(2)}) collective-permute-start(bf16[4,3,128,128]{3,2,1,0:T(8,128)(2,1)S(1)} %bitcast.50), channel_id=1, source_target_pairs={{8,0},{12,4},{16,8},{20,12},{24,16},{28,20},{32,24},{36,28},{40,32... | collective-permute-start | bytes 1179656 | tf_op jit(solution)/shard_map/ppermute | solution.py:32
  113.9 11.6 %collective-permute-start.11 = (bf16[4,3,128,128]{3,2,1,0:T(8,128)(2,1)S(1)}, bf16[4,3,128,128]{3,2,1,0:T(8,128)(2,1)S(1)}, u32[]{:S(2)}, u32[]{:S(2)}) collective-permute-start(bf16[4,3,128,128]{3,2,1,0:T(8,128)(2,1)S(1)} %bitcast.51), channel_id=1, source_target_pairs={{4,0},{8,4},{12,8},{16,12},{20,16},{24,20},{28,24},{32,28},{36,32}... | collective-permute-start | bytes 1179656 | tf_op jit(solution)/shard_map/ppermute | solution.py:32
where the time goes:
time: 167 us; the launch traced here: 164 us
  starting transfers between devices  62.3 us (37%)
  local copies, waits for them, and re-layouts  37.6 us (23%)
  blocking collectives  34.8 us (21%)
  matrix products  17 us (10%)
  waiting for transfers between devices  5.64 us (3%)
  other arithmetic  5.26 us (3%)
    ppermute x14, starting transfers between devices, shifted(): return lax.ppermute(block, axis, route)  53.8 us
    unnamed x2, blocking collectives  34.8 us
    unnamed x21, local copies, waits for them, and re-layouts  14.2 us
    reshape x1, local copies, waits for them, and re-layouts, on_device(): products.reshape(panel_rows, row_slots * per_group, block_size, block_size)  12 us
    dot_general x1, matrix products, on_device(): jnp.einsum('poq,pqac->poac', onehot, products.reshape(panel_rows, row_slo...  9.58 us
    all_to_all x2, starting transfers between devices, sent_to_all(): lax.all_to_all(jnp.broadcast_to(shard[None], (size, *shard.shape)), axis,...  8.53 us
    dot_general x1, matrix products, on_device(): jnp.einsum('ptab,ptsbc->ptsac', left_vals, right_vals, preferred_element_...  7.41 us
    ppermute x14, waiting for transfers between devices, shifted(): return lax.ppermute(block, axis, route)  5.63 us
  transfers between devices with their start and end apart: 16, of which 1 were waited for; matrix products, arithmetic and copies ran while one was open for 15% of the time, Pallas kernels for 0%

commit v1 on v0

v1 whole, which is shorter than its diff:
```python
import jax
import jax.numpy as jnp
from jax import lax
from jax.experimental import pallas as pl
from jax.experimental.pallas import tpu as pltpu
from jax.sharding import Mesh
from jax.sharding import PartitionSpec as P

HP = 4
PB = 4
KG = 3
GROUPS = 4
BS = 128
NP = 128
WIDTH = 36
USED = 15
WIN = 2 * HP
ROWS = ("rows_0", "rows_1", "rows_2")
SLOTS = ((4, 5, 2, 3, 6, 7, 0, 1), (4, 3, 2, 1, 6, 5, 0, 7))


def place():
    return lax.axis_index(ROWS), lax.axis_index("cols")


def index_kernel(tab_ref, cols_ref, starts_ref, map_ref, pres_ref):
    p0, c = place()
    table = tab_ref[...]
    j_of = lax.broadcasted_iota(jnp.int32, (NP, BS), 1)
    panel_of = lax.broadcasted_iota(jnp.int32, (NP, BS), 0)
    one = jnp.float32(1)
    zero = jnp.float32(0)
    rights = []
    for r in range(PB):
        hit = None
        for s in range(KG):
            col = jnp.zeros((NP, 1), jnp.int32)
            for g in range(GROUPS):
                at = 12 * g + KG * r + s
                col = jnp.where(c == g, table[:, at : at + 1], col)
            same = lax.shift_right_logical(col, 2) == j_of
            hit = same if hit is None else hit | same
        rights.append(jnp.where(hit, one, zero).astype(jnp.bfloat16))
    right = jnp.concatenate(rights, axis=0)
    lane = lax.broadcasted_iota(jnp.int32, (NP, PB * NP), 1)
    row_of_lane = 4 * (lane & (NP - 1)) + lax.shift_right_logical(lane, 7)
    every = jnp.zeros((NP, BS), jnp.float32)
    for r in range(PB):
        hit = None
        for g in range(GROUPS):
            for s in range(KG):
                at = 12 * g + KG * r + s
                same = table[:, at : at + 1] == row_of_lane
                hit = same if hit is None else hit | same
        left = jnp.where(hit, one, zero).astype(jnp.bfloat16)
        paths = jnp.dot(left, right, preferred_element_type=jnp.float32)
        present = jnp.where(paths > 0.5, one, zero)
        pres_ref[r] = present
        every = every + present
    before = jnp.sum(jnp.where(panel_of < p0, every, zero)).astype(jnp.int32)
    own = [pres_ref[r, pl.ds(p0, 1), :] for r in range(PB)]
    own = jnp.concatenate(own + own, axis=0)
    upper = jnp.where(panel_of < j_of, one, zero).astype(jnp.bfloat16)
    rank = jnp.dot(own.astype(jnp.bfloat16), upper, preferred_element_type=jnp.float32)
    rank = rank.astype(jnp.int32)
    slot = lax.broadcasted_iota(jnp.int32, (40, BS), 0)
    js = lax.broadcasted_iota(jnp.int32, (8, BS), 1).astype(jnp.bfloat16)
    row = lax.broadcasted_iota(jnp.int32, (PB, 1), 0)
    starts = jnp.zeros((PB, 1), jnp.int32) + before
    for r in range(PB):
        taken = (rank[r : r + 1, :] == slot) & (own[r : r + 1, :] > 0.5)
        taken = jnp.where(taken, one, zero).astype(jnp.bfloat16)
        found = lax.dot_general(
            js, taken, (((1,), (1,)), ((), ())), preferred_element_type=jnp.float32
        )
        count = jnp.sum(own[r : r + 1, :]).astype(jnp.int32)
        slots = lax.broadcasted_iota(jnp.int32, (1, 40), 1)
        cols = jnp.where(slots < count, 4 * found[:1].astype(jnp.int32) + c, -1)
        cols_ref[r : r + 1, :] = cols[:, :WIDTH]
        starts = starts + jnp.where(row > r, count, 0)
    starts_ref[...] = starts
    map_ref[...] = jnp.zeros((16, BS), jnp.int32)
    for w in range(WIN):
        map_ref[w : w + 1, 0:48] = tab_ref[pl.ds((p0 - HP + w) & (NP - 1), 1), :]
    map_ref[8:16, :] = rank


def square_kernel(map_ref, left_ref, *refs):
    pieces = refs[:WIN]
    out_ref = refs[WIN]
    lefts, rights = refs[WIN + 1 : WIN + 3]
    sums = refs[WIN + 3 : WIN + 3 + PB]
    staged, blank, in_sem, zero_sem, out_sem = refs[WIN + 3 + PB :]
    p0, c = place()
    blank[...] = jnp.zeros(blank.shape, blank.dtype)
    for r in range(PB):
        pltpu.make_async_copy(blank, out_ref.at[r, USED:], zero_sem.at[r]).start()
    copies = [pltpu.make_async_copy(left_ref, lefts, in_sem.at[WIN])]
    core = p0 & 1
    for n in range(WIN):
        w = jnp.where(core == 0, SLOTS[0][n], SLOTS[1][n])
        copies.append(pltpu.make_async_copy(pieces[n], rights.at[w], in_sem.at[n]))
    for copy in copies:
        copy.start()
    for r in range(PB):
        sums[r][...] = jnp.zeros((USED, BS, BS), jnp.float32)
    for copy in copies:
        copy.wait()

    def group_step(g, carry):
        for s0 in range(KG):
            for r in range(PB):
                k = map_ref[HP, 12 * g + KG * r + s0]
                w = (lax.shift_right_logical(k, 2) - p0 + HP) & (WIN - 1)
                kr = k & (PB - 1)
                slots = []
                for s in range(KG):
                    col = map_ref[w, 12 * c + KG * kr + s]
                    slots.append(map_ref[8 + r, lax.shift_right_logical(col, 2)])
                right = jnp.concatenate([rights[w, kr, s] for s in range(KG)], axis=1)
                product = jnp.dot(
                    lefts[g, r, s0], right, preferred_element_type=jnp.float32
                )
                new = [
                    sums[r][slots[s]] + product[:, BS * s : BS * (s + 1)] for s in range(KG)
                ]
                for s in range(KG):
                    sums[r][slots[s]] = new[s]
        return carry

    lax.fori_loop(0, GROUPS, group_step, 0)
    for r in range(PB):
        staged[r] = sums[r][...].astype(jnp.bfloat16)
        pltpu.make_async_copy(staged.at[r], out_ref.at[r, :USED], out_sem.at[r]).start()
    for r in range(PB):
        pltpu.make_async_copy(blank, out_ref.at[r, USED:], zero_sem.at[r]).wait()
        pltpu.make_async_copy(staged.at[r], out_ref.at[r, :USED], out_sem.at[r]).wait()


def indices(table):
    vmem = pl.BlockSpec(memory_space=pltpu.VMEM)
    return pl.pallas_call(
        index_kernel,
        out_shape=(
            jax.ShapeDtypeStruct((PB, WIDTH), jnp.int32),
            jax.ShapeDtypeStruct((PB, 1), jnp.int32),
            jax.ShapeDtypeStruct((16, BS), jnp.int32),
        ),
        in_specs=[vmem],
        out_specs=(vmem, vmem, vmem),
        scratch_shapes=[pltpu.VMEM((PB, NP, BS), jnp.float32)],
        name="indices",
    )(table)


def square(where, left, pieces):
    hbm = pl.BlockSpec(memory_space=pl.ANY)
    return pl.pallas_call(
        square_kernel,
        out_shape=jax.ShapeDtypeStruct((PB, WIDTH, BS, BS), jnp.bfloat16),
        in_specs=[pl.BlockSpec(memory_space=pltpu.SMEM)] + [hbm] * (1 + WIN),
        out_specs=hbm,
        scratch_shapes=[
            pltpu.VMEM((GROUPS, PB, KG, BS, BS), jnp.bfloat16),
            pltpu.VMEM((WIN, PB, KG, BS, BS), jnp.bfloat16),
        ]
        + [pltpu.VMEM((USED, BS, BS), jnp.float32) for _ in range(PB)]
        + [
            pltpu.VMEM((PB, USED, BS, BS), jnp.bfloat16),
            pltpu.VMEM((WIDTH - USED, BS, BS), jnp.bfloat16),
            pltpu.SemaphoreType.DMA((WIN + 1,)),
            pltpu.SemaphoreType.DMA((PB,)),
            pltpu.SemaphoreType.DMA((PB,)),
        ],
        name="square",
    )(where, left, *pieces)


def sent_to_all(shard, axis):
    size = lax.axis_size(axis)
    return lax.all_to_all(
        jnp.broadcast_to(shard[None], (size, *shard.shape)), axis, 0, 0, tiled=True
    )


def moved(block, chips, cross=False, low=None):
    chip_count = NP // 2
    route = []
    for q in range(chip_count):
        for core in range(2):
            step = chips
            if low is not None:
                step = -low if core else low
            route.append((2 * q + core, 2 * ((q + step) % chip_count) + (core ^ cross)))
    return lax.ppermute(block, ROWS, route)


def on_device(blocks, block_cols):
    own = blocks[:, 0]
    slab = sent_to_all(block_cols.reshape(12), ("rows_1", "rows_2", "cols"))
    table = sent_to_all(slab.reshape(8, 48), "rows_0").reshape(NP, 48)
    columns, starts, where = indices(table)
    behind = moved(own, 1)
    ahead = moved(own, -1)
    behind2 = moved(own, 2)
    far = moved(own, 0, True, low=-2)
    left = sent_to_all(own, "cols")
    partner = moved(own, 0, True)
    behind_x = moved(behind, 0, True)
    ahead_x = moved(ahead, 0, True)
    pieces = [own, partner, behind, behind_x, ahead, ahead_x, behind2, far]
    out = square(where, left, pieces)
    return out[:, None], columns[:, None], starts


def solution(mesh):
    split = Mesh(
        mesh.devices.reshape(16, 4, 2, mesh.shape["cols"]), ("rows_0", "rows_1", "rows_2", "cols")
    )
    return jax.shard_map(
        on_device,
        mesh=split,
        in_specs=(P(ROWS, "cols", None, None, None), P(ROWS, "cols", None)),
        out_specs=(P(ROWS, "cols", None, None, None), P(ROWS, "cols", None), P(ROWS, "cols")),
        check_vma=False,
    )
```

time: 167 us -> 96.8 us (0.58); the launches traced: 164 us -> 96 us
  starting transfers between devices: 62.3 us -> 30 us
  local copies, waits for them, and re-layouts: 37.6 us -> 8.63 us
  matrix products: 17 us -> 0 us
  Pallas kernels: 0 us -> 11.7 us
  blocking collectives: 34.8 us -> 41.6 us
  waiting for transfers between devices: 5.64 us -> 0.51 us
  other arithmetic: 5.26 us -> 2.74 us
    all_to_all x0 -> x2, blocking collectives: none -> 41.6 us  [sent_to_all(): lax.all_to_all(jnp.broadcast_to(shard[None], (size, *shard.shape)), axis,...]
    unnamed x2 -> x0, blocking collectives: 34.8 us -> none
    ppermute x14 -> x7, starting transfers between devices: 53.8 us -> 26.3 us  [moved(): return lax.ppermute(block, ROWS, route)]
    dot_general x2 -> x0, matrix products: 17 us -> none  [the longest x1 9.58 us: on_device(): jnp.einsum('poq,pqac->poac', onehot, products.reshape(panel_rows, row_slo...]
    reshape x4 -> x0, local copies, waits for them, and re-layouts: 12.3 us -> none  [the longest x1 12 us: on_device(): products.reshape(panel_rows, row_slots * per_group, block_size, block_size)]
    pallas_call x0 -> x2, Pallas kernels: none -> 11.7 us  [the longest x1 7.55 us: square(): pl.pallas_call(square_kernel, out_shape=jax.ShapeDtypeStruct((PB, WIDTH,...]
    unnamed x21 -> x16, local copies, waits for them, and re-layouts: 14.2 us -> 4.91 us
    ppermute x14 -> x7, waiting for transfers between devices: 5.63 us -> 0.51 us  [moved(): return lax.ppermute(block, ROWS, route)]
  transfers between devices with their start and end apart: 16 -> 8, of which waited for: 1 -> 1; matrix products, arithmetic and copies ran while one was open for 15% -> 5% of each run, Pallas kernels for 0% -> 4%
where the time goes in v1:
time: 96.8 us; the launch traced here: 96 us
  blocking collectives  41.6 us (43%)
  starting transfers between devices  30 us (31%)
  Pallas kernels  11.7 us (12%)
  local copies, waits for them, and re-layouts  8.63 us (9%)
  other arithmetic  2.74 us (3%)
    all_to_all x2, blocking collectives, sent_to_all(): lax.all_to_all(jnp.broadcast_to(shard[None], (size, *shard.shape)), axis,...  41.6 us
    ppermute x7, starting transfers between devices, moved(): return lax.ppermute(block, ROWS, route)  26.3 us
    pallas_call x1, Pallas kernels, square(): pl.pallas_call(square_kernel, out_shape=jax.ShapeDtypeStruct((PB, WIDTH,...  7.55 us
    unnamed x16, local copies, waits for them, and re-layouts  4.91 us
    pallas_call x1, Pallas kernels, indices(): pl.pallas_call(index_kernel, out_shape=(jax.ShapeDtypeStruct((PB, WIDTH),...  4.17 us
    all_to_all x1, starting transfers between devices, sent_to_all(): lax.all_to_all(jnp.broadcast_to(shard[None], (size, *shard.shape)), axis,...  3.69 us
    all_to_all x2, other arithmetic, sent_to_all(): lax.all_to_all(jnp.broadcast_to(shard[None], (size, *shard.shape)), axis,...  2.74 us
    broadcast_in_dim x5, local copies, waits for them, and re-layouts, sent_to_all(): jnp.broadcast_to(shard[None], (size, *shard.shape))  2.7 us
  transfers between devices with their start and end apart: 8, of which 1 were waited for; matrix products, arithmetic and copies ran while one was open for 5% of the time, Pallas kernels for 4%

profile of v1, /device:TPU:1, one launch (start us, length us, event | category | flops | bytes accessed | tf_op | source)
XLA Modules:
  0.0 96.0 jit_solution(12100700777093808606)
XLA Ops:
  0.6 0.8 copy.13
  1.4 0.1 broadcast_in_dim.27
  1.5 16.5 %all_to_all.16 = s32[32,1,12]{2,1,0:T(1,128)S(1)} all-to-all(s32[32,1,12]{2,1,0:T(1,128)S(1)} %broadcast_in_dim.28), channel_id=1, replica_groups=mesh['rows_0'=16,'rows_1'=4,'rows_2'=2,'cols'=4] {'rows_1','rows_2','cols'}, dimensions={0} | all-to-all | bytes 3072 | tf_op jit(solution)/shard_map/all_to_all | solution.py:181
  18.0 0.5 broadcast.6
  18.5 0.7 reduce.3
  19.2 0.1 broadcast_in_dim.29
  19.3 0.1 reshape.30
  19.4 25.1 %all_to_all.17 = s32[16,1,384]{2,1,0:T(1,128)} all-to-all(s32[16,1,384]{2,1,0:T(1,128)S(1)} %reshape.30), channel_id=1, replica_groups=mesh['rows_0'=16,'rows_1'=4,'rows_2'=2,'cols'=4] {'rows_0'}, dimensions={0} | all-to-all | bytes 49152 | tf_op jit(solution)/shard_map/all_to_all | solution.py:181
  44.5 2.5 %broadcast_in_dim.32 = bf16[4,4,3,128,128]{4,3,2,1,0:T(8,128)(2,1)} broadcast(bf16[4,3,128,128]{3,2,1,0:T(8,128)(2,1)} %bitcast.11), dimensions={1,2,3,4} | broadcast | bytes 1966080 | tf_op jit(solution)/shard_map/broadcast_in_dim | solution.py:182
  47.0 3.7 %all-to-all-start.2 = ((bf16[4,4,3,128,128]{4,3,2,1,0:T(8,128)(2,1)}), bf16[4,4,3,128,128]{4,3,2,1,0:T(8,128)(2,1)S(1)}, u32[]{:S(2)}, u32[]{:S(2)}) async-start(bf16[4,4,3,128,128]{4,3,2,1,0:T(8,128)(2,1)} %broadcast_in_dim.32), calls=%async_computation.2 | async-start | bytes 3145728 | tf_op jit(solution)/shard_map/all_to_all | solution.py:181
  50.7 3.4 %collective-permute-start.3 = (bf16[4,3,128,128]{3,2,1,0:T(8,128)(2,1)S(1)}, bf16[4,3,128,128]{3,2,1,0:T(8,128)(2,1)S(1)}, u32[]{:S(2)}, u32[]{:S(2)}) collective-permute-start(bf16[4,3,128,128]{3,2,1,0:T(8,128)(2,1)S(1)} %bitcast.13), channel_id=1, source_target_pairs={{0,504},{4,508},{8,0},{12,4},{16,8},{20,12},{24,16},{28,20},{32,24... | collective-permute-start | bytes 1179656 | tf_op jit(solution)/shard_map/ppermute | solution.py:195
  54.1 1.9 %collective-permute-start.1 = (bf16[4,3,128,128]{3,2,1,0:T(8,128)(2,1)S(1)}, bf16[4,3,128,128]{3,2,1,0:T(8,128)(2,1)S(1)}, u32[]{:S(2)}, u32[]{:S(2)}) collective-permute-start(bf16[4,3,128,128]{3,2,1,0:T(8,128)(2,1)S(1)} %bitcast.14), channel_id=1, source_target_pairs={{0,8},{4,12},{8,16},{12,20},{16,24},{20,28},{24,32},{28,36},{32,40... | collective-permute-start | bytes 1179656 | tf_op jit(solution)/shard_map/ppermute | solution.py:195
  56.0 5.4 %collective-permute-start.6 = (bf16[4,3,128,128]{3,2,1,0:T(8,128)(2,1)S(1)}, bf16[4,3,128,128]{3,2,1,0:T(8,128)(2,1)S(1)}, u32[]{:S(2)}, u32[]{:S(2)}) collective-permute-start(bf16[4,3,128,128]{3,2,1,0:T(8,128)(2,1)S(1)} %bitcast.15), channel_id=1, source_target_pairs={{0,500},{4,16},{8,508},{12,24},{16,4},{20,32},{24,12},{28,40},{32,... | collective-permute-start | bytes 1179656 | tf_op jit(solution)/shard_map/ppermute | solution.py:195
  61.4 4.1 %collective-permute-start.5 = (bf16[4,3,128,128]{3,2,1,0:T(8,128)(2,1)S(1)}, bf16[4,3,128,128]{3,2,1,0:T(8,128)(2,1)S(1)}, u32[]{:S(2)}, u32[]{:S(2)}) collective-permute-start(bf16[4,3,128,128]{3,2,1,0:T(8,128)(2,1)S(1)} %bitcast.16), channel_id=1, source_target_pairs={{0,16},{4,20},{8,24},{12,28},{16,32},{20,36},{24,40},{28,44},{32,4... | collective-permute-start | bytes 1179656 | tf_op jit(solution)/shard_map/ppermute | solution.py:195
  65.5 1.9 %collective-permute-start = (bf16[4,3,128,128]{3,2,1,0:T(8,128)(2,1)S(1)}, bf16[4,3,128,128]{3,2,1,0:T(8,128)(2,1)}, u32[]{:S(2)}, u32[]{:S(2)}) collective-permute-start(bf16[4,3,128,128]{3,2,1,0:T(8,128)(2,1)S(1)} %bitcast.17), channel_id=1, source_target_pairs={{0,4},{4,0},{8,12},{12,8},{16,20},{20,16},{24,28},{28,24},{32,36},... | collective-permute-start | bytes 1179656 | tf_op jit(solution)/shard_map/ppermute | solution.py:195
  67.4 0.0 collective-permute-done.3.refs_4_
  67.4 2.4 %collective-permute-start.4 = (bf16[4,3,128,128]{3,2,1,0:T(8,128)(2,1)S(1)}, bf16[4,3,128,128]{3,2,1,0:T(8,128)(2,1)}, u32[]{:S(2)}, u32[]{:S(2)}) collective-permute-start(bf16[4,3,128,128]{3,2,1,0:T(8,128)(2,1)S(1)} %collective-permute-done.3.refs_4_), channel_id=1, source_target_pairs={{0,4},{4,0},{8,12},{12,8},{16,20},{20,16},{24,28},{28,24},{32,36},... | collective-permute-start | bytes 1179656 | tf_op jit(solution)/shard_map/ppermute | solution.py:195
  69.8 0.0 collective-permute-done.1.refs_2_
  69.9 7.2 %collective-permute-start.2 = (bf16[4,3,128,128]{3,2,1,0:T(8,128)(2,1)S(1)}, bf16[4,3,128,128]{3,2,1,0:T(8,128)(2,1)}, u32[]{:S(2)}, u32[]{:S(2)}) collective-permute-start(bf16[4,3,128,128]{3,2,1,0:T(8,128)(2,1)S(1)} %collective-permute-done.1.refs_2_), channel_id=1, source_target_pairs={{0,4},{4,0},{8,12},{12,8},{16,20},{20,16},{24,28},{28,24},{32,36},... | collective-permute-start | bytes 1179656 | tf_op jit(solution)/shard_map/ppermute | solution.py:195
  77.1 0.5 broadcast.7
  77.6 2.0 %reduce.4 = s32[16,384]{1,0:T(8,128)} reduce(s32[16,1,384]{2,1,0:T(1,128)} %all_to_all.17, s32[]{:T(128)} %broadcast.7), dimensions={1}, to_apply=%all_to_all.11.reduce_sub_computation | reduce | bytes 49156 | tf_op jit(solution)/shard_map/all_to_all | solution.py:181
  79.7 1.4 %reshape.31 = s32[16,8,48]{2,1,0:T(8,128)} reshape(s32[16,384]{1,0:T(8,128)} %reduce.4) | data formatting | bytes 49152
  81.1 4.2 %indices.1 = (s32[4,36]{1,0:T(4,128)}, s32[4,1]{1,0:T(4,128)}, s32[16,128]{1,0:T(8,128)}) custom-call(s32[128,48]{1,0:T(8,128)} %bitcast.18), custom_call_target="tpu_custom_call" | custom-call | tf_op jit(solution)/shard_map/indices/pallas_call | solution.py:142
  85.3 1.2 %copy.16 = s32[4,1]{0,1:T(1,128)} copy(s32[4,1]{1,0:T(4,128)} %get-tuple-element.17) | data formatting | bytes 32
  86.5 0.5 collective-permute-done.6.refs_7_
  87.0 0.0 collective-permute-done.5.refs_6_
  87.0 0.0 collective-permute-done.refs_1_
  87.1 0.0 all-to-all-done.2.left_ref
  87.1 0.7 copy-done.4
  87.8 0.1 copy-done.5
  87.9 0.5 copy-done
  88.4 7.6 %square.1 = bf16[4,36,128,128]{3,2,1,0:T(8,128)(2,1)} custom-call(s32[16,128]{1,0:T(8,128)} %get-tuple-element.6.map_ref, bf16[4,4,3,128,128]{4,3,2,1,0:T(8,128)(2,1)} %copy-done, bf16[4,3,128,128]{3,2,1,0:T(8,128)(2,1)} %bitcast.12, bf16[4,3,128,128]{3,2,1,0:T(8,128)(2,1)} %collective-permute-done.refs_1_, bf16[4,3,128,128]{3,2,1,0:T(8,128)(2,1)} %copy-done.3, ...), custom_call_target="tpu_custom_call" | custom-call | tf_op jit(solution)/shard_map/square/pallas_call | solution.py:158
  (13 shorter events, 0.0 us)
Async XLA Ops:
  47.0 3.7 %copy-start.1 = (bf16[4,1,3,128,128]{4,3,2,1,0:T(8,128)(2,1)S(1)}, bf16[4,1,3,128,128]{4,3,2,1,0:T(8,128)(2,1)}, u32[]{:S(2)}) copy-start(bf16[4,1,3,128,128]{4,3,2,1,0:T(8,128)(2,1)} %param.2) | copy-start | bytes 1179652
  47.0 40.0 %all-to-all-start.2 = ((bf16[4,4,3,128,128]{4,3,2,1,0:T(8,128)(2,1)}), bf16[4,4,3,128,128]{4,3,2,1,0:T(8,128)(2,1)S(1)}, u32[]{:S(2)}, u32[]{:S(2)}) async-start(bf16[4,4,3,128,128]{4,3,2,1,0:T(8,128)(2,1)} %broadcast_in_dim.32), calls=%async_computation.2 | async-start | bytes 3145728 | tf_op jit(solution)/shard_map/all_to_all | solution.py:181
  50.7 16.7 %collective-permute-start.3 = (bf16[4,3,128,128]{3,2,1,0:T(8,128)(2,1)S(1)}, bf16[4,3,128,128]{3,2,1,0:T(8,128)(2,1)S(1)}, u32[]{:S(2)}, u32[]{:S(2)}) collective-permute-start(bf16[4,3,128,128]{3,2,1,0:T(8,128)(2,1)S(1)} %bitcast.13), channel_id=1, source_target_pairs={{0,504},{4,508},{8,0},{12,4},{16,8},{20,12},{24,16},{28,20},{32,24... | collective-permute-start | bytes 1179656 | tf_op jit(solution)/shard_map/ppermute | solution.py:195
  54.1 15.7 %collective-permute-start.1 = (bf16[4,3,128,128]{3,2,1,0:T(8,128)(2,1)S(1)}, bf16[4,3,128,128]{3,2,1,0:T(8,128)(2,1)S(1)}, u32[]{:S(2)}, u32[]{:S(2)}) collective-permute-start(bf16[4,3,128,128]{3,2,1,0:T(8,128)(2,1)S(1)} %bitcast.14), channel_id=1, source_target_pairs={{0,8},{4,12},{8,16},{12,20},{16,24},{20,28},{24,32},{28,36},{32,40... | collective-permute-start | bytes 1179656 | tf_op jit(solution)/shard_map/ppermute | solution.py:195
  56.0 31.0 %collective-permute-start.6 = (bf16[4,3,128,128]{3,2,1,0:T(8,128)(2,1)S(1)}, bf16[4,3,128,128]{3,2,1,0:T(8,128)(2,1)S(1)}, u32[]{:S(2)}, u32[]{:S(2)}) collective-permute-start(bf16[4,3,128,128]{3,2,1,0:T(8,128)(2,1)S(1)} %bitcast.15), channel_id=1, source_target_pairs={{0,500},{4,16},{8,508},{12,24},{16,4},{20,32},{24,12},{28,40},{32,... | collective-permute-start | bytes 1179656 | tf_op jit(solution)/shard_map/ppermute | solution.py:195
  61.4 25.6 %collective-permute-start.5 = (bf16[4,3,128,128]{3,2,1,0:T(8,128)(2,1)S(1)}, bf16[4,3,128,128]{3,2,1,0:T(8,128)(2,1)S(1)}, u32[]{:S(2)}, u32[]{:S(2)}) collective-permute-start(bf16[4,3,128,128]{3,2,1,0:T(8,128)(2,1)S(1)} %bitcast.16), channel_id=1, source_target_pairs={{0,16},{4,20},{8,24},{12,28},{16,32},{20,36},{24,40},{28,44},{32,4... | collective-permute-start | bytes 1179656 | tf_op jit(solution)/shard_map/ppermute | solution.py:195
  65.5 21.6 %collective-permute-start = (bf16[4,3,128,128]{3,2,1,0:T(8,128)(2,1)S(1)}, bf16[4,3,128,128]{3,2,1,0:T(8,128)(2,1)}, u32[]{:S(2)}, u32[]{:S(2)}) collective-permute-start(bf16[4,3,128,128]{3,2,1,0:T(8,128)(2,1)S(1)} %bitcast.17), channel_id=1, source_target_pairs={{0,4},{4,0},{8,12},{12,8},{16,20},{20,16},{24,28},{28,24},{32,36},... | collective-permute-start | bytes 1179656 | tf_op jit(solution)/shard_map/ppermute | solution.py:195
  67.4 19.7 %copy-start.2 = (bf16[4,3,128,128]{3,2,1,0:T(8,128)(2,1)}, bf16[4,3,128,128]{3,2,1,0:T(8,128)(2,1)S(1)}, u32[]{:S(2)}) copy-start(bf16[4,3,128,128]{3,2,1,0:T(8,128)(2,1)S(1)} %collective-permute-done.3.refs_4_) | copy-start | bytes 1179652
  67.4 19.6 %collective-permute-start.4 = (bf16[4,3,128,128]{3,2,1,0:T(8,128)(2,1)S(1)}, bf16[4,3,128,128]{3,2,1,0:T(8,128)(2,1)}, u32[]{:S(2)}, u32[]{:S(2)}) collective-permute-start(bf16[4,3,128,128]{3,2,1,0:T(8,128)(2,1)S(1)} %collective-permute-done.3.refs_4_), channel_id=1, source_target_pairs={{0,4},{4,0},{8,12},{12,8},{16,20},{20,16},{24,28},{28,24},{32,36},... | collective-permute-start | bytes 1179656 | tf_op jit(solution)/shard_map/ppermute | solution.py:195
  69.8 17.2 %copy-start.3 = (bf16[4,3,128,128]{3,2,1,0:T(8,128)(2,1)}, bf16[4,3,128,128]{3,2,1,0:T(8,128)(2,1)S(1)}, u32[]{:S(2)}) copy-start(bf16[4,3,128,128]{3,2,1,0:T(8,128)(2,1)S(1)} %collective-permute-done.1.refs_2_) | copy-start | bytes 1179652
  69.9 17.2 %collective-permute-start.2 = (bf16[4,3,128,128]{3,2,1,0:T(8,128)(2,1)S(1)}, bf16[4,3,128,128]{3,2,1,0:T(8,128)(2,1)}, u32[]{:S(2)}, u32[]{:S(2)}) collective-permute-start(bf16[4,3,128,128]{3,2,1,0:T(8,128)(2,1)S(1)} %collective-permute-done.1.refs_2_), channel_id=1, source_target_pairs={{0,4},{4,0},{8,12},{12,8},{16,20},{20,16},{24,28},{28,24},{32,36},... | collective-permute-start | bytes 1179656 | tf_op jit(solution)/shard_map/ppermute | solution.py:195
  87.0 0.7 copy-start.4
  87.0 0.9 copy-start.5
  87.1 1.4 %copy-start = (bf16[4,4,3,128,128]{4,3,2,1,0:T(8,128)(2,1)}, bf16[4,4,3,128,128]{4,3,2,1,0:T(8,128)(2,1)S(1)}, u32[]{:S(2)}) copy-start(bf16[4,4,3,128,128]{4,3,2,1,0:T(8,128)(2,1)S(1)} %all-to-all-done.2.left_ref) | copy-start | bytes 4718596

commit v2 on v1

v2 whole, which is shorter than its diff:
```python
import jax
import jax.numpy as jnp
from jax import lax
from jax.experimental import pallas as pl
from jax.experimental.pallas import tpu as pltpu
from jax.sharding import Mesh
from jax.sharding import PartitionSpec as P

HP = 4
PB = 4
KG = 3
GROUPS = 4
BS = 128
NP = 128
WIDTH = 36
USED = 15
WIN = 2 * HP
PER = PB * KG
ROWS = ("rows_0", "rows_1", "rows_2")
SLAB = ("rows_1", "rows_2", "cols")


def place():
    return lax.axis_index(ROWS), lax.axis_index("cols")


def spread_kernel(cols_ref, out_ref):
    _, c = place()
    lane = lax.broadcasted_iota(jnp.int32, (1, BS), 1)
    row = jnp.zeros((1, BS), jnp.int32)
    for r in range(PB):
        for s in range(KG):
            row = jnp.where(lane == PER * c + KG * r + s, cols_ref[r, s], row)
    out_ref[...] = jnp.broadcast_to(row[None], out_ref.shape)


def slab_kernel(in_ref, out_ref):
    rows = []
    for n in range(8):
        part = [in_ref[GROUPS * n + g] for g in range(GROUPS)]
        rows.append((part[0] + part[1]) + (part[2] + part[3]))
    tile = jnp.concatenate(rows, axis=0)
    out_ref[...] = jnp.broadcast_to(tile[None], out_ref.shape)


def bits_set(x):
    x = x - ((x >> 1) & 0x5555)
    x = (x & 0x3333) + ((x >> 2) & 0x3333)
    x = (x + (x >> 4)) & 0x0F0F
    return (x + (x >> 8)) & 0x1F


def index_kernel(tab_ref, cols_ref, starts_ref, map_ref, turned_ref):
    p0, c = place()
    turned_ref[...] = jnp.transpose(tab_ref[...].reshape(NP, BS))
    panel = lax.broadcasted_iota(jnp.int32, (1, NP), 1)
    wants = []
    owns = []
    for r in range(PB):
        want = jnp.zeros((1, NP), jnp.int32)
        for g in range(GROUPS):
            for s in range(KG):
                at = PER * g + KG * r + s
                local = (turned_ref[at : at + 1, :] - PB * (panel - HP)) & (PB * NP - 1)
                want = want | jnp.left_shift(1, local)
        wants.append(want)
        own = jnp.zeros((1, NP), jnp.int32)
        for s in range(KG):
            col = turned_ref[pl.ds(PER * c + KG * r + s, 1), :]
            own = own | jnp.left_shift(1, ((col >> 2) - panel + HP) & (NP - 1))
        owns.append(own)
    pad = [jnp.zeros((PB, NP), jnp.int32)]
    want = jnp.concatenate(wants + pad, axis=0)
    own = jnp.concatenate(owns + pad, axis=0)
    found = jnp.zeros((8, NP), jnp.int32)
    for w in range(WIN):
        there = pltpu.roll(own, (HP - w) % NP, 1) if w != HP else own
        there = there << w
        for kr in range(PB):
            used = -((want >> (PB * w + kr)) & 1)
            found = found | (used & there[kr : kr + 1, :])
    counts = bits_set(found)
    before = jnp.sum(jnp.where(panel < p0, counts, 0).astype(jnp.float32)).astype(jnp.int32)
    here = jnp.where(panel == p0, 1, 0)
    mask = jnp.sum((found * here).astype(jnp.float32), axis=1, keepdims=True)
    count = jnp.sum((counts * here).astype(jnp.float32), axis=1, keepdims=True).astype(jnp.int32)
    mask = mask.astype(jnp.int32)
    lane = lax.broadcasted_iota(jnp.int32, (8, BS), 1)
    held = jnp.where(lane < 16, (jnp.broadcast_to(mask, (8, BS)) >> (lane & 15)) & 1, 0)
    turn = (2 * HP - p0) & (NP - 1)
    turn = jnp.where(turn > 14, 0, turn)
    col_of = lax.broadcasted_iota(jnp.int32, (BS, BS), 1)
    row_of = lax.broadcasted_iota(jnp.int32, (BS, BS), 0)
    ahead = ((row_of - turn) & 15) < ((col_of - turn) & 15)
    ahead = jnp.where(ahead, 1.0, 0.0).astype(jnp.bfloat16)
    rank = jnp.dot(held.astype(jnp.bfloat16), ahead, preferred_element_type=jnp.float32)
    rank = rank.astype(jnp.int32)
    slot = lax.broadcasted_iota(jnp.int32, (40, BS), 0)
    panels = ((p0 - 2 * HP + lane) & (NP - 1)).astype(jnp.bfloat16)
    slots = lax.broadcasted_iota(jnp.int32, (1, 40), 1)
    start = before
    for r in range(PB):
        taken = (rank[r : r + 1, :] == slot) & (held[r : r + 1, :] > 0)
        taken = jnp.where(taken, 1.0, 0.0).astype(jnp.bfloat16)
        col = lax.dot_general(
            panels, taken, (((1,), (1,)), ((), ())), preferred_element_type=jnp.float32
        )
        cols = jnp.where(slots < count[r : r + 1, :], PB * col[:1].astype(jnp.int32) + c, -1)
        cols_ref[r : r + 1, :] = cols[:, :WIDTH]
        starts_ref[r : r + 1, :] = jnp.broadcast_to(start, (1, 1))
        start = start + count[r : r + 1, :]
    for w in range(WIN):
        at = (p0 - HP + w) & (NP - 1)
        row = tab_ref[at >> 3, pl.ds(at & 7, 1), :]
        map_ref[w : w + 1, :] = (((row >> 2) - at + HP) & (NP - 1)) + w
        if w == HP:
            map_ref[WIN : WIN + 1, :] = (row - PB * (p0 - HP)) & (PB * NP - 1)
    map_ref[WIN + 1 : 16, :] = rank[: 16 - WIN - 1, :]


def square_kernel(map_ref, left_ref, pair_ref, next_ref, swap_ref, far_ref, last_ref, *refs):
    out_ref = refs[0]
    lefts, rights = refs[1:3]
    sums = refs[3 : 3 + PB]
    staged, blank, in_sem, zero_sem, out_sem = refs[3 + PB :]
    p0, c = place()
    core = p0 & 1
    blank[...] = jnp.zeros(blank.shape, blank.dtype)
    for r in range(PB):
        pltpu.make_async_copy(blank, out_ref.at[r, USED:], zero_sem.at[r]).start()
    moves = (
        (pair_ref, 0, HP, HP),
        (pair_ref, 1, 5, 3),
        (next_ref, 0, 2, 6),
        (next_ref, 1, 3, 5),
        (swap_ref, 0, 7, 1),
        (swap_ref, 1, 6, 2),
        (far_ref, 1, 1, 7),
    )
    copies = [pltpu.make_async_copy(left_ref, lefts, in_sem.at[WIN])]
    for n, (ref, half, even, odd) in enumerate(moves):
        w = jnp.where(core == 0, even, odd)
        copies.append(pltpu.make_async_copy(ref.at[half], rights.at[w], in_sem.at[n]))
    for copy in copies:
        copy.start()
    low = pltpu.make_async_copy(far_ref.at[0], rights.at[0], in_sem.at[WIN - 1])
    crossed = pltpu.make_async_copy(last_ref, rights.at[0], in_sem.at[WIN - 1])
    pl.when(core == 0)(low.start)
    pl.when(core == 1)(crossed.start)
    for r in range(PB):
        sums[r][...] = jnp.zeros((USED, BS, BS), jnp.float32)
    for copy in copies:
        copy.wait()
    low.wait()

    def group_step(g, carry):
        for s0 in range(KG):
            for r in range(PB):
                local = map_ref[WIN, PER * g + KG * r + s0]
                w = local >> 2
                kr = local & (PB - 1)
                slots = []
                for s in range(KG):
                    slots.append(map_ref[WIN + 1 + r, map_ref[w, PER * c + KG * kr + s]])
                right = jnp.concatenate([rights[w, kr, s] for s in range(KG)], axis=1)
                product = jnp.dot(lefts[g, r, s0], right, preferred_element_type=jnp.float32)
                new = [
                    sums[r][slots[s]] + product[:, BS * s : BS * (s + 1)] for s in range(KG)
                ]
                for s in range(KG):
                    sums[r][slots[s]] = new[s]
        return carry

    lax.fori_loop(0, GROUPS, group_step, 0)
    for r in range(PB):
        staged[r] = sums[r][...].astype(jnp.bfloat16)
        pltpu.make_async_copy(staged.at[r], out_ref.at[r, :USED], out_sem.at[r]).start()
    for r in range(PB):
        pltpu.make_async_copy(blank, out_ref.at[r, USED:], zero_sem.at[r]).wait()
        pltpu.make_async_copy(staged.at[r], out_ref.at[r, :USED], out_sem.at[r]).wait()


VMEM = pl.BlockSpec(memory_space=pltpu.VMEM)
SMEM = pl.BlockSpec(memory_space=pltpu.SMEM)
HBM = pl.BlockSpec(memory_space=pl.ANY)


def spread(cols):
    return pl.pallas_call(
        spread_kernel,
        out_shape=jax.ShapeDtypeStruct((32, 1, BS), jnp.int32),
        in_specs=[SMEM],
        out_specs=VMEM,
        name="spread",
    )(cols)


def slab_table(parts):
    return pl.pallas_call(
        slab_kernel,
        out_shape=jax.ShapeDtypeStruct((16, 8, BS), jnp.int32),
        in_specs=[VMEM],
        out_specs=VMEM,
        name="slab_table",
    )(parts)


def indices(table):
    return pl.pallas_call(
        index_kernel,
        out_shape=(
            jax.ShapeDtypeStruct((PB, WIDTH), jnp.int32),
            jax.ShapeDtypeStruct((PB, 1), jnp.int32),
            jax.ShapeDtypeStruct((16, BS), jnp.int32),
        ),
        in_specs=[VMEM],
        out_specs=(VMEM, VMEM, VMEM),
        scratch_shapes=[pltpu.VMEM((BS, NP), jnp.int32)],
        name="indices",
    )(table)


def square(where, left, pieces):
    return pl.pallas_call(
        square_kernel,
        out_shape=jax.ShapeDtypeStruct((PB, WIDTH, BS, BS), jnp.bfloat16),
        in_specs=[SMEM] + [HBM] * (1 + len(pieces)),
        out_specs=HBM,
        scratch_shapes=[
            pltpu.VMEM((GROUPS, PB, KG, BS, BS), jnp.bfloat16),
            pltpu.VMEM((WIN, PB, KG, BS, BS), jnp.bfloat16),
        ]
        + [pltpu.VMEM((USED, BS, BS), jnp.float32) for _ in range(PB)]
        + [
            pltpu.VMEM((PB, USED, BS, BS), jnp.bfloat16),
            pltpu.VMEM((WIDTH - USED, BS, BS), jnp.bfloat16),
            pltpu.SemaphoreType.DMA((WIN + 1,)),
            pltpu.SemaphoreType.DMA((PB,)),
            pltpu.SemaphoreType.DMA((PB,)),
        ],
        name="square",
    )(where, left, *pieces)


def exchange(array, axes):
    return lax.all_to_all(array, axes, 0, 0, tiled=True)


def swapped(block):
    return lax.ppermute(block, "rows_2", [(0, 1), (1, 0)])


def outward(pair):
    chips = NP // 2
    route = []
    for q in range(chips):
        route.append((2 * q, 2 * ((q + 1) % chips)))
        route.append((2 * q + 1, 2 * ((q - 1) % chips) + 1))
    return lax.ppermute(pair, ROWS, route)


def on_device(blocks, block_cols):
    own = blocks[:, 0]
    parts = exchange(spread(block_cols[:, 0]), SLAB)
    table = exchange(slab_table(parts), "rows_0")
    columns, starts, where = indices(table)
    partner = swapped(own)
    pair = jnp.stack([own, partner])
    near = outward(pair)
    left = exchange(jnp.broadcast_to(own[None], (GROUPS, *own.shape)), "cols")
    far = outward(near)
    swap = swapped(near)
    last = lax.ppermute(far[1], "rows_2", [(0, 1)])
    out = square(where, left, (pair, near, swap, far, last))
    return out[:, None], columns[:, None], starts


def solution(mesh):
    split = Mesh(
        mesh.devices.reshape(16, 4, 2, mesh.shape["cols"]), ("rows_0", "rows_1", "rows_2", "cols")
    )
    return jax.shard_map(
        on_device,
        mesh=split,
        in_specs=(P(ROWS, "cols", None, None, None), P(ROWS, "cols", None)),
        out_specs=(P(ROWS, "cols", None, None, None), P(ROWS, "cols", None), P(ROWS, "cols")),
        check_vma=False,
    )
```

time: 96.8 us -> 88.5 us (0.914)
  blocking collectives: 41.6 us -> 11.4 us
  waiting for transfers between devices: 0.51 us -> 17 us
  starting transfers between devices: 30 us -> 38.6 us
  local copies, waits for them, and re-layouts: 8.63 us -> 5.83 us
  other arithmetic: 2.74 us -> 1.07 us
    all_to_all x2 -> x1, blocking collectives: 41.6 us -> 11.4 us  [exchange(): return lax.all_to_all(array, axes, 0, 0, tiled=True)]
    all_to_all x1 -> x2, waiting for transfers between devices: 0.01 us -> 15.5 us  [exchange(): return lax.all_to_all(array, axes, 0, 0, tiled=True)]
    all_to_all x1 -> x2, starting transfers between devices: 3.69 us -> 11 us  [exchange(): return lax.all_to_all(array, axes, 0, 0, tiled=True)]
    all_to_all x2 -> x0, other arithmetic: 2.74 us -> none  [sent_to_all(): lax.all_to_all(jnp.broadcast_to(shard[None], (size, *shard.shape)), axis,...]
    pallas_call x0 -> x2, Pallas kernels: none -> 2.68 us  [the longest x1 1.36 us: slab_table(): pl.pallas_call(slab_kernel, out_shape=jax.ShapeDtypeStruct((16, 8, BS), j...]
    pallas_call x1, Pallas kernels: 4.17 us -> 2 us  [indices(): pl.pallas_call(index_kernel, out_shape=(jax.ShapeDtypeStruct((PB, WIDTH),...]
    unnamed x16 -> x18, local copies, waits for them, and re-layouts: 4.91 us -> 3.47 us
    ppermute x7 -> x5, starting transfers between devices: 26.3 us -> 27.6 us  [the longest x2 13.3 us: outward(): return lax.ppermute(pair, ROWS, route)]
  transfers between devices with their start and end apart: 8 -> 7, of which waited for: 1 -> 3; matrix products, arithmetic and copies ran while one was open for 5% -> 5% of each run, Pallas kernels for 4% -> 5%
where the time goes in v2:
time: 88.5 us; the launch traced here: 86.9 us
  starting transfers between devices  38.6 us (44%)
  waiting for transfers between devices  17 us (19%)
  Pallas kernels  12.2 us (14%)
  blocking collectives  11.4 us (13%)
  local copies, waits for them, and re-layouts  5.83 us (7%)
  other arithmetic  1.07 us (1%)
    all_to_all x2, waiting for transfers between devices, exchange(): return lax.all_to_all(array, axes, 0, 0, tiled=True)  15.5 us
    ppermute x2, starting transfers between devices, outward(): return lax.ppermute(pair, ROWS, route)  13.3 us
    ppermute x2, starting transfers between devices, swapped(): return lax.ppermute(block, 'rows_2', [(0, 1), (1, 0)])  13 us
    all_to_all x1, blocking collectives, exchange(): return lax.all_to_all(array, axes, 0, 0, tiled=True)  11.4 us
    all_to_all x2, starting transfers between devices, exchange(): return lax.all_to_all(array, axes, 0, 0, tiled=True)  11 us
    pallas_call x1, Pallas kernels, square(): pl.pallas_call(square_kernel, out_shape=jax.ShapeDtypeStruct((PB, WIDTH,...  7.56 us
    unnamed x18, local copies, waits for them, and re-layouts  3.47 us
    pallas_call x1, Pallas kernels, indices(): pl.pallas_call(index_kernel, out_shape=(jax.ShapeDtypeStruct((PB, WIDTH),...  2 us
  transfers between devices with their start and end apart: 7, of which 3 were waited for; matrix products, arithmetic and copies ran while one was open for 5% of the time, Pallas kernels for 5%

profile of v2, /device:TPU:1, one launch (start us, length us, event | category | flops | bytes accessed | tf_op | source)
XLA Modules:
  0.0 86.9 jit_solution(13243595750268787154)
XLA Ops:
  0.6 0.0 copy-start.3
  0.6 0.0 copy-start.7
  0.7 8.9 %collective-permute-start = (bf16[4,3,128,128]{3,2,1,0:T(8,128)(2,1)}, bf16[4,3,128,128]{3,2,1,0:T(8,128)(2,1)S(1)}, u32[]{:S(2)}, u32[]{:S(2)}) collective-permute-start(bf16[4,3,128,128]{3,2,1,0:T(8,128)(2,1)} %bitcast.13), channel_id=1, source_target_pairs={{0,4},{4,0},{1,5},{5,1},{2,6},{6,2},{3,7},{7,3},{8,12},{12,8},{9,1... | collective-permute-start | bytes 1179656 | tf_op jit(solution)/shard_map/ppermute | solution.py:250
  9.5 1.5 %collective-permute-done = bf16[4,3,128,128]{3,2,1,0:T(8,128)(2,1)S(1)} collective-permute-done((bf16[4,3,128,128]{3,2,1,0:T(8,128)(2,1)}, bf16[4,3,128,128]{3,2,1,0:T(8,128)(2,1)S(1)}, u32[]{:S(2)}, u32[]{:S(2)}) %collective-permute-start) | collective-permute-done | bytes 393248 | tf_op jit(solution)/shard_map/ppermute | solution.py:250
  11.1 1.1 %pad_maximum_fusion.pair_ref = bf16[2,4,3,128,128]{4,3,2,1,0:T(8,128)(2,1)S(1)} fusion(bf16[1,4,3,128,128]{4,3,2,1,0:T(8,128)(2,1)S(1)} %bitcast.16, bf16[1,4,3,128,128]{4,3,2,1,0:T(8,128)(2,1)} %bitcast.14), kind=kLoop, calls=%fused_computation | loop fusion | flops 393216 | bytes 1572864 | tf_op jit(solution)/shard_map/stack | solution.py:268
  12.2 8.2 %collective-permute-start.1 = (bf16[2,4,3,128,128]{4,3,2,1,0:T(8,128)(2,1)S(1)}, bf16[2,4,3,128,128]{4,3,2,1,0:T(8,128)(2,1)}, u32[]{:S(2)}, u32[]{:S(2)}) collective-permute-start(bf16[2,4,3,128,128]{4,3,2,1,0:T(8,128)(2,1)S(1)} %pad_maximum_fusion.pair_ref), channel_id=1, source_target_pairs={{0,8},{4,508},{8,16},{12,4},{16,24},{20,12},{24,32},{28,20},{32,40... | collective-permute-start | bytes 2359304 | tf_op jit(solution)/shard_map/ppermute | solution.py:259
  20.4 0.7 copy.5
  21.1 1.3 %spread.1 = s32[32,1,128]{2,1,0:T(1,128)} custom-call(s32[4,3]{1,0:T(4,128)} %bitcast.17), custom_call_target="tpu_custom_call" | custom-call | tf_op jit(solution)/shard_map/spread/pallas_call | solution.py:189
  22.4 11.4 %all_to_all.15.in_ref = s32[32,1,128]{2,1,0:T(1,128)} all-to-all(s32[32,1,128]{2,1,0:T(1,128)} %spread.1), channel_id=1, replica_groups=mesh['rows_0'=16,'rows_1'=4,'rows_2'=2,'cols'=4] {'rows_1','rows_2','cols'}, dimensions={0} | all-to-all | bytes 32768 | tf_op jit(solution)/shard_map/all_to_all | solution.py:246
  33.8 1.4 %slab_table.1 = s32[16,8,128]{2,1,0:T(8,128)} custom-call(s32[32,1,128]{2,1,0:T(1,128)} %all_to_all.15.in_ref), custom_call_target="tpu_custom_call" | custom-call | tf_op jit(solution)/shard_map/slab_table/pallas_call | solution.py:199
  35.2 7.4 %all-to-all-start.1 = ((s32[16,8,128]{2,1,0:T(8,128)}), s32[16,8,128]{2,1,0:T(8,128)S(1)}, u32[]{:S(2)}, u32[]{:S(2)}) async-start(s32[16,8,128]{2,1,0:T(8,128)} %slab_table.1), calls=%async_computation.1 | async-start | bytes 131072 | tf_op jit(solution)/shard_map/all_to_all | solution.py:246
  42.6 0.0 collective-permute-done.1.next_ref
  42.6 5.1 %collective-permute-start.3 = (bf16[2,4,3,128,128]{4,3,2,1,0:T(8,128)(2,1)}, bf16[2,4,3,128,128]{4,3,2,1,0:T(8,128)(2,1)S(1)}, u32[]{:S(2)}, u32[]{:S(2)}) collective-permute-start(bf16[2,4,3,128,128]{4,3,2,1,0:T(8,128)(2,1)} %collective-permute-done.1.next_ref), channel_id=1, source_target_pairs={{0,8},{4,508},{8,16},{12,4},{16,24},{20,12},{24,32},{28,20},{32,40... | collective-permute-start | bytes 2359304 | tf_op jit(solution)/shard_map/ppermute | solution.py:259
  47.7 6.5 %all-to-all-done.1.tab_ref = s32[16,8,128]{2,1,0:T(8,128)S(1)} async-done(((s32[16,8,128]{2,1,0:T(8,128)}), s32[16,8,128]{2,1,0:T(8,128)S(1)}, u32[]{:S(2)}, u32[]{:S(2)}) %all-to-all-start.1) | async-done | bytes 65568 | tf_op jit(solution)/shard_map/all_to_all | solution.py:246
  54.2 1.5 %broadcast_in_dim.14 = bf16[4,4,3,128,128]{4,3,2,1,0:T(8,128)(2,1)} broadcast(bf16[4,3,128,128]{3,2,1,0:T(8,128)(2,1)S(1)} %bitcast.15), dimensions={1,2,3,4} | broadcast | bytes 1966080 | tf_op jit(solution)/shard_map/broadcast_in_dim | solution.py:270
  55.7 3.6 %all-to-all-start.2 = ((bf16[4,4,3,128,128]{4,3,2,1,0:T(8,128)(2,1)}), bf16[4,4,3,128,128]{4,3,2,1,0:T(8,128)(2,1)S(1)}, u32[]{:S(2)}, u32[]{:S(2)}) async-start(bf16[4,4,3,128,128]{4,3,2,1,0:T(8,128)(2,1)} %broadcast_in_dim.14), calls=%async_computation.2 | async-start | bytes 3145728 | tf_op jit(solution)/shard_map/all_to_all | solution.py:246
  59.3 4.1 %collective-permute-start.2 = (bf16[2,4,3,128,128]{4,3,2,1,0:T(8,128)(2,1)}, bf16[2,4,3,128,128]{4,3,2,1,0:T(8,128)(2,1)S(1)}, u32[]{:S(2)}, u32[]{:S(2)}) collective-permute-start(bf16[2,4,3,128,128]{4,3,2,1,0:T(8,128)(2,1)} %collective-permute-done.1.next_ref), channel_id=1, source_target_pairs={{0,4},{4,0},{1,5},{5,1},{2,6},{6,2},{3,7},{7,3},{8,12},{12,8},{9,1... | collective-permute-start | bytes 2359304 | tf_op jit(solution)/shard_map/ppermute | solution.py:250
  63.4 0.0 collective-permute-done.3.far_ref
  63.4 0.0 copy-start.2
  63.4 0.8 slice_bitcast_fusion
  64.3 1.3 %collective-permute-start.4 = (bf16[4,3,128,128]{3,2,1,0:T(8,128)(2,1)}, bf16[4,3,128,128]{3,2,1,0:T(8,128)(2,1)S(1)}, u32[]{:S(2)}, u32[]{:S(2)}) collective-permute-start(bf16[4,3,128,128]{3,2,1,0:T(8,128)(2,1)} %slice_bitcast_fusion), channel_id=1, source_target_pairs={{0,4},{1,5},{2,6},{3,7},{8,12},{9,13},{10,14},{11,15},{16,20},{17,... | collective-permute-start | bytes 1179656 | tf_op jit(solution)/shard_map/ppermute | solution.py:273
  65.5 2.0 %indices.1 = (s32[4,36]{1,0:T(4,128)}, s32[4,1]{1,0:T(4,128)}, s32[16,128]{1,0:T(8,128)}) custom-call(s32[16,8,128]{2,1,0:T(8,128)} %copy-done.6), custom_call_target="tpu_custom_call" | custom-call | tf_op jit(solution)/shard_map/indices/pallas_call | solution.py:209
  67.5 1.2 %copy.8 = s32[4,1]{0,1:T(1,128)} copy(s32[4,1]{1,0:T(4,128)} %get-tuple-element.11) | data formatting | bytes 32
  68.8 9.0 %all-to-all-done.2.left_ref = bf16[4,4,3,128,128]{4,3,2,1,0:T(8,128)(2,1)S(1)} async-done(((bf16[4,4,3,128,128]{4,3,2,1,0:T(8,128)(2,1)}), bf16[4,4,3,128,128]{4,3,2,1,0:T(8,128)(2,1)S(1)}, u32[]{:S(2)}, u32[]{:S(2)}) %all-to-all-start.2) | async-done | bytes 1572896 | tf_op jit(solution)/shard_map/all_to_all | solution.py:246
  77.8 0.0 collective-permute-done.2.swap_ref
  77.8 0.0 collective-permute-done.4.last_ref
  77.8 0.0 copy-start.5
  77.8 0.0 copy-done.2
  77.8 1.1 %copy-done = bf16[4,4,3,128,128]{4,3,2,1,0:T(8,128)(2,1)} copy-done((bf16[4,4,3,128,128]{4,3,2,1,0:T(8,128)(2,1)}, bf16[4,4,3,128,128]{4,3,2,1,0:T(8,128)(2,1)S(1)}, u32[]{:S(2)}) %copy-start) | copy-done | bytes 1572888
  79.0 0.3 copy-done.4
  79.3 0.1 copy-done.5
  79.4 7.6 %square.1 = bf16[4,36,128,128]{3,2,1,0:T(8,128)(2,1)} custom-call(s32[16,128]{1,0:T(8,128)} %get-tuple-element.6.map_ref, bf16[4,4,3,128,128]{4,3,2,1,0:T(8,128)(2,1)} %copy-done, bf16[2,4,3,128,128]{4,3,2,1,0:T(8,128)(2,1)} %copy-done.1, bf16[2,4,3,128,128]{4,3,2,1,0:T(8,128)(2,1)} %collective-permute-done.1.next_ref, ...), custom_call_target="tpu_custom_call" | custom-call | tf_op jit(solution)/shard_map/square/pallas_call | solution.py:224
  (8 shorter events, 0.0 us)
Async XLA Ops:
  0.6 53.5 %copy-start.3 = (bf16[4,1,3,128,128]{4,3,2,1,0:T(8,128)(2,1)S(1)}, bf16[4,1,3,128,128]{4,3,2,1,0:T(8,128)(2,1)}, u32[]{:S(2)}) copy-start(bf16[4,1,3,128,128]{4,3,2,1,0:T(8,128)(2,1)} %param.2) | copy-start | bytes 1179652
  0.6 19.8 %copy-start.7 = (s32[4,1,3]{0,1,2:T(1,128)S(1)}, s32[4,1,3]{0,1,2:T(1,128)}, u32[]{:S(2)}) copy-start(s32[4,1,3]{0,1,2:T(1,128)} %param.3) | copy-start | bytes 148
  0.7 10.4 %collective-permute-start = (bf16[4,3,128,128]{3,2,1,0:T(8,128)(2,1)}, bf16[4,3,128,128]{3,2,1,0:T(8,128)(2,1)S(1)}, u32[]{:S(2)}, u32[]{:S(2)}) collective-permute-start(bf16[4,3,128,128]{3,2,1,0:T(8,128)(2,1)} %bitcast.13), channel_id=1, source_target_pairs={{0,4},{4,0},{1,5},{5,1},{2,6},{6,2},{3,7},{7,3},{8,12},{12,8},{9,1... | collective-permute-start | bytes 1179656 | tf_op jit(solution)/shard_map/ppermute | solution.py:250
  12.1 43.5 %copy-start.1 = (bf16[2,4,3,128,128]{4,3,2,1,0:T(8,128)(2,1)}, bf16[2,4,3,128,128]{4,3,2,1,0:T(8,128)(2,1)S(1)}, u32[]{:S(2)}) copy-start(bf16[2,4,3,128,128]{4,3,2,1,0:T(8,128)(2,1)S(1)} %pad_maximum_fusion.pair_ref) | copy-start | bytes 2359300
  12.2 30.4 %collective-permute-start.1 = (bf16[2,4,3,128,128]{4,3,2,1,0:T(8,128)(2,1)S(1)}, bf16[2,4,3,128,128]{4,3,2,1,0:T(8,128)(2,1)}, u32[]{:S(2)}, u32[]{:S(2)}) collective-permute-start(bf16[2,4,3,128,128]{4,3,2,1,0:T(8,128)(2,1)S(1)} %pad_maximum_fusion.pair_ref), channel_id=1, source_target_pairs={{0,8},{4,508},{8,16},{12,4},{16,24},{20,12},{24,32},{28,20},{32,40... | collective-permute-start | bytes 2359304 | tf_op jit(solution)/shard_map/ppermute | solution.py:259
  35.2 19.0 %all-to-all-start.1 = ((s32[16,8,128]{2,1,0:T(8,128)}), s32[16,8,128]{2,1,0:T(8,128)S(1)}, u32[]{:S(2)}, u32[]{:S(2)}) async-start(s32[16,8,128]{2,1,0:T(8,128)} %slab_table.1), calls=%async_computation.1 | async-start | bytes 131072 | tf_op jit(solution)/shard_map/all_to_all | solution.py:246
  42.6 20.8 %collective-permute-start.3 = (bf16[2,4,3,128,128]{4,3,2,1,0:T(8,128)(2,1)}, bf16[2,4,3,128,128]{4,3,2,1,0:T(8,128)(2,1)S(1)}, u32[]{:S(2)}, u32[]{:S(2)}) collective-permute-start(bf16[2,4,3,128,128]{4,3,2,1,0:T(8,128)(2,1)} %collective-permute-done.1.next_ref), channel_id=1, source_target_pairs={{0,8},{4,508},{8,16},{12,4},{16,24},{20,12},{24,32},{28,20},{32,40... | collective-permute-start | bytes 2359304 | tf_op jit(solution)/shard_map/ppermute | solution.py:259
  54.2 1.5 %copy-start.6 = (s32[16,8,128]{2,1,0:T(8,128)}, s32[16,8,128]{2,1,0:T(8,128)S(1)}, u32[]{:S(2)}) copy-start(s32[16,8,128]{2,1,0:T(8,128)S(1)} %all-to-all-done.1.tab_ref) | copy-start | bytes 196612
  55.7 22.1 %all-to-all-start.2 = ((bf16[4,4,3,128,128]{4,3,2,1,0:T(8,128)(2,1)}), bf16[4,4,3,128,128]{4,3,2,1,0:T(8,128)(2,1)S(1)}, u32[]{:S(2)}, u32[]{:S(2)}) async-start(bf16[4,4,3,128,128]{4,3,2,1,0:T(8,128)(2,1)} %broadcast_in_dim.14), calls=%async_computation.2 | async-start | bytes 3145728 | tf_op jit(solution)/shard_map/all_to_all | solution.py:246
  59.3 18.6 %collective-permute-start.2 = (bf16[2,4,3,128,128]{4,3,2,1,0:T(8,128)(2,1)}, bf16[2,4,3,128,128]{4,3,2,1,0:T(8,128)(2,1)S(1)}, u32[]{:S(2)}, u32[]{:S(2)}) collective-permute-start(bf16[2,4,3,128,128]{4,3,2,1,0:T(8,128)(2,1)} %collective-permute-done.1.next_ref), channel_id=1, source_target_pairs={{0,4},{4,0},{1,5},{5,1},{2,6},{6,2},{3,7},{7,3},{8,12},{12,8},{9,1... | collective-permute-start | bytes 2359304 | tf_op jit(solution)/shard_map/ppermute | solution.py:250
  63.4 14.4 %copy-start.2 = (bf16[2,4,3,128,128]{4,3,2,1,0:T(8,128)(2,1)}, bf16[2,4,3,128,128]{4,3,2,1,0:T(8,128)(2,1)S(1)}, u32[]{:S(2)}) copy-start(bf16[2,4,3,128,128]{4,3,2,1,0:T(8,128)(2,1)S(1)} %collective-permute-done.3.far_ref) | copy-start | bytes 2359300
  64.3 13.6 %collective-permute-start.4 = (bf16[4,3,128,128]{3,2,1,0:T(8,128)(2,1)}, bf16[4,3,128,128]{3,2,1,0:T(8,128)(2,1)S(1)}, u32[]{:S(2)}, u32[]{:S(2)}) collective-permute-start(bf16[4,3,128,128]{3,2,1,0:T(8,128)(2,1)} %slice_bitcast_fusion), channel_id=1, source_target_pairs={{0,4},{1,5},{2,6},{3,7},{8,12},{9,13},{10,14},{11,15},{16,20},{17,... | collective-permute-start | bytes 1179656 | tf_op jit(solution)/shard_map/ppermute | solution.py:273
  77.8 1.2 %copy-start = (bf16[4,4,3,128,128]{4,3,2,1,0:T(8,128)(2,1)}, bf16[4,4,3,128,128]{4,3,2,1,0:T(8,128)(2,1)S(1)}, u32[]{:S(2)}) copy-start(bf16[4,4,3,128,128]{4,3,2,1,0:T(8,128)(2,1)S(1)} %all-to-all-done.2.left_ref) | copy-start | bytes 4718596
  77.8 1.4 %copy-start.4 = (bf16[2,4,3,128,128]{4,3,2,1,0:T(8,128)(2,1)}, bf16[2,4,3,128,128]{4,3,2,1,0:T(8,128)(2,1)S(1)}, u32[]{:S(2)}) copy-start(bf16[2,4,3,128,128]{4,3,2,1,0:T(8,128)(2,1)S(1)} %collective-permute-done.2.swap_ref) | copy-start | bytes 2359300
  77.8 1.6 %copy-start.5 = (bf16[4,3,128,128]{3,2,1,0:T(8,128)(2,1)}, bf16[4,3,128,128]{3,2,1,0:T(8,128)(2,1)S(1)}, u32[]{:S(2)}) copy-start(bf16[4,3,128,128]{3,2,1,0:T(8,128)(2,1)S(1)} %collective-permute-done.4.last_ref) | copy-start | bytes 1179652

commit v3 on v2

--- a/solution.py
+++ b/solution.py
@@ -107,7 +107,7 @@
         )
         cols = jnp.where(slots < count[r : r + 1, :], PB * col[:1].astype(jnp.int32) + c, -1)
         cols_ref[r : r + 1, :] = cols[:, :WIDTH]
-        starts_ref[r : r + 1, :] = jnp.broadcast_to(start, (1, 1))
+        starts_ref[:, r : r + 1] = jnp.broadcast_to(start, (1, 1))
         start = start + count[r : r + 1, :]
     for w in range(WIN):
         at = (p0 - HP + w) & (NP - 1)
@@ -118,11 +118,11 @@
     map_ref[WIN + 1 : 16, :] = rank[: 16 - WIN - 1, :]
 
 
-def square_kernel(map_ref, left_ref, pair_ref, next_ref, swap_ref, far_ref, last_ref, *refs):
+def square_kernel(map_ref, up_ref, over_ref, down_ref, pair_ref, next_ref, swap_ref, far_ref, last_ref, *refs):
     out_ref = refs[0]
-    lefts, rights = refs[1:3]
-    sums = refs[3 : 3 + PB]
-    staged, blank, in_sem, zero_sem, out_sem = refs[3 + PB :]
+    rights = refs[1]
+    sums = refs[2 : 2 + PB]
+    staged, blank, in_sem, zero_sem, out_sem = refs[2 + PB :]
     p0, c = place()
     core = p0 & 1
     blank[...] = jnp.zeros(blank.shape, blank.dtype)
@@ -137,7 +137,7 @@
         (swap_ref, 1, 6, 2),
         (far_ref, 1, 1, 7),
     )
-    copies = [pltpu.make_async_copy(left_ref, lefts, in_sem.at[WIN])]
+    copies = []
     for n, (ref, half, even, odd) in enumerate(moves):
         w = jnp.where(core == 0, even, odd)
         copies.append(pltpu.make_async_copy(ref.at[half], rights.at[w], in_sem.at[n]))
@@ -153,8 +153,10 @@
         copy.wait()
     low.wait()
 
-    def group_step(g, carry):
-        for s0 in range(KG):
+    def block_step(s0, carry):
+        for d in range(GROUPS):
+            g = (c + d) & (GROUPS - 1)
+            left_ref = (None, up_ref, over_ref, down_ref)[d]
             for r in range(PB):
                 local = map_ref[WIN, PER * g + KG * r + s0]
                 w = local >> 2
@@ -163,7 +165,8 @@
                 for s in range(KG):
                     slots.append(map_ref[WIN + 1 + r, map_ref[w, PER * c + KG * kr + s]])
                 right = jnp.concatenate([rights[w, kr, s] for s in range(KG)], axis=1)
-                product = jnp.dot(lefts[g, r, s0], right, preferred_element_type=jnp.float32)
+                left = left_ref[r, s0] if d else pair_ref[0, r, s0]
+                product = jnp.dot(left, right, preferred_element_type=jnp.float32)
                 new = [
                     sums[r][slots[s]] + product[:, BS * s : BS * (s + 1)] for s in range(KG)
                 ]
@@ -171,7 +174,7 @@
                     sums[r][slots[s]] = new[s]
         return carry
 
-    lax.fori_loop(0, GROUPS, group_step, 0)
+    lax.fori_loop(0, KG, block_step, 0)
     for r in range(PB):
         staged[r] = sums[r][...].astype(jnp.bfloat16)
         pltpu.make_async_copy(staged.at[r], out_ref.at[r, :USED], out_sem.at[r]).start()
@@ -183,6 +186,10 @@
 VMEM = pl.BlockSpec(memory_space=pltpu.VMEM)
 SMEM = pl.BlockSpec(memory_space=pltpu.SMEM)
 HBM = pl.BlockSpec(memory_space=pl.ANY)
+
+
+def near_core(array):
+    return pltpu.with_memory_space_constraint(array, pltpu.VMEM)
 
 
 def spread(cols):
@@ -191,6 +198,7 @@
         out_shape=jax.ShapeDtypeStruct((32, 1, BS), jnp.int32),
         in_specs=[SMEM],
         out_specs=VMEM,
+        compiler_params=pltpu.CompilerParams(vmem_limit_bytes=8 << 20),
         name="spread",
     )(cols)
 
@@ -201,6 +209,7 @@
         out_shape=jax.ShapeDtypeStruct((16, 8, BS), jnp.int32),
         in_specs=[VMEM],
         out_specs=VMEM,
+        compiler_params=pltpu.CompilerParams(vmem_limit_bytes=8 << 20),
         name="slab_table",
     )(parts)
 
@@ -210,36 +219,37 @@
         index_kernel,
         out_shape=(
             jax.ShapeDtypeStruct((PB, WIDTH), jnp.int32),
-            jax.ShapeDtypeStruct((PB, 1), jnp.int32),
+            jax.ShapeDtypeStruct((1, PB), jnp.int32),
             jax.ShapeDtypeStruct((16, BS), jnp.int32),
         ),
         in_specs=[VMEM],
         out_specs=(VMEM, VMEM, VMEM),
         scratch_shapes=[pltpu.VMEM((BS, NP), jnp.int32)],
+        compiler_params=pltpu.CompilerParams(vmem_limit_bytes=8 << 20),
         name="indices",
     )(table)
 
 
-def square(where, left, pieces):
+def square(where, lefts, pieces):
     return pl.pallas_call(
         square_kernel,
         out_shape=jax.ShapeDtypeStruct((PB, WIDTH, BS, BS), jnp.bfloat16),
-        in_specs=[SMEM] + [HBM] * (1 + len(pieces)),
+        in_specs=[SMEM] + [VMEM] * (len(lefts) + len(pieces)),
         out_specs=HBM,
         scratch_shapes=[
-            pltpu.VMEM((GROUPS, PB, KG, BS, BS), jnp.bfloat16),
             pltpu.VMEM((WIN, PB, KG, BS, BS), jnp.bfloat16),
         ]
         + [pltpu.VMEM((USED, BS, BS), jnp.float32) for _ in range(PB)]
         + [
             pltpu.VMEM((PB, USED, BS, BS), jnp.bfloat16),
             pltpu.VMEM((WIDTH - USED, BS, BS), jnp.bfloat16),
-            pltpu.SemaphoreType.DMA((WIN + 1,)),
+            pltpu.SemaphoreType.DMA((WIN,)),
             pltpu.SemaphoreType.DMA((PB,)),
             pltpu.SemaphoreType.DMA((PB,)),
         ],
+        compiler_params=pltpu.CompilerParams(vmem_limit_bytes=24 << 20),
         name="square",
-    )(where, left, *pieces)
+    )(where, *[near_core(piece) for piece in (*lefts, *pieces)])
 
 
 def exchange(array, axes):
@@ -248,6 +258,10 @@
 
 def swapped(block):
     return lax.ppermute(block, "rows_2", [(0, 1), (1, 0)])
+
+
+def turned(block, distance):
+    return lax.ppermute(block, "cols", [((c + distance) % GROUPS, c) for c in range(GROUPS)])
 
 
 def outward(pair):
@@ -267,12 +281,14 @@
     partner = swapped(own)
     pair = jnp.stack([own, partner])
     near = outward(pair)
-    left = exchange(jnp.broadcast_to(own[None], (GROUPS, *own.shape)), "cols")
+    up = turned(own, 1)
+    down = turned(own, 3)
+    over = turned(own, 2)
     far = outward(near)
     swap = swapped(near)
     last = lax.ppermute(far[1], "rows_2", [(0, 1)])
-    out = square(where, left, (pair, near, swap, far, last))
-    return out[:, None], columns[:, None], starts
+    out = square(where, (up, over, down), (pair, near, swap, far, last))
+    return out[:, None], columns[:, None], starts.reshape(PB, 1)
 
 
 def solution(mesh):

time: 88.5 us -> 91.9 us (1.038)
  blocking collectives: 11.4 us -> 30.9 us
  waiting for transfers between devices: 17 us -> 10.5 us
  local copies, waits for them, and re-layouts: 5.83 us -> 1.54 us
  Pallas kernels: 12.2 us -> 8.2 us
    all_to_all x1 -> x2, blocking collectives: 11.4 us -> 30.9 us  [exchange(): return lax.all_to_all(array, axes, 0, 0, tiled=True)]
    all_to_all x2 -> x0, waiting for transfers between devices: 15.5 us -> none  [exchange(): return lax.all_to_all(array, axes, 0, 0, tiled=True)]
    all_to_all x2 -> x0, starting transfers between devices: 11 us -> none  [exchange(): return lax.all_to_all(array, axes, 0, 0, tiled=True)]
    ppermute x0 -> x3, starting transfers between devices: none -> 10.5 us  [turned(): lax.ppermute(block, 'cols', [((c + distance) % GROUPS, c) for c in range(...]
    ppermute x2, waiting for transfers between devices: 0.01 us -> 8.92 us  [outward(): return lax.ppermute(pair, ROWS, route)]
    unnamed x18 -> x1, local copies, waits for them, and re-layouts: 3.47 us -> 0.77 us
    ppermute x2, starting transfers between devices: 13 us -> 10.7 us  [swapped(): return lax.ppermute(block, 'rows_2', [(0, 1), (1, 0)])]
    ppermute x2, starting transfers between devices: 13.3 us -> 15.4 us  [outward(): return lax.ppermute(pair, ROWS, route)]
  transfers between devices with their start and end apart: 7 -> 8, of which waited for: 3 -> 2; matrix products, arithmetic and copies ran while one was open for 5% -> 2% of each run, Pallas kernels for 5% -> 2%
where the time goes in v3:
time: 91.9 us; the launch traced here: 90.8 us
  starting transfers between devices  37.8 us (41%)
  blocking collectives  30.9 us (34%)
  waiting for transfers between devices  10.5 us (11%)
  Pallas kernels  8.2 us (9%)
  local copies, waits for them, and re-layouts  1.54 us (2%)
  other arithmetic  1.07 us (1%)
    all_to_all x2, blocking collectives, exchange(): return lax.all_to_all(array, axes, 0, 0, tiled=True)  30.9 us
    ppermute x2, starting transfers between devices, outward(): return lax.ppermute(pair, ROWS, route)  15.4 us
    ppermute x2, starting transfers between devices, swapped(): return lax.ppermute(block, 'rows_2', [(0, 1), (1, 0)])  10.7 us
    ppermute x3, starting transfers between devices, turned(): lax.ppermute(block, 'cols', [((c + distance) % GROUPS, c) for c in range(...  10.5 us
    ppermute x2, waiting for transfers between devices, outward(): return lax.ppermute(pair, ROWS, route)  8.92 us
    pallas_call x1, Pallas kernels, square(): pl.pallas_call(square_kernel, out_shape=jax.ShapeDtypeStruct((PB, WIDTH,...  6.44 us
  transfers between devices with their start and end apart: 8, of which 2 were waited for; matrix products, arithmetic and copies ran while one was open for 2% of the time, Pallas kernels for 2%

profile of v3, /device:TPU:1, one launch (start us, length us, event | category | flops | bytes accessed | tf_op | source)
XLA Modules:
  0.0 90.8 jit_solution(18435423696016136323)
XLA Ops:
  0.6 8.7 %collective-permute-start.3 = (bf16[4,3,128,128]{3,2,1,0:T(8,128)(2,1)}, bf16[4,3,128,128]{3,2,1,0:T(8,128)(2,1)S(1)}, u32[]{:S(2)}, u32[]{:S(2)}) collective-permute-start(bf16[4,3,128,128]{3,2,1,0:T(8,128)(2,1)} %bitcast.15), channel_id=1, source_target_pairs={{0,4},{4,0},{1,5},{5,1},{2,6},{6,2},{3,7},{7,3},{8,12},{12,8},{9,1... | collective-permute-start | bytes 1179656 | tf_op jit(solution)/shard_map/ppermute | solution.py:260
  9.4 1.5 %collective-permute-done.3 = bf16[4,3,128,128]{3,2,1,0:T(8,128)(2,1)S(1)} collective-permute-done((bf16[4,3,128,128]{3,2,1,0:T(8,128)(2,1)}, bf16[4,3,128,128]{3,2,1,0:T(8,128)(2,1)S(1)}, u32[]{:S(2)}, u32[]{:S(2)}) %collective-permute-start.3) | collective-permute-done | bytes 393248 | tf_op jit(solution)/shard_map/ppermute | solution.py:260
  10.9 1.1 %pad_maximum_fusion.pair_ref = bf16[2,4,3,128,128]{4,3,2,1,0:T(8,128)(2,1)S(1)} fusion(bf16[1,4,3,128,128]{4,3,2,1,0:T(8,128)(2,1)S(1)} %bitcast.20, bf16[1,4,3,128,128]{4,3,2,1,0:T(8,128)(2,1)} %bitcast.16), kind=kLoop, calls=%fused_computation | loop fusion | flops 393216 | bytes 1572864 | tf_op jit(solution)/shard_map/stack | solution.py:282
  12.0 8.2 %collective-permute-start.4 = (bf16[2,4,3,128,128]{4,3,2,1,0:T(8,128)(2,1)S(1)}, bf16[2,4,3,128,128]{4,3,2,1,0:T(8,128)(2,1)S(1)}, u32[]{:S(2)}, u32[]{:S(2)}) collective-permute-start(bf16[2,4,3,128,128]{4,3,2,1,0:T(8,128)(2,1)S(1)} %pad_maximum_fusion.pair_ref), channel_id=1, source_target_pairs={{0,8},{4,508},{8,16},{12,4},{16,24},{20,12},{24,32},{28,20},{32,40... | collective-permute-start | bytes 2359304 | tf_op jit(solution)/shard_map/ppermute | solution.py:273
  20.2 8.9 %collective-permute-done.4.next_ref = bf16[2,4,3,128,128]{4,3,2,1,0:T(8,128)(2,1)S(1)} collective-permute-done((bf16[2,4,3,128,128]{4,3,2,1,0:T(8,128)(2,1)S(1)}, bf16[2,4,3,128,128]{4,3,2,1,0:T(8,128)(2,1)S(1)}, u32[]{:S(2)}, u32[]{:S(2)}) %collective-permute-start.4) | collective-permute-done | bytes 786464 | tf_op jit(solution)/shard_map/ppermute | solution.py:273
  29.1 7.1 %collective-permute-start.6 = (bf16[2,4,3,128,128]{4,3,2,1,0:T(8,128)(2,1)S(1)}, bf16[2,4,3,128,128]{4,3,2,1,0:T(8,128)(2,1)S(1)}, u32[]{:S(2)}, u32[]{:S(2)}) collective-permute-start(bf16[2,4,3,128,128]{4,3,2,1,0:T(8,128)(2,1)S(1)} %collective-permute-done.4.next_ref), channel_id=1, source_target_pairs={{0,8},{4,508},{8,16},{12,4},{16,24},{20,12},{24,32},{28,20},{32,40... | collective-permute-start | bytes 2359304 | tf_op jit(solution)/shard_map/ppermute | solution.py:273
  36.3 1.9 %collective-permute-start.5 = (bf16[2,4,3,128,128]{4,3,2,1,0:T(8,128)(2,1)S(1)}, bf16[2,4,3,128,128]{4,3,2,1,0:T(8,128)(2,1)S(1)}, u32[]{:S(2)}, u32[]{:S(2)}) collective-permute-start(bf16[2,4,3,128,128]{4,3,2,1,0:T(8,128)(2,1)S(1)} %collective-permute-done.4.next_ref), channel_id=1, source_target_pairs={{0,4},{4,0},{1,5},{5,1},{2,6},{6,2},{3,7},{7,3},{8,12},{12,8},{9,1... | collective-permute-start | bytes 2359304 | tf_op jit(solution)/shard_map/ppermute | solution.py:260
  38.2 3.1 %collective-permute-start.2 = (bf16[4,3,128,128]{3,2,1,0:T(8,128)(2,1)}, bf16[4,3,128,128]{3,2,1,0:T(8,128)(2,1)S(1)}, u32[]{:S(2)}, u32[]{:S(2)}) collective-permute-start(bf16[4,3,128,128]{3,2,1,0:T(8,128)(2,1)} %bitcast.17), channel_id=1, source_target_pairs={{3,0},{0,1},{1,2},{2,3},{7,4},{4,5},{5,6},{6,7},{11,8},{8,9},{9,10... | collective-permute-start | bytes 1179656 | tf_op jit(solution)/shard_map/ppermute | solution.py:264
  41.3 4.4 %collective-permute-start.1 = (bf16[4,3,128,128]{3,2,1,0:T(8,128)(2,1)}, bf16[4,3,128,128]{3,2,1,0:T(8,128)(2,1)}, u32[]{:S(2)}, u32[]{:S(2)}) collective-permute-start(bf16[4,3,128,128]{3,2,1,0:T(8,128)(2,1)} %bitcast.18), channel_id=1, source_target_pairs={{2,0},{3,1},{0,2},{1,3},{6,4},{7,5},{4,6},{5,7},{10,8},{11,9},{8,1... | collective-permute-start | bytes 1179656 | tf_op jit(solution)/shard_map/ppermute | solution.py:264
  45.7 3.1 %collective-permute-start = (bf16[4,3,128,128]{3,2,1,0:T(8,128)(2,1)}, bf16[4,3,128,128]{3,2,1,0:T(8,128)(2,1)}, u32[]{:S(2)}, u32[]{:S(2)}) collective-permute-start(bf16[4,3,128,128]{3,2,1,0:T(8,128)(2,1)} %bitcast.19), channel_id=1, source_target_pairs={{1,0},{2,1},{3,2},{0,3},{5,4},{6,5},{7,6},{4,7},{9,8},{10,9},{11,1... | collective-permute-start | bytes 1179656 | tf_op jit(solution)/shard_map/ppermute | solution.py:264
  48.8 0.0 collective-permute-done.6.far_ref
  48.8 0.8 slice_bitcast_fusion
  49.6 1.3 %collective-permute-start.7 = (bf16[4,3,128,128]{3,2,1,0:T(8,128)(2,1)}, bf16[4,3,128,128]{3,2,1,0:T(8,128)(2,1)}, u32[]{:S(2)}, u32[]{:S(2)}) collective-permute-start(bf16[4,3,128,128]{3,2,1,0:T(8,128)(2,1)} %slice_bitcast_fusion), channel_id=1, source_target_pairs={{0,4},{1,5},{2,6},{3,7},{8,12},{9,13},{10,14},{11,15},{16,20},{17,... | collective-permute-start | bytes 1179656 | tf_op jit(solution)/shard_map/ppermute | solution.py:289
  50.8 0.8 copy.5
  51.6 0.6 spread.1
  52.2 11.8 %all_to_all.10.in_ref = s32[32,1,128]{2,1,0:T(1,128)S(1)} all-to-all(s32[32,1,128]{2,1,0:T(1,128)S(1)} %spread.1), channel_id=1, replica_groups=mesh['rows_0'=16,'rows_1'=4,'rows_2'=2,'cols'=4] {'rows_1','rows_2','cols'}, dimensions={0} | all-to-all | bytes 32768 | tf_op jit(solution)/shard_map/all_to_all | solution.py:256
  64.0 19.1 %all_to_all.11.tab_ref = s32[16,8,128]{2,1,0:T(8,128)S(1)} all-to-all(s32[16,8,128]{2,1,0:T(8,128)S(1)} %slab_table.1), channel_id=1, replica_groups=mesh['rows_0'=16,'rows_1'=4,'rows_2'=2,'cols'=4] {'rows_0'}, dimensions={0} | all-to-all | bytes 131072 | tf_op jit(solution)/shard_map/all_to_all | solution.py:256
  83.1 1.2 %indices.1 = (s32[4,36]{1,0:T(4,128)}, s32[1,4]{1,0:T(1,128)}, s32[16,128]{1,0:T(8,128)S(1)}) custom-call(s32[16,8,128]{2,1,0:T(8,128)S(1)} %all_to_all.11.tab_ref), custom_call_target="tpu_custom_call" | custom-call | tf_op jit(solution)/shard_map/indices/pallas_call | solution.py:218
  84.3 0.0 collective-permute-done.2.down_ref
  84.3 0.0 collective-permute-done.1.over_ref
  84.3 0.0 collective-permute-done.up_ref
  84.3 0.0 collective-permute-done.5.swap_ref
  84.3 0.0 collective-permute-done.7.last_ref
  84.3 6.4 %square.1 = bf16[4,36,128,128]{3,2,1,0:T(8,128)(2,1)} custom-call(s32[16,128]{1,0:T(8,128)S(1)} %get-tuple-element.6.map_ref, bf16[4,3,128,128]{3,2,1,0:T(8,128)(2,1)} %collective-permute-done.up_ref, bf16[4,3,128,128]{3,2,1,0:T(8,128)(2,1)} %collective-permute-done.1.over_ref, bf16[4,3,128,128]{3,2,1,0:T(8,128)(2,1)S(1)} %collective-permute-done.2.down_ref, ...), custom_call_target="tpu_custom_call" | custom-call | tf_op jit(solution)/shard_map/square/pallas_call | solution.py:234
  (1 shorter events, 0.0 us)
Async XLA Ops:
  0.6 10.3 %collective-permute-start.3 = (bf16[4,3,128,128]{3,2,1,0:T(8,128)(2,1)}, bf16[4,3,128,128]{3,2,1,0:T(8,128)(2,1)S(1)}, u32[]{:S(2)}, u32[]{:S(2)}) collective-permute-start(bf16[4,3,128,128]{3,2,1,0:T(8,128)(2,1)} %bitcast.15), channel_id=1, source_target_pairs={{0,4},{4,0},{1,5},{5,1},{2,6},{6,2},{3,7},{7,3},{8,12},{12,8},{9,1... | collective-permute-start | bytes 1179656 | tf_op jit(solution)/shard_map/ppermute | solution.py:260
  12.0 17.1 %collective-permute-start.4 = (bf16[2,4,3,128,128]{4,3,2,1,0:T(8,128)(2,1)S(1)}, bf16[2,4,3,128,128]{4,3,2,1,0:T(8,128)(2,1)S(1)}, u32[]{:S(2)}, u32[]{:S(2)}) collective-permute-start(bf16[2,4,3,128,128]{4,3,2,1,0:T(8,128)(2,1)S(1)} %pad_maximum_fusion.pair_ref), channel_id=1, source_target_pairs={{0,8},{4,508},{8,16},{12,4},{16,24},{20,12},{24,32},{28,20},{32,40... | collective-permute-start | bytes 2359304 | tf_op jit(solution)/shard_map/ppermute | solution.py:273
  29.1 19.6 %collective-permute-start.6 = (bf16[2,4,3,128,128]{4,3,2,1,0:T(8,128)(2,1)S(1)}, bf16[2,4,3,128,128]{4,3,2,1,0:T(8,128)(2,1)S(1)}, u32[]{:S(2)}, u32[]{:S(2)}) collective-permute-start(bf16[2,4,3,128,128]{4,3,2,1,0:T(8,128)(2,1)S(1)} %collective-permute-done.4.next_ref), channel_id=1, source_target_pairs={{0,8},{4,508},{8,16},{12,4},{16,24},{20,12},{24,32},{28,20},{32,40... | collective-permute-start | bytes 2359304 | tf_op jit(solution)/shard_map/ppermute | solution.py:273
  36.3 48.0 %collective-permute-start.5 = (bf16[2,4,3,128,128]{4,3,2,1,0:T(8,128)(2,1)S(1)}, bf16[2,4,3,128,128]{4,3,2,1,0:T(8,128)(2,1)S(1)}, u32[]{:S(2)}, u32[]{:S(2)}) collective-permute-start(bf16[2,4,3,128,128]{4,3,2,1,0:T(8,128)(2,1)S(1)} %collective-permute-done.4.next_ref), channel_id=1, source_target_pairs={{0,4},{4,0},{1,5},{5,1},{2,6},{6,2},{3,7},{7,3},{8,12},{12,8},{9,1... | collective-permute-start | bytes 2359304 | tf_op jit(solution)/shard_map/ppermute | solution.py:260
  38.2 46.1 %collective-permute-start.2 = (bf16[4,3,128,128]{3,2,1,0:T(8,128)(2,1)}, bf16[4,3,128,128]{3,2,1,0:T(8,128)(2,1)S(1)}, u32[]{:S(2)}, u32[]{:S(2)}) collective-permute-start(bf16[4,3,128,128]{3,2,1,0:T(8,128)(2,1)} %bitcast.17), channel_id=1, source_target_pairs={{3,0},{0,1},{1,2},{2,3},{7,4},{4,5},{5,6},{6,7},{11,8},{8,9},{9,10... | collective-permute-start | bytes 1179656 | tf_op jit(solution)/shard_map/ppermute | solution.py:264
  41.3 43.0 %collective-permute-start.1 = (bf16[4,3,128,128]{3,2,1,0:T(8,128)(2,1)}, bf16[4,3,128,128]{3,2,1,0:T(8,128)(2,1)}, u32[]{:S(2)}, u32[]{:S(2)}) collective-permute-start(bf16[4,3,128,128]{3,2,1,0:T(8,128)(2,1)} %bitcast.18), channel_id=1, source_target_pairs={{2,0},{3,1},{0,2},{1,3},{6,4},{7,5},{4,6},{5,7},{10,8},{11,9},{8,1... | collective-permute-start | bytes 1179656 | tf_op jit(solution)/shard_map/ppermute | solution.py:264
  45.7 38.6 %collective-permute-start = (bf16[4,3,128,128]{3,2,1,0:T(8,128)(2,1)}, bf16[4,3,128,128]{3,2,1,0:T(8,128)(2,1)}, u32[]{:S(2)}, u32[]{:S(2)}) collective-permute-start(bf16[4,3,128,128]{3,2,1,0:T(8,128)(2,1)} %bitcast.19), channel_id=1, source_target_pairs={{1,0},{2,1},{3,2},{0,3},{5,4},{6,5},{7,6},{4,7},{9,8},{10,9},{11,1... | collective-permute-start | bytes 1179656 | tf_op jit(solution)/shard_map/ppermute | solution.py:264
  49.6 34.8 %collective-permute-start.7 = (bf16[4,3,128,128]{3,2,1,0:T(8,128)(2,1)}, bf16[4,3,128,128]{3,2,1,0:T(8,128)(2,1)}, u32[]{:S(2)}, u32[]{:S(2)}) collective-permute-start(bf16[4,3,128,128]{3,2,1,0:T(8,128)(2,1)} %slice_bitcast_fusion), channel_id=1, source_target_pairs={{0,4},{1,5},{2,6},{3,7},{8,12},{9,13},{10,14},{11,15},{16,20},{17,... | collective-permute-start | bytes 1179656 | tf_op jit(solution)/shard_map/ppermute | solution.py:289

commit v4 on v3

--- a/solution.py
+++ b/solution.py
@@ -17,7 +17,9 @@
 WIN = 2 * HP
 PER = PB * KG
 ROWS = ("rows_0", "rows_1", "rows_2")
-SLAB = ("rows_1", "rows_2", "cols")
+CHIP_LINE = ("rows_2", "cols")
+CHIPS = ("rows_0", "rows_1")
+HALF = 64
 
 
 def place():
@@ -25,22 +27,21 @@
 
 
 def spread_kernel(cols_ref, out_ref):
-    _, c = place()
+    p0, c = place()
     lane = lax.broadcasted_iota(jnp.int32, (1, BS), 1)
+    first = HALF * (p0 & 1) + PER * c
     row = jnp.zeros((1, BS), jnp.int32)
     for r in range(PB):
         for s in range(KG):
-            row = jnp.where(lane == PER * c + KG * r + s, cols_ref[r, s], row)
+            row = jnp.where(lane == first + KG * r + s, cols_ref[r, s] >> 2, row)
     out_ref[...] = jnp.broadcast_to(row[None], out_ref.shape)
 
 
-def slab_kernel(in_ref, out_ref):
-    rows = []
-    for n in range(8):
-        part = [in_ref[GROUPS * n + g] for g in range(GROUPS)]
-        rows.append((part[0] + part[1]) + (part[2] + part[3]))
-    tile = jnp.concatenate(rows, axis=0)
-    out_ref[...] = jnp.broadcast_to(tile[None], out_ref.shape)
+def chip_kernel(in_ref, out_ref):
+    part = [in_ref[n] for n in range(2 * GROUPS)]
+    while len(part) > 1:
+        part = [a + b for a, b in zip(part[::2], part[1::2])]
+    out_ref[...] = jnp.broadcast_to(part[0][None], out_ref.shape)
 
 
 def bits_set(x):
@@ -50,9 +51,23 @@
     return (x + (x >> 8)) & 0x1F
 
 
-def index_kernel(tab_ref, cols_ref, starts_ref, map_ref, turned_ref):
+def index_kernel(tab_ref, cols_ref, starts_ref, map_ref, table_ref, turned_ref):
     p0, c = place()
-    turned_ref[...] = jnp.transpose(tab_ref[...].reshape(NP, BS))
+    for n in range(HALF):
+        table_ref[n : n + 1, :] = tab_ref[n]
+    table = table_ref[...].astype(jnp.float32).astype(jnp.bfloat16)
+    chip = lax.broadcasted_iota(jnp.int32, (HALF, NP), 0)
+    spot = lax.broadcasted_iota(jnp.int32, (HALF, NP), 1)
+    turned = jnp.zeros((HALF, NP), jnp.float32)
+    for core in range(2):
+        pick = jnp.where(spot == 2 * chip + core, 1.0, 0.0).astype(jnp.bfloat16)
+        turned = turned + lax.dot_general(
+            table[:, HALF * core : HALF * (core + 1)],
+            pick,
+            (((0,), (0,)), ((), ())),
+            preferred_element_type=jnp.float32,
+        )
+    turned_ref[...] = (turned.astype(jnp.int32) - spot + HP) & (NP - 1)
     panel = lax.broadcasted_iota(jnp.int32, (1, NP), 1)
     wants = []
     owns = []
@@ -61,13 +76,11 @@
         for g in range(GROUPS):
             for s in range(KG):
                 at = PER * g + KG * r + s
-                local = (turned_ref[at : at + 1, :] - PB * (panel - HP)) & (PB * NP - 1)
-                want = want | jnp.left_shift(1, local)
+                want = want | jnp.left_shift(1, PB * turned_ref[at : at + 1, :] + g)
         wants.append(want)
         own = jnp.zeros((1, NP), jnp.int32)
         for s in range(KG):
-            col = turned_ref[pl.ds(PER * c + KG * r + s, 1), :]
-            own = own | jnp.left_shift(1, ((col >> 2) - panel + HP) & (NP - 1))
+            own = own | jnp.left_shift(1, turned_ref[pl.ds(PER * c + KG * r + s, 1), :])
         owns.append(own)
     pad = [jnp.zeros((PB, NP), jnp.int32)]
     want = jnp.concatenate(wants + pad, axis=0)
@@ -109,12 +122,18 @@
         cols_ref[r : r + 1, :] = cols[:, :WIDTH]
         starts_ref[:, r : r + 1] = jnp.broadcast_to(start, (1, 1))
         start = start + count[r : r + 1, :]
+    spread = lax.broadcasted_iota(jnp.int32, (1, BS), 1)
+    group = jnp.zeros((1, BS), jnp.int32)
+    for g in range(1, GROUPS):
+        group = group + jnp.where(spread >= PER * g, 1, 0)
     for w in range(WIN):
         at = (p0 - HP + w) & (NP - 1)
-        row = tab_ref[at >> 3, pl.ds(at & 7, 1), :]
-        map_ref[w : w + 1, :] = (((row >> 2) - at + HP) & (NP - 1)) + w
+        row = table_ref[pl.ds(at >> 1, 1), :]
+        row = jnp.where((at & 1) == 1, pltpu.roll(row, HALF, 1), row)
+        row = (row - at + HP) & (NP - 1)
+        map_ref[w : w + 1, :] = row + w
         if w == HP:
-            map_ref[WIN : WIN + 1, :] = (row - PB * (p0 - HP)) & (PB * NP - 1)
+            map_ref[WIN : WIN + 1, :] = PB * row + group
     map_ref[WIN + 1 : 16, :] = rank[: 16 - WIN - 1, :]
 
 
@@ -195,7 +214,7 @@
 def spread(cols):
     return pl.pallas_call(
         spread_kernel,
-        out_shape=jax.ShapeDtypeStruct((32, 1, BS), jnp.int32),
+        out_shape=jax.ShapeDtypeStruct((2 * GROUPS, 1, BS), jnp.int32),
         in_specs=[SMEM],
         out_specs=VMEM,
         compiler_params=pltpu.CompilerParams(vmem_limit_bytes=8 << 20),
@@ -203,14 +222,14 @@
     )(cols)
 
 
-def slab_table(parts):
+def chip_table(parts):
     return pl.pallas_call(
-        slab_kernel,
-        out_shape=jax.ShapeDtypeStruct((16, 8, BS), jnp.int32),
+        chip_kernel,
+        out_shape=jax.ShapeDtypeStruct((HALF, 1, BS), jnp.int32),
         in_specs=[VMEM],
         out_specs=VMEM,
         compiler_params=pltpu.CompilerParams(vmem_limit_bytes=8 << 20),
-        name="slab_table",
+        name="chip_table",
     )(parts)
 
 
@@ -224,7 +243,7 @@
         ),
         in_specs=[VMEM],
         out_specs=(VMEM, VMEM, VMEM),
-        scratch_shapes=[pltpu.VMEM((BS, NP), jnp.int32)],
+        scratch_shapes=[pltpu.VMEM((HALF, BS), jnp.int32), pltpu.VMEM((HALF, NP), jnp.int32)],
         compiler_params=pltpu.CompilerParams(vmem_limit_bytes=8 << 20),
         name="indices",
     )(table)
@@ -275,8 +294,8 @@
 
 def on_device(blocks, block_cols):
     own = blocks[:, 0]
-    parts = exchange(spread(block_cols[:, 0]), SLAB)
-    table = exchange(slab_table(parts), "rows_0")
+    parts = exchange(spread(block_cols[:, 0]), CHIP_LINE)
+    table = exchange(chip_table(parts), CHIPS)
     columns, starts, where = indices(table)
     partner = swapped(own)
     pair = jnp.stack([own, partner])

time: 91.9 us -> 94.9 us (1.033)
  blocking collectives: 30.9 us -> 33.2 us
    all_to_all x2, blocking collectives: 30.9 us -> 33.2 us  [exchange(): return lax.all_to_all(array, axes, 0, 0, tiled=True)]
where the time goes in v4:
time: 94.9 us; the launch traced here: 93.2 us
  starting transfers between devices  37.8 us (40%)
  blocking collectives  33.2 us (35%)
  waiting for transfers between devices  10.5 us (11%)
  Pallas kernels  8.39 us (9%)
  local copies, waits for them, and re-layouts  1.54 us (2%)
  other arithmetic  1.07 us (1%)
    all_to_all x2, blocking collectives, exchange(): return lax.all_to_all(array, axes, 0, 0, tiled=True)  33.2 us
    ppermute x2, starting transfers between devices, outward(): return lax.ppermute(pair, ROWS, route)  15.4 us
    ppermute x2, starting transfers between devices, swapped(): return lax.ppermute(block, 'rows_2', [(0, 1), (1, 0)])  10.7 us
    ppermute x3, starting transfers between devices, turned(): lax.ppermute(block, 'cols', [((c + distance) % GROUPS, c) for c in range(...  10.5 us
    ppermute x2, waiting for transfers between devices, outward(): return lax.ppermute(pair, ROWS, route)  8.92 us
    pallas_call x1, Pallas kernels, square(): pl.pallas_call(square_kernel, out_shape=jax.ShapeDtypeStruct((PB, WIDTH,...  6.45 us
  transfers between devices with their start and end apart: 8, of which 2 were waited for; matrix products, arithmetic and copies ran while one was open for 2% of the time, Pallas kernels for 2%

profile of v4, /device:TPU:1, one launch (start us, length us, event | category | flops | bytes accessed | tf_op | source)
XLA Modules:
  0.0 93.2 jit_solution(13368610663907319905)
XLA Ops:
  0.6 8.7 %collective-permute-start.3 = (bf16[4,3,128,128]{3,2,1,0:T(8,128)(2,1)}, bf16[4,3,128,128]{3,2,1,0:T(8,128)(2,1)S(1)}, u32[]{:S(2)}, u32[]{:S(2)}) collective-permute-start(bf16[4,3,128,128]{3,2,1,0:T(8,128)(2,1)} %bitcast.15), channel_id=1, source_target_pairs={{0,4},{4,0},{1,5},{5,1},{2,6},{6,2},{3,7},{7,3},{8,12},{12,8},{9,1... | collective-permute-start | bytes 1179656 | tf_op jit(solution)/shard_map/ppermute | solution.py:279
  9.4 1.5 %collective-permute-done.3 = bf16[4,3,128,128]{3,2,1,0:T(8,128)(2,1)S(1)} collective-permute-done((bf16[4,3,128,128]{3,2,1,0:T(8,128)(2,1)}, bf16[4,3,128,128]{3,2,1,0:T(8,128)(2,1)S(1)}, u32[]{:S(2)}, u32[]{:S(2)}) %collective-permute-start.3) | collective-permute-done | bytes 393248 | tf_op jit(solution)/shard_map/ppermute | solution.py:279
  10.9 1.1 %pad_maximum_fusion.pair_ref = bf16[2,4,3,128,128]{4,3,2,1,0:T(8,128)(2,1)S(1)} fusion(bf16[1,4,3,128,128]{4,3,2,1,0:T(8,128)(2,1)S(1)} %bitcast.20, bf16[1,4,3,128,128]{4,3,2,1,0:T(8,128)(2,1)} %bitcast.16), kind=kLoop, calls=%fused_computation | loop fusion | flops 393216 | bytes 1572864 | tf_op jit(solution)/shard_map/stack | solution.py:301
  12.0 8.2 %collective-permute-start.4 = (bf16[2,4,3,128,128]{4,3,2,1,0:T(8,128)(2,1)S(1)}, bf16[2,4,3,128,128]{4,3,2,1,0:T(8,128)(2,1)S(1)}, u32[]{:S(2)}, u32[]{:S(2)}) collective-permute-start(bf16[2,4,3,128,128]{4,3,2,1,0:T(8,128)(2,1)S(1)} %pad_maximum_fusion.pair_ref), channel_id=1, source_target_pairs={{0,8},{4,508},{8,16},{12,4},{16,24},{20,12},{24,32},{28,20},{32,40... | collective-permute-start | bytes 2359304 | tf_op jit(solution)/shard_map/ppermute | solution.py:292
  20.2 8.9 %collective-permute-done.4.next_ref = bf16[2,4,3,128,128]{4,3,2,1,0:T(8,128)(2,1)S(1)} collective-permute-done((bf16[2,4,3,128,128]{4,3,2,1,0:T(8,128)(2,1)S(1)}, bf16[2,4,3,128,128]{4,3,2,1,0:T(8,128)(2,1)S(1)}, u32[]{:S(2)}, u32[]{:S(2)}) %collective-permute-start.4) | collective-permute-done | bytes 786464 | tf_op jit(solution)/shard_map/ppermute | solution.py:292
  29.1 7.1 %collective-permute-start.6 = (bf16[2,4,3,128,128]{4,3,2,1,0:T(8,128)(2,1)S(1)}, bf16[2,4,3,128,128]{4,3,2,1,0:T(8,128)(2,1)S(1)}, u32[]{:S(2)}, u32[]{:S(2)}) collective-permute-start(bf16[2,4,3,128,128]{4,3,2,1,0:T(8,128)(2,1)S(1)} %collective-permute-done.4.next_ref), channel_id=1, source_target_pairs={{0,8},{4,508},{8,16},{12,4},{16,24},{20,12},{24,32},{28,20},{32,40... | collective-permute-start | bytes 2359304 | tf_op jit(solution)/shard_map/ppermute | solution.py:292
  36.3 1.9 %collective-permute-start.5 = (bf16[2,4,3,128,128]{4,3,2,1,0:T(8,128)(2,1)S(1)}, bf16[2,4,3,128,128]{4,3,2,1,0:T(8,128)(2,1)S(1)}, u32[]{:S(2)}, u32[]{:S(2)}) collective-permute-start(bf16[2,4,3,128,128]{4,3,2,1,0:T(8,128)(2,1)S(1)} %collective-permute-done.4.next_ref), channel_id=1, source_target_pairs={{0,4},{4,0},{1,5},{5,1},{2,6},{6,2},{3,7},{7,3},{8,12},{12,8},{9,1... | collective-permute-start | bytes 2359304 | tf_op jit(solution)/shard_map/ppermute | solution.py:279
  38.2 3.1 %collective-permute-start.2 = (bf16[4,3,128,128]{3,2,1,0:T(8,128)(2,1)}, bf16[4,3,128,128]{3,2,1,0:T(8,128)(2,1)S(1)}, u32[]{:S(2)}, u32[]{:S(2)}) collective-permute-start(bf16[4,3,128,128]{3,2,1,0:T(8,128)(2,1)} %bitcast.17), channel_id=1, source_target_pairs={{3,0},{0,1},{1,2},{2,3},{7,4},{4,5},{5,6},{6,7},{11,8},{8,9},{9,10... | collective-permute-start | bytes 1179656 | tf_op jit(solution)/shard_map/ppermute | solution.py:283
  41.3 4.4 %collective-permute-start.1 = (bf16[4,3,128,128]{3,2,1,0:T(8,128)(2,1)}, bf16[4,3,128,128]{3,2,1,0:T(8,128)(2,1)}, u32[]{:S(2)}, u32[]{:S(2)}) collective-permute-start(bf16[4,3,128,128]{3,2,1,0:T(8,128)(2,1)} %bitcast.18), channel_id=1, source_target_pairs={{2,0},{3,1},{0,2},{1,3},{6,4},{7,5},{4,6},{5,7},{10,8},{11,9},{8,1... | collective-permute-start | bytes 1179656 | tf_op jit(solution)/shard_map/ppermute | solution.py:283
  45.7 3.1 %collective-permute-start = (bf16[4,3,128,128]{3,2,1,0:T(8,128)(2,1)}, bf16[4,3,128,128]{3,2,1,0:T(8,128)(2,1)}, u32[]{:S(2)}, u32[]{:S(2)}) collective-permute-start(bf16[4,3,128,128]{3,2,1,0:T(8,128)(2,1)} %bitcast.19), channel_id=1, source_target_pairs={{1,0},{2,1},{3,2},{0,3},{5,4},{6,5},{7,6},{4,7},{9,8},{10,9},{11,1... | collective-permute-start | bytes 1179656 | tf_op jit(solution)/shard_map/ppermute | solution.py:283
  48.8 0.0 collective-permute-done.6.far_ref
  48.8 0.8 slice_bitcast_fusion
  49.6 1.3 %collective-permute-start.7 = (bf16[4,3,128,128]{3,2,1,0:T(8,128)(2,1)}, bf16[4,3,128,128]{3,2,1,0:T(8,128)(2,1)}, u32[]{:S(2)}, u32[]{:S(2)}) collective-permute-start(bf16[4,3,128,128]{3,2,1,0:T(8,128)(2,1)} %slice_bitcast_fusion), channel_id=1, source_target_pairs={{0,4},{1,5},{2,6},{3,7},{8,12},{9,13},{10,14},{11,15},{16,20},{17,... | collective-permute-start | bytes 1179656 | tf_op jit(solution)/shard_map/ppermute | solution.py:308
  50.8 0.8 copy.5
  51.6 0.6 spread.1
  52.2 11.5 %all_to_all.10.in_ref = s32[8,1,128]{2,1,0:T(1,128)S(1)} all-to-all(s32[8,1,128]{2,1,0:T(1,128)S(1)} %spread.1), channel_id=1, replica_groups=mesh['rows_0'=16,'rows_1'=4,'rows_2'=2,'cols'=4] {'rows_2','cols'}, dimensions={0} | all-to-all | bytes 8192 | tf_op jit(solution)/shard_map/all_to_all | solution.py:275
  63.8 21.6 %all_to_all.11.tab_ref = s32[64,1,128]{2,1,0:T(1,128)S(1)} all-to-all(s32[64,1,128]{2,1,0:T(1,128)S(1)} %chip_table.1), channel_id=1, replica_groups=mesh['rows_0'=16,'rows_1'=4,'rows_2'=2,'cols'=4] {'rows_0','rows_1'}, dimensions={0} | all-to-all | bytes 65536 | tf_op jit(solution)/shard_map/all_to_all | solution.py:275
  85.4 1.3 %indices.1 = (s32[4,36]{1,0:T(4,128)}, s32[1,4]{1,0:T(1,128)}, s32[16,128]{1,0:T(8,128)S(1)}) custom-call(s32[64,1,128]{2,1,0:T(1,128)S(1)} %all_to_all.11.tab_ref), custom_call_target="tpu_custom_call" | custom-call | tf_op jit(solution)/shard_map/indices/pallas_call | solution.py:237
  86.7 0.0 collective-permute-done.2.down_ref
  86.7 0.0 collective-permute-done.1.over_ref
  86.7 0.0 collective-permute-done.up_ref
  86.8 0.0 collective-permute-done.5.swap_ref
  86.8 0.0 collective-permute-done.7.last_ref
  86.8 6.4 %square.1 = bf16[4,36,128,128]{3,2,1,0:T(8,128)(2,1)} custom-call(s32[16,128]{1,0:T(8,128)S(1)} %get-tuple-element.6.map_ref, bf16[4,3,128,128]{3,2,1,0:T(8,128)(2,1)} %collective-permute-done.up_ref, bf16[4,3,128,128]{3,2,1,0:T(8,128)(2,1)} %collective-permute-done.1.over_ref, bf16[4,3,128,128]{3,2,1,0:T(8,128)(2,1)S(1)} %collective-permute-done.2.down_ref, ...), custom_call_target="tpu_custom_call" | custom-call | tf_op jit(solution)/shard_map/square/pallas_call | solution.py:253
  (1 shorter events, 0.0 us)
Async XLA Ops:
  0.6 10.3 %collective-permute-start.3 = (bf16[4,3,128,128]{3,2,1,0:T(8,128)(2,1)}, bf16[4,3,128,128]{3,2,1,0:T(8,128)(2,1)S(1)}, u32[]{:S(2)}, u32[]{:S(2)}) collective-permute-start(bf16[4,3,128,128]{3,2,1,0:T(8,128)(2,1)} %bitcast.15), channel_id=1, source_target_pairs={{0,4},{4,0},{1,5},{5,1},{2,6},{6,2},{3,7},{7,3},{8,12},{12,8},{9,1... | collective-permute-start | bytes 1179656 | tf_op jit(solution)/shard_map/ppermute | solution.py:279
  12.0 17.1 %collective-permute-start.4 = (bf16[2,4,3,128,128]{4,3,2,1,0:T(8,128)(2,1)S(1)}, bf16[2,4,3,128,128]{4,3,2,1,0:T(8,128)(2,1)S(1)}, u32[]{:S(2)}, u32[]{:S(2)}) collective-permute-start(bf16[2,4,3,128,128]{4,3,2,1,0:T(8,128)(2,1)S(1)} %pad_maximum_fusion.pair_ref), channel_id=1, source_target_pairs={{0,8},{4,508},{8,16},{12,4},{16,24},{20,12},{24,32},{28,20},{32,40... | collective-permute-start | bytes 2359304 | tf_op jit(solution)/shard_map/ppermute | solution.py:292
  29.1 19.6 %collective-permute-start.6 = (bf16[2,4,3,128,128]{4,3,2,1,0:T(8,128)(2,1)S(1)}, bf16[2,4,3,128,128]{4,3,2,1,0:T(8,128)(2,1)S(1)}, u32[]{:S(2)}, u32[]{:S(2)}) collective-permute-start(bf16[2,4,3,128,128]{4,3,2,1,0:T(8,128)(2,1)S(1)} %collective-permute-done.4.next_ref), channel_id=1, source_target_pairs={{0,8},{4,508},{8,16},{12,4},{16,24},{20,12},{24,32},{28,20},{32,40... | collective-permute-start | bytes 2359304 | tf_op jit(solution)/shard_map/ppermute | solution.py:292
  36.3 50.5 %collective-permute-start.5 = (bf16[2,4,3,128,128]{4,3,2,1,0:T(8,128)(2,1)S(1)}, bf16[2,4,3,128,128]{4,3,2,1,0:T(8,128)(2,1)S(1)}, u32[]{:S(2)}, u32[]{:S(2)}) collective-permute-start(bf16[2,4,3,128,128]{4,3,2,1,0:T(8,128)(2,1)S(1)} %collective-permute-done.4.next_ref), channel_id=1, source_target_pairs={{0,4},{4,0},{1,5},{5,1},{2,6},{6,2},{3,7},{7,3},{8,12},{12,8},{9,1... | collective-permute-start | bytes 2359304 | tf_op jit(solution)/shard_map/ppermute | solution.py:279
  38.2 48.5 %collective-permute-start.2 = (bf16[4,3,128,128]{3,2,1,0:T(8,128)(2,1)}, bf16[4,3,128,128]{3,2,1,0:T(8,128)(2,1)S(1)}, u32[]{:S(2)}, u32[]{:S(2)}) collective-permute-start(bf16[4,3,128,128]{3,2,1,0:T(8,128)(2,1)} %bitcast.17), channel_id=1, source_target_pairs={{3,0},{0,1},{1,2},{2,3},{7,4},{4,5},{5,6},{6,7},{11,8},{8,9},{9,10... | collective-permute-start | bytes 1179656 | tf_op jit(solution)/shard_map/ppermute | solution.py:283
  41.3 45.4 %collective-permute-start.1 = (bf16[4,3,128,128]{3,2,1,0:T(8,128)(2,1)}, bf16[4,3,128,128]{3,2,1,0:T(8,128)(2,1)}, u32[]{:S(2)}, u32[]{:S(2)}) collective-permute-start(bf16[4,3,128,128]{3,2,1,0:T(8,128)(2,1)} %bitcast.18), channel_id=1, source_target_pairs={{2,0},{3,1},{0,2},{1,3},{6,4},{7,5},{4,6},{5,7},{10,8},{11,9},{8,1... | collective-permute-start | bytes 1179656 | tf_op jit(solution)/shard_map/ppermute | solution.py:283
  45.7 41.0 %collective-permute-start = (bf16[4,3,128,128]{3,2,1,0:T(8,128)(2,1)}, bf16[4,3,128,128]{3,2,1,0:T(8,128)(2,1)}, u32[]{:S(2)}, u32[]{:S(2)}) collective-permute-start(bf16[4,3,128,128]{3,2,1,0:T(8,128)(2,1)} %bitcast.19), channel_id=1, source_target_pairs={{1,0},{2,1},{3,2},{0,3},{5,4},{6,5},{7,6},{4,7},{9,8},{10,9},{11,1... | collective-permute-start | bytes 1179656 | tf_op jit(solution)/shard_map/ppermute | solution.py:283
  49.6 37.2 %collective-permute-start.7 = (bf16[4,3,128,128]{3,2,1,0:T(8,128)(2,1)}, bf16[4,3,128,128]{3,2,1,0:T(8,128)(2,1)}, u32[]{:S(2)}, u32[]{:S(2)}) collective-permute-start(bf16[4,3,128,128]{3,2,1,0:T(8,128)(2,1)} %slice_bitcast_fusion), channel_id=1, source_target_pairs={{0,4},{1,5},{2,6},{3,7},{8,12},{9,13},{10,14},{11,15},{16,20},{17,... | collective-permute-start | bytes 1179656 | tf_op jit(solution)/shard_map/ppermute | solution.py:308

commit v5 on v3

--- a/solution.py
+++ b/solution.py
@@ -15,9 +15,8 @@
 WIDTH = 36
 USED = 15
 WIN = 2 * HP
-PER = PB * KG
 ROWS = ("rows_0", "rows_1", "rows_2")
-SLAB = ("rows_1", "rows_2", "cols")
+ROOM = 16
 
 
 def place():
@@ -25,22 +24,19 @@
 
 
 def spread_kernel(cols_ref, out_ref):
-    _, c = place()
     lane = lax.broadcasted_iota(jnp.int32, (1, BS), 1)
     row = jnp.zeros((1, BS), jnp.int32)
     for r in range(PB):
         for s in range(KG):
-            row = jnp.where(lane == PER * c + KG * r + s, cols_ref[r, s], row)
+            row = jnp.where(lane == KG * r + s, cols_ref[r, s] >> 2, row)
     out_ref[...] = jnp.broadcast_to(row[None], out_ref.shape)
 
 
-def slab_kernel(in_ref, out_ref):
-    rows = []
-    for n in range(8):
-        part = [in_ref[GROUPS * n + g] for g in range(GROUPS)]
-        rows.append((part[0] + part[1]) + (part[2] + part[3]))
-    tile = jnp.concatenate(rows, axis=0)
-    out_ref[...] = jnp.broadcast_to(tile[None], out_ref.shape)
+def turn_kernel(in_ref, out_ref, table_ref):
+    for n in range(NP):
+        table_ref[n : n + 1, :] = in_ref[n]
+    turned = jnp.transpose(table_ref[...])
+    out_ref[...] = jnp.broadcast_to(turned[None, :ROOM], out_ref.shape)
 
 
 def bits_set(x):
@@ -52,7 +48,9 @@
 
 def index_kernel(tab_ref, cols_ref, starts_ref, map_ref, turned_ref):
     p0, c = place()
-    turned_ref[...] = jnp.transpose(tab_ref[...].reshape(NP, BS))
+    spot = lax.broadcasted_iota(jnp.int32, (GROUPS * ROOM, NP), 1)
+    turned = (tab_ref[...].reshape(GROUPS * ROOM, NP) - spot + HP) & (NP - 1)
+    turned_ref[...] = turned
     panel = lax.broadcasted_iota(jnp.int32, (1, NP), 1)
     wants = []
     owns = []
@@ -60,14 +58,12 @@
         want = jnp.zeros((1, NP), jnp.int32)
         for g in range(GROUPS):
             for s in range(KG):
-                at = PER * g + KG * r + s
-                local = (turned_ref[at : at + 1, :] - PB * (panel - HP)) & (PB * NP - 1)
-                want = want | jnp.left_shift(1, local)
+                at = ROOM * g + KG * r + s
+                want = want | jnp.left_shift(1, PB * turned_ref[at : at + 1, :] + g)
         wants.append(want)
         own = jnp.zeros((1, NP), jnp.int32)
         for s in range(KG):
-            col = turned_ref[pl.ds(PER * c + KG * r + s, 1), :]
-            own = own | jnp.left_shift(1, ((col >> 2) - panel + HP) & (NP - 1))
+            own = own | jnp.left_shift(1, turned_ref[pl.ds(ROOM * c + KG * r + s, 1), :])
         owns.append(own)
     pad = [jnp.zeros((PB, NP), jnp.int32)]
     want = jnp.concatenate(wants + pad, axis=0)
@@ -109,13 +105,17 @@
         cols_ref[r : r + 1, :] = cols[:, :WIDTH]
         starts_ref[:, r : r + 1] = jnp.broadcast_to(start, (1, 1))
         start = start + count[r : r + 1, :]
-    for w in range(WIN):
-        at = (p0 - HP + w) & (NP - 1)
-        row = tab_ref[at >> 3, pl.ds(at & 7, 1), :]
-        map_ref[w : w + 1, :] = (((row >> 2) - at + HP) & (NP - 1)) + w
-        if w == HP:
-            map_ref[WIN : WIN + 1, :] = (row - PB * (p0 - HP)) & (PB * NP - 1)
-    map_ref[WIN + 1 : 16, :] = rank[: 16 - WIN - 1, :]
+    window = lax.broadcasted_iota(jnp.int32, (2 * WIN, NP), 0)
+    panels = lax.broadcasted_iota(jnp.int32, (2 * WIN, NP), 1)
+    pick = jnp.where(panels == ((p0 - HP + window) & (NP - 1)), 1.0, 0.0).astype(jnp.bfloat16)
+    near = lax.dot_general(
+        pick,
+        turned.astype(jnp.float32).astype(jnp.bfloat16),
+        (((1,), (1,)), ((), ())),
+        preferred_element_type=jnp.float32,
+    )
+    map_ref[:WIN, : GROUPS * ROOM] = near[:WIN].astype(jnp.int32)
+    map_ref[WIN:, :] = rank
 
 
 def square_kernel(map_ref, up_ref, over_ref, down_ref, pair_ref, next_ref, swap_ref, far_ref, last_ref, *refs):
@@ -158,13 +158,11 @@
             g = (c + d) & (GROUPS - 1)
             left_ref = (None, up_ref, over_ref, down_ref)[d]
             for r in range(PB):
-                local = map_ref[WIN, PER * g + KG * r + s0]
-                w = local >> 2
-                kr = local & (PB - 1)
+                w = map_ref[HP, ROOM * g + KG * r + s0]
                 slots = []
                 for s in range(KG):
-                    slots.append(map_ref[WIN + 1 + r, map_ref[w, PER * c + KG * kr + s]])
-                right = jnp.concatenate([rights[w, kr, s] for s in range(KG)], axis=1)
+                    slots.append(map_ref[WIN + r, map_ref[w, ROOM * c + KG * g + s] + w])
+                right = jnp.concatenate([rights[w, g, s] for s in range(KG)], axis=1)
                 left = left_ref[r, s0] if d else pair_ref[0, r, s0]
                 product = jnp.dot(left, right, preferred_element_type=jnp.float32)
                 new = [
@@ -195,7 +193,7 @@
 def spread(cols):
     return pl.pallas_call(
         spread_kernel,
-        out_shape=jax.ShapeDtypeStruct((32, 1, BS), jnp.int32),
+        out_shape=jax.ShapeDtypeStruct((NP, 1, BS), jnp.int32),
         in_specs=[SMEM],
         out_specs=VMEM,
         compiler_params=pltpu.CompilerParams(vmem_limit_bytes=8 << 20),
@@ -203,14 +201,15 @@
     )(cols)
 
 
-def slab_table(parts):
+def turned_table(parts):
     return pl.pallas_call(
-        slab_kernel,
-        out_shape=jax.ShapeDtypeStruct((16, 8, BS), jnp.int32),
+        turn_kernel,
+        out_shape=jax.ShapeDtypeStruct((GROUPS, ROOM, BS), jnp.int32),
         in_specs=[VMEM],
         out_specs=VMEM,
+        scratch_shapes=[pltpu.VMEM((NP, BS), jnp.int32)],
         compiler_params=pltpu.CompilerParams(vmem_limit_bytes=8 << 20),
-        name="slab_table",
+        name="turned_table",
     )(parts)
 
 
@@ -224,7 +223,7 @@
         ),
         in_specs=[VMEM],
         out_specs=(VMEM, VMEM, VMEM),
-        scratch_shapes=[pltpu.VMEM((BS, NP), jnp.int32)],
+        scratch_shapes=[pltpu.VMEM((GROUPS * ROOM, NP), jnp.int32)],
         compiler_params=pltpu.CompilerParams(vmem_limit_bytes=8 << 20),
         name="indices",
     )(table)
@@ -275,8 +274,8 @@
 
 def on_device(blocks, block_cols):
     own = blocks[:, 0]
-    parts = exchange(spread(block_cols[:, 0]), SLAB)
-    table = exchange(slab_table(parts), "rows_0")
+    parts = exchange(spread(block_cols[:, 0]), ROWS)
+    table = exchange(turned_table(parts), "cols")
     columns, starts, where = indices(table)
     partner = swapped(own)
     pair = jnp.stack([own, partner])

time: 91.9 us -> 93.2 us (1.014)
  blocking collectives: 30.9 us -> 32.6 us
    all_to_all x2, blocking collectives: 30.9 us -> 32.6 us  [exchange(): return lax.all_to_all(array, axes, 0, 0, tiled=True)]
where the time goes in v5:
time: 93.2 us; the launch traced here: 92.7 us
  starting transfers between devices  37.8 us (41%)
  blocking collectives  32.6 us (35%)
  waiting for transfers between devices  10.5 us (11%)
  Pallas kernels  8.4 us (9%)
  local copies, waits for them, and re-layouts  1.54 us (2%)
  other arithmetic  1.07 us (1%)
    all_to_all x2, blocking collectives, exchange(): return lax.all_to_all(array, axes, 0, 0, tiled=True)  32.6 us
    ppermute x2, starting transfers between devices, outward(): return lax.ppermute(pair, ROWS, route)  15.4 us
    ppermute x2, starting transfers between devices, swapped(): return lax.ppermute(block, 'rows_2', [(0, 1), (1, 0)])  10.7 us
    ppermute x3, starting transfers between devices, turned(): lax.ppermute(block, 'cols', [((c + distance) % GROUPS, c) for c in range(...  10.5 us
    ppermute x2, waiting for transfers between devices, outward(): return lax.ppermute(pair, ROWS, route)  8.92 us
    pallas_call x1, Pallas kernels, square(): pl.pallas_call(square_kernel, out_shape=jax.ShapeDtypeStruct((PB, WIDTH,...  6.65 us
  transfers between devices with their start and end apart: 8, of which 2 were waited for; matrix products, arithmetic and copies ran while one was open for 2% of the time, Pallas kernels for 2%

profile of v5, /device:TPU:1, one launch (start us, length us, event | category | flops | bytes accessed | tf_op | source)
XLA Modules:
  0.0 92.7 jit_solution(14368809661733114707)
XLA Ops:
  0.6 8.7 %collective-permute-start.3 = (bf16[4,3,128,128]{3,2,1,0:T(8,128)(2,1)}, bf16[4,3,128,128]{3,2,1,0:T(8,128)(2,1)S(1)}, u32[]{:S(2)}, u32[]{:S(2)}) collective-permute-start(bf16[4,3,128,128]{3,2,1,0:T(8,128)(2,1)} %bitcast.15), channel_id=1, source_target_pairs={{0,4},{4,0},{1,5},{5,1},{2,6},{6,2},{3,7},{7,3},{8,12},{12,8},{9,1... | collective-permute-start | bytes 1179656 | tf_op jit(solution)/shard_map/ppermute | solution.py:259
  9.4 1.5 %collective-permute-done.3 = bf16[4,3,128,128]{3,2,1,0:T(8,128)(2,1)S(1)} collective-permute-done((bf16[4,3,128,128]{3,2,1,0:T(8,128)(2,1)}, bf16[4,3,128,128]{3,2,1,0:T(8,128)(2,1)S(1)}, u32[]{:S(2)}, u32[]{:S(2)}) %collective-permute-start.3) | collective-permute-done | bytes 393248 | tf_op jit(solution)/shard_map/ppermute | solution.py:259
  10.9 1.1 %pad_maximum_fusion.pair_ref = bf16[2,4,3,128,128]{4,3,2,1,0:T(8,128)(2,1)S(1)} fusion(bf16[1,4,3,128,128]{4,3,2,1,0:T(8,128)(2,1)S(1)} %bitcast.20, bf16[1,4,3,128,128]{4,3,2,1,0:T(8,128)(2,1)} %bitcast.16), kind=kLoop, calls=%fused_computation | loop fusion | flops 393216 | bytes 1572864 | tf_op jit(solution)/shard_map/stack | solution.py:281
  12.0 8.2 %collective-permute-start.4 = (bf16[2,4,3,128,128]{4,3,2,1,0:T(8,128)(2,1)S(1)}, bf16[2,4,3,128,128]{4,3,2,1,0:T(8,128)(2,1)S(1)}, u32[]{:S(2)}, u32[]{:S(2)}) collective-permute-start(bf16[2,4,3,128,128]{4,3,2,1,0:T(8,128)(2,1)S(1)} %pad_maximum_fusion.pair_ref), channel_id=1, source_target_pairs={{0,8},{4,508},{8,16},{12,4},{16,24},{20,12},{24,32},{28,20},{32,40... | collective-permute-start | bytes 2359304 | tf_op jit(solution)/shard_map/ppermute | solution.py:272
  20.2 8.9 %collective-permute-done.4.next_ref = bf16[2,4,3,128,128]{4,3,2,1,0:T(8,128)(2,1)S(1)} collective-permute-done((bf16[2,4,3,128,128]{4,3,2,1,0:T(8,128)(2,1)S(1)}, bf16[2,4,3,128,128]{4,3,2,1,0:T(8,128)(2,1)S(1)}, u32[]{:S(2)}, u32[]{:S(2)}) %collective-permute-start.4) | collective-permute-done | bytes 786464 | tf_op jit(solution)/shard_map/ppermute | solution.py:272
  29.1 7.1 %collective-permute-start.6 = (bf16[2,4,3,128,128]{4,3,2,1,0:T(8,128)(2,1)S(1)}, bf16[2,4,3,128,128]{4,3,2,1,0:T(8,128)(2,1)S(1)}, u32[]{:S(2)}, u32[]{:S(2)}) collective-permute-start(bf16[2,4,3,128,128]{4,3,2,1,0:T(8,128)(2,1)S(1)} %collective-permute-done.4.next_ref), channel_id=1, source_target_pairs={{0,8},{4,508},{8,16},{12,4},{16,24},{20,12},{24,32},{28,20},{32,40... | collective-permute-start | bytes 2359304 | tf_op jit(solution)/shard_map/ppermute | solution.py:272
  36.3 1.9 %collective-permute-start.5 = (bf16[2,4,3,128,128]{4,3,2,1,0:T(8,128)(2,1)S(1)}, bf16[2,4,3,128,128]{4,3,2,1,0:T(8,128)(2,1)S(1)}, u32[]{:S(2)}, u32[]{:S(2)}) collective-permute-start(bf16[2,4,3,128,128]{4,3,2,1,0:T(8,128)(2,1)S(1)} %collective-permute-done.4.next_ref), channel_id=1, source_target_pairs={{0,4},{4,0},{1,5},{5,1},{2,6},{6,2},{3,7},{7,3},{8,12},{12,8},{9,1... | collective-permute-start | bytes 2359304 | tf_op jit(solution)/shard_map/ppermute | solution.py:259
  38.2 3.1 %collective-permute-start.2 = (bf16[4,3,128,128]{3,2,1,0:T(8,128)(2,1)}, bf16[4,3,128,128]{3,2,1,0:T(8,128)(2,1)S(1)}, u32[]{:S(2)}, u32[]{:S(2)}) collective-permute-start(bf16[4,3,128,128]{3,2,1,0:T(8,128)(2,1)} %bitcast.17), channel_id=1, source_target_pairs={{3,0},{0,1},{1,2},{2,3},{7,4},{4,5},{5,6},{6,7},{11,8},{8,9},{9,10... | collective-permute-start | bytes 1179656 | tf_op jit(solution)/shard_map/ppermute | solution.py:263
  41.3 4.4 %collective-permute-start.1 = (bf16[4,3,128,128]{3,2,1,0:T(8,128)(2,1)}, bf16[4,3,128,128]{3,2,1,0:T(8,128)(2,1)}, u32[]{:S(2)}, u32[]{:S(2)}) collective-permute-start(bf16[4,3,128,128]{3,2,1,0:T(8,128)(2,1)} %bitcast.18), channel_id=1, source_target_pairs={{2,0},{3,1},{0,2},{1,3},{6,4},{7,5},{4,6},{5,7},{10,8},{11,9},{8,1... | collective-permute-start | bytes 1179656 | tf_op jit(solution)/shard_map/ppermute | solution.py:263
  45.7 3.1 %collective-permute-start = (bf16[4,3,128,128]{3,2,1,0:T(8,128)(2,1)}, bf16[4,3,128,128]{3,2,1,0:T(8,128)(2,1)}, u32[]{:S(2)}, u32[]{:S(2)}) collective-permute-start(bf16[4,3,128,128]{3,2,1,0:T(8,128)(2,1)} %bitcast.19), channel_id=1, source_target_pairs={{1,0},{2,1},{3,2},{0,3},{5,4},{6,5},{7,6},{4,7},{9,8},{10,9},{11,1... | collective-permute-start | bytes 1179656 | tf_op jit(solution)/shard_map/ppermute | solution.py:263
  48.8 0.0 collective-permute-done.6.far_ref
  48.8 0.8 slice_bitcast_fusion
  49.6 1.3 %collective-permute-start.7 = (bf16[4,3,128,128]{3,2,1,0:T(8,128)(2,1)}, bf16[4,3,128,128]{3,2,1,0:T(8,128)(2,1)}, u32[]{:S(2)}, u32[]{:S(2)}) collective-permute-start(bf16[4,3,128,128]{3,2,1,0:T(8,128)(2,1)} %slice_bitcast_fusion), channel_id=1, source_target_pairs={{0,4},{1,5},{2,6},{3,7},{8,12},{9,13},{10,14},{11,15},{16,20},{17,... | collective-permute-start | bytes 1179656 | tf_op jit(solution)/shard_map/ppermute | solution.py:288
  50.8 0.8 copy.5
  51.6 0.6 spread.1
  52.2 25.5 %all_to_all.10.in_ref = s32[128,1,128]{2,1,0:T(1,128)S(1)} all-to-all(s32[128,1,128]{2,1,0:T(1,128)S(1)} %spread.1), channel_id=1, replica_groups=mesh['rows_0'=16,'rows_1'=4,'rows_2'=2,'cols'=4] {'rows_0','rows_1','row..., dimensions={0} | all-to-all | bytes 131072 | tf_op jit(solution)/shard_map/all_to_all | solution.py:255
  77.8 0.1 turned_table.1
  77.8 7.1 %all_to_all.11.tab_ref = s32[4,16,128]{2,1,0:T(8,128)S(1)} all-to-all(s32[4,16,128]{2,1,0:T(8,128)S(1)} %turned_table.1), channel_id=1, replica_groups=mesh['rows_0'=16,'rows_1'=4,'rows_2'=2,'cols'=4] {'cols'}, dimensions={0} | all-to-all | bytes 65536 | tf_op jit(solution)/shard_map/all_to_all | solution.py:255
  84.9 1.1 %indices.1 = (s32[4,36]{1,0:T(4,128)}, s32[1,4]{1,0:T(1,128)}, s32[16,128]{1,0:T(8,128)S(1)}) custom-call(s32[4,16,128]{2,1,0:T(8,128)S(1)} %all_to_all.11.tab_ref), custom_call_target="tpu_custom_call" | custom-call | tf_op jit(solution)/shard_map/indices/pallas_call | solution.py:217
  86.0 0.0 collective-permute-done.2.down_ref
  86.0 0.0 collective-permute-done.1.over_ref
  86.0 0.0 collective-permute-done.up_ref
  86.0 0.0 collective-permute-done.5.swap_ref
  86.0 0.0 collective-permute-done.7.last_ref
  86.1 6.6 %square.1 = bf16[4,36,128,128]{3,2,1,0:T(8,128)(2,1)} custom-call(s32[16,128]{1,0:T(8,128)S(1)} %get-tuple-element.6.map_ref, bf16[4,3,128,128]{3,2,1,0:T(8,128)(2,1)} %collective-permute-done.up_ref, bf16[4,3,128,128]{3,2,1,0:T(8,128)(2,1)} %collective-permute-done.1.over_ref, bf16[4,3,128,128]{3,2,1,0:T(8,128)(2,1)S(1)} %collective-permute-done.2.down_ref, ...), custom_call_target="tpu_custom_call" | custom-call | tf_op jit(solution)/shard_map/square/pallas_call | solution.py:233
Async XLA Ops:
  0.6 10.3 %collective-permute-start.3 = (bf16[4,3,128,128]{3,2,1,0:T(8,128)(2,1)}, bf16[4,3,128,128]{3,2,1,0:T(8,128)(2,1)S(1)}, u32[]{:S(2)}, u32[]{:S(2)}) collective-permute-start(bf16[4,3,128,128]{3,2,1,0:T(8,128)(2,1)} %bitcast.15), channel_id=1, source_target_pairs={{0,4},{4,0},{1,5},{5,1},{2,6},{6,2},{3,7},{7,3},{8,12},{12,8},{9,1... | collective-permute-start | bytes 1179656 | tf_op jit(solution)/shard_map/ppermute | solution.py:259
  12.0 17.1 %collective-permute-start.4 = (bf16[2,4,3,128,128]{4,3,2,1,0:T(8,128)(2,1)S(1)}, bf16[2,4,3,128,128]{4,3,2,1,0:T(8,128)(2,1)S(1)}, u32[]{:S(2)}, u32[]{:S(2)}) collective-permute-start(bf16[2,4,3,128,128]{4,3,2,1,0:T(8,128)(2,1)S(1)} %pad_maximum_fusion.pair_ref), channel_id=1, source_target_pairs={{0,8},{4,508},{8,16},{12,4},{16,24},{20,12},{24,32},{28,20},{32,40... | collective-permute-start | bytes 2359304 | tf_op jit(solution)/shard_map/ppermute | solution.py:272
  29.1 19.6 %collective-permute-start.6 = (bf16[2,4,3,128,128]{4,3,2,1,0:T(8,128)(2,1)S(1)}, bf16[2,4,3,128,128]{4,3,2,1,0:T(8,128)(2,1)S(1)}, u32[]{:S(2)}, u32[]{:S(2)}) collective-permute-start(bf16[2,4,3,128,128]{4,3,2,1,0:T(8,128)(2,1)S(1)} %collective-permute-done.4.next_ref), channel_id=1, source_target_pairs={{0,8},{4,508},{8,16},{12,4},{16,24},{20,12},{24,32},{28,20},{32,40... | collective-permute-start | bytes 2359304 | tf_op jit(solution)/shard_map/ppermute | solution.py:272
  36.3 49.8 %collective-permute-start.5 = (bf16[2,4,3,128,128]{4,3,2,1,0:T(8,128)(2,1)S(1)}, bf16[2,4,3,128,128]{4,3,2,1,0:T(8,128)(2,1)S(1)}, u32[]{:S(2)}, u32[]{:S(2)}) collective-permute-start(bf16[2,4,3,128,128]{4,3,2,1,0:T(8,128)(2,1)S(1)} %collective-permute-done.4.next_ref), channel_id=1, source_target_pairs={{0,4},{4,0},{1,5},{5,1},{2,6},{6,2},{3,7},{7,3},{8,12},{12,8},{9,1... | collective-permute-start | bytes 2359304 | tf_op jit(solution)/shard_map/ppermute | solution.py:259
  38.2 47.8 %collective-permute-start.2 = (bf16[4,3,128,128]{3,2,1,0:T(8,128)(2,1)}, bf16[4,3,128,128]{3,2,1,0:T(8,128)(2,1)S(1)}, u32[]{:S(2)}, u32[]{:S(2)}) collective-permute-start(bf16[4,3,128,128]{3,2,1,0:T(8,128)(2,1)} %bitcast.17), channel_id=1, source_target_pairs={{3,0},{0,1},{1,2},{2,3},{7,4},{4,5},{5,6},{6,7},{11,8},{8,9},{9,10... | collective-permute-start | bytes 1179656 | tf_op jit(solution)/shard_map/ppermute | solution.py:263
  41.3 44.7 %collective-permute-start.1 = (bf16[4,3,128,128]{3,2,1,0:T(8,128)(2,1)}, bf16[4,3,128,128]{3,2,1,0:T(8,128)(2,1)}, u32[]{:S(2)}, u32[]{:S(2)}) collective-permute-start(bf16[4,3,128,128]{3,2,1,0:T(8,128)(2,1)} %bitcast.18), channel_id=1, source_target_pairs={{2,0},{3,1},{0,2},{1,3},{6,4},{7,5},{4,6},{5,7},{10,8},{11,9},{8,1... | collective-permute-start | bytes 1179656 | tf_op jit(solution)/shard_map/ppermute | solution.py:263
  45.7 40.3 %collective-permute-start = (bf16[4,3,128,128]{3,2,1,0:T(8,128)(2,1)}, bf16[4,3,128,128]{3,2,1,0:T(8,128)(2,1)}, u32[]{:S(2)}, u32[]{:S(2)}) collective-permute-start(bf16[4,3,128,128]{3,2,1,0:T(8,128)(2,1)} %bitcast.19), channel_id=1, source_target_pairs={{1,0},{2,1},{3,2},{0,3},{5,4},{6,5},{7,6},{4,7},{9,8},{10,9},{11,1... | collective-permute-start | bytes 1179656 | tf_op jit(solution)/shard_map/ppermute | solution.py:263
  49.6 36.5 %collective-permute-start.7 = (bf16[4,3,128,128]{3,2,1,0:T(8,128)(2,1)}, bf16[4,3,128,128]{3,2,1,0:T(8,128)(2,1)}, u32[]{:S(2)}, u32[]{:S(2)}) collective-permute-start(bf16[4,3,128,128]{3,2,1,0:T(8,128)(2,1)} %slice_bitcast_fusion), channel_id=1, source_target_pairs={{0,4},{1,5},{2,6},{3,7},{8,12},{9,13},{10,14},{11,15},{16,20},{17,... | collective-permute-start | bytes 1179656 | tf_op jit(solution)/shard_map/ppermute | solution.py:288

commit v6 on v5

--- a/solution.py
+++ b/solution.py
@@ -17,6 +17,10 @@
 WIN = 2 * HP
 ROWS = ("rows_0", "rows_1", "rows_2")
 ROOM = 16
+FAR = 32
+NEAR = 16
+FAR_AXES = ("rows_0", "rows_2")
+NEAR_AXES = ("rows_1", "cols")
 
 
 def place():
@@ -33,8 +37,11 @@
 
 
 def turn_kernel(in_ref, out_ref, table_ref):
-    for n in range(NP):
-        table_ref[n : n + 1, :] = in_ref[n]
+    p0, _ = place()
+    table_ref[...] = jnp.zeros((NP, BS), jnp.int32)
+    for n in range(FAR):
+        spot = 8 * (n // 2) + (p0 & 6) + n % 2
+        table_ref[pl.ds(spot, 1), :] = in_ref[n]
     turned = jnp.transpose(table_ref[...])
     out_ref[...] = jnp.broadcast_to(turned[None, :ROOM], out_ref.shape)
 
@@ -49,7 +56,9 @@
 def index_kernel(tab_ref, cols_ref, starts_ref, map_ref, turned_ref):
     p0, c = place()
     spot = lax.broadcasted_iota(jnp.int32, (GROUPS * ROOM, NP), 1)
-    turned = (tab_ref[...].reshape(GROUPS * ROOM, NP) - spot + HP) & (NP - 1)
+    parts = [tab_ref[GROUPS * n : GROUPS * (n + 1)] for n in range(NEAR // GROUPS)]
+    turned = ((parts[0] + parts[1]) + (parts[2] + parts[3])).reshape(GROUPS * ROOM, NP)
+    turned = (turned - spot + HP) & (NP - 1)
     turned_ref[...] = turned
     panel = lax.broadcasted_iota(jnp.int32, (1, NP), 1)
     wants = []
@@ -193,7 +202,7 @@
 def spread(cols):
     return pl.pallas_call(
         spread_kernel,
-        out_shape=jax.ShapeDtypeStruct((NP, 1, BS), jnp.int32),
+        out_shape=jax.ShapeDtypeStruct((FAR, 1, BS), jnp.int32),
         in_specs=[SMEM],
         out_specs=VMEM,
         compiler_params=pltpu.CompilerParams(vmem_limit_bytes=8 << 20),
@@ -204,7 +213,7 @@
 def turned_table(parts):
     return pl.pallas_call(
         turn_kernel,
-        out_shape=jax.ShapeDtypeStruct((GROUPS, ROOM, BS), jnp.int32),
+        out_shape=jax.ShapeDtypeStruct((NEAR, ROOM, BS), jnp.int32),
         in_specs=[VMEM],
         out_specs=VMEM,
         scratch_shapes=[pltpu.VMEM((NP, BS), jnp.int32)],
@@ -274,8 +283,8 @@
 
 def on_device(blocks, block_cols):
     own = blocks[:, 0]
-    parts = exchange(spread(block_cols[:, 0]), ROWS)
-    table = exchange(turned_table(parts), "cols")
+    parts = exchange(spread(block_cols[:, 0]), FAR_AXES)
+    table = exchange(turned_table(parts), NEAR_AXES)
     columns, starts, where = indices(table)
     partner = swapped(own)
     pair = jnp.stack([own, partner])

time: 93.2 us -> 91.5 us (0.982)
  blocking collectives: 32.6 us -> 31 us
    all_to_all x2, blocking collectives: 32.6 us -> 31 us  [exchange(): return lax.all_to_all(array, axes, 0, 0, tiled=True)]
where the time goes in v6:
time: 91.5 us; the launch traced here: 91.1 us
  starting transfers between devices  37.8 us (41%)
  blocking collectives  31 us (34%)
  waiting for transfers between devices  10.5 us (11%)
  Pallas kernels  8.37 us (9%)
  local copies, waits for them, and re-layouts  1.54 us (2%)
  other arithmetic  1.07 us (1%)
    all_to_all x2, blocking collectives, exchange(): return lax.all_to_all(array, axes, 0, 0, tiled=True)  31 us
    ppermute x2, starting transfers between devices, outward(): return lax.ppermute(pair, ROWS, route)  15.4 us
    ppermute x2, starting transfers between devices, swapped(): return lax.ppermute(block, 'rows_2', [(0, 1), (1, 0)])  10.7 us
    ppermute x3, starting transfers between devices, turned(): lax.ppermute(block, 'cols', [((c + distance) % GROUPS, c) for c in range(...  10.5 us
    ppermute x2, waiting for transfers between devices, outward(): return lax.ppermute(pair, ROWS, route)  8.92 us
    pallas_call x1, Pallas kernels, square(): pl.pallas_call(square_kernel, out_shape=jax.ShapeDtypeStruct((PB, WIDTH,...  6.63 us
  transfers between devices with their start and end apart: 8, of which 2 were waited for; matrix products, arithmetic and copies ran while one was open for 2% of the time, Pallas kernels for 2%

profile of v6, /device:TPU:1, one launch (start us, length us, event | category | flops | bytes accessed | tf_op | source)
XLA Modules:
  0.0 91.1 jit_solution(14076325383738930946)
XLA Ops:
  0.6 8.7 %collective-permute-start.3 = (bf16[4,3,128,128]{3,2,1,0:T(8,128)(2,1)}, bf16[4,3,128,128]{3,2,1,0:T(8,128)(2,1)S(1)}, u32[]{:S(2)}, u32[]{:S(2)}) collective-permute-start(bf16[4,3,128,128]{3,2,1,0:T(8,128)(2,1)} %bitcast.15), channel_id=1, source_target_pairs={{0,4},{4,0},{1,5},{5,1},{2,6},{6,2},{3,7},{7,3},{8,12},{12,8},{9,1... | collective-permute-start | bytes 1179656 | tf_op jit(solution)/shard_map/ppermute | solution.py:268
  9.4 1.5 %collective-permute-done.3 = bf16[4,3,128,128]{3,2,1,0:T(8,128)(2,1)S(1)} collective-permute-done((bf16[4,3,128,128]{3,2,1,0:T(8,128)(2,1)}, bf16[4,3,128,128]{3,2,1,0:T(8,128)(2,1)S(1)}, u32[]{:S(2)}, u32[]{:S(2)}) %collective-permute-start.3) | collective-permute-done | bytes 393248 | tf_op jit(solution)/shard_map/ppermute | solution.py:268
  10.9 1.1 %pad_maximum_fusion.pair_ref = bf16[2,4,3,128,128]{4,3,2,1,0:T(8,128)(2,1)S(1)} fusion(bf16[1,4,3,128,128]{4,3,2,1,0:T(8,128)(2,1)S(1)} %bitcast.20, bf16[1,4,3,128,128]{4,3,2,1,0:T(8,128)(2,1)} %bitcast.16), kind=kLoop, calls=%fused_computation | loop fusion | flops 393216 | bytes 1572864 | tf_op jit(solution)/shard_map/stack | solution.py:290
  12.0 8.2 %collective-permute-start.4 = (bf16[2,4,3,128,128]{4,3,2,1,0:T(8,128)(2,1)S(1)}, bf16[2,4,3,128,128]{4,3,2,1,0:T(8,128)(2,1)S(1)}, u32[]{:S(2)}, u32[]{:S(2)}) collective-permute-start(bf16[2,4,3,128,128]{4,3,2,1,0:T(8,128)(2,1)S(1)} %pad_maximum_fusion.pair_ref), channel_id=1, source_target_pairs={{0,8},{4,508},{8,16},{12,4},{16,24},{20,12},{24,32},{28,20},{32,40... | collective-permute-start | bytes 2359304 | tf_op jit(solution)/shard_map/ppermute | solution.py:281
  20.2 8.9 %collective-permute-done.4.next_ref = bf16[2,4,3,128,128]{4,3,2,1,0:T(8,128)(2,1)S(1)} collective-permute-done((bf16[2,4,3,128,128]{4,3,2,1,0:T(8,128)(2,1)S(1)}, bf16[2,4,3,128,128]{4,3,2,1,0:T(8,128)(2,1)S(1)}, u32[]{:S(2)}, u32[]{:S(2)}) %collective-permute-start.4) | collective-permute-done | bytes 786464 | tf_op jit(solution)/shard_map/ppermute | solution.py:281
  29.1 7.1 %collective-permute-start.6 = (bf16[2,4,3,128,128]{4,3,2,1,0:T(8,128)(2,1)S(1)}, bf16[2,4,3,128,128]{4,3,2,1,0:T(8,128)(2,1)S(1)}, u32[]{:S(2)}, u32[]{:S(2)}) collective-permute-start(bf16[2,4,3,128,128]{4,3,2,1,0:T(8,128)(2,1)S(1)} %collective-permute-done.4.next_ref), channel_id=1, source_target_pairs={{0,8},{4,508},{8,16},{12,4},{16,24},{20,12},{24,32},{28,20},{32,40... | collective-permute-start | bytes 2359304 | tf_op jit(solution)/shard_map/ppermute | solution.py:281
  36.3 1.9 %collective-permute-start.5 = (bf16[2,4,3,128,128]{4,3,2,1,0:T(8,128)(2,1)S(1)}, bf16[2,4,3,128,128]{4,3,2,1,0:T(8,128)(2,1)S(1)}, u32[]{:S(2)}, u32[]{:S(2)}) collective-permute-start(bf16[2,4,3,128,128]{4,3,2,1,0:T(8,128)(2,1)S(1)} %collective-permute-done.4.next_ref), channel_id=1, source_target_pairs={{0,4},{4,0},{1,5},{5,1},{2,6},{6,2},{3,7},{7,3},{8,12},{12,8},{9,1... | collective-permute-start | bytes 2359304 | tf_op jit(solution)/shard_map/ppermute | solution.py:268
  38.2 3.1 %collective-permute-start.2 = (bf16[4,3,128,128]{3,2,1,0:T(8,128)(2,1)}, bf16[4,3,128,128]{3,2,1,0:T(8,128)(2,1)S(1)}, u32[]{:S(2)}, u32[]{:S(2)}) collective-permute-start(bf16[4,3,128,128]{3,2,1,0:T(8,128)(2,1)} %bitcast.17), channel_id=1, source_target_pairs={{3,0},{0,1},{1,2},{2,3},{7,4},{4,5},{5,6},{6,7},{11,8},{8,9},{9,10... | collective-permute-start | bytes 1179656 | tf_op jit(solution)/shard_map/ppermute | solution.py:272
  41.3 4.4 %collective-permute-start.1 = (bf16[4,3,128,128]{3,2,1,0:T(8,128)(2,1)}, bf16[4,3,128,128]{3,2,1,0:T(8,128)(2,1)}, u32[]{:S(2)}, u32[]{:S(2)}) collective-permute-start(bf16[4,3,128,128]{3,2,1,0:T(8,128)(2,1)} %bitcast.18), channel_id=1, source_target_pairs={{2,0},{3,1},{0,2},{1,3},{6,4},{7,5},{4,6},{5,7},{10,8},{11,9},{8,1... | collective-permute-start | bytes 1179656 | tf_op jit(solution)/shard_map/ppermute | solution.py:272
  45.7 3.1 %collective-permute-start = (bf16[4,3,128,128]{3,2,1,0:T(8,128)(2,1)}, bf16[4,3,128,128]{3,2,1,0:T(8,128)(2,1)}, u32[]{:S(2)}, u32[]{:S(2)}) collective-permute-start(bf16[4,3,128,128]{3,2,1,0:T(8,128)(2,1)} %bitcast.19), channel_id=1, source_target_pairs={{1,0},{2,1},{3,2},{0,3},{5,4},{6,5},{7,6},{4,7},{9,8},{10,9},{11,1... | collective-permute-start | bytes 1179656 | tf_op jit(solution)/shard_map/ppermute | solution.py:272
  48.8 0.0 collective-permute-done.6.far_ref
  48.8 0.8 slice_bitcast_fusion
  49.6 1.3 %collective-permute-start.7 = (bf16[4,3,128,128]{3,2,1,0:T(8,128)(2,1)}, bf16[4,3,128,128]{3,2,1,0:T(8,128)(2,1)}, u32[]{:S(2)}, u32[]{:S(2)}) collective-permute-start(bf16[4,3,128,128]{3,2,1,0:T(8,128)(2,1)} %slice_bitcast_fusion), channel_id=1, source_target_pairs={{0,4},{1,5},{2,6},{3,7},{8,12},{9,13},{10,14},{11,15},{16,20},{17,... | collective-permute-start | bytes 1179656 | tf_op jit(solution)/shard_map/ppermute | solution.py:297
  50.8 0.8 copy.5
  51.6 0.6 spread.1
  52.2 20.3 %all_to_all.10.in_ref = s32[32,1,128]{2,1,0:T(1,128)S(1)} all-to-all(s32[32,1,128]{2,1,0:T(1,128)S(1)} %spread.1), channel_id=1, replica_groups=mesh['rows_0'=16,'rows_1'=4,'rows_2'=2,'cols'=4] {'rows_0','rows_2'}, dimensions={0} | all-to-all | bytes 32768 | tf_op jit(solution)/shard_map/all_to_all | solution.py:264
  72.5 0.1 turned_table.1
  72.5 10.8 %all_to_all.11.tab_ref = s32[16,16,128]{2,1,0:T(8,128)S(1)} all-to-all(s32[16,16,128]{2,1,0:T(8,128)S(1)} %turned_table.1), channel_id=1, replica_groups=mesh['rows_0'=16,'rows_1'=4,'rows_2'=2,'cols'=4] {'rows_1','cols'}, dimensions={0} | all-to-all | bytes 262144 | tf_op jit(solution)/shard_map/all_to_all | solution.py:264
  83.3 1.1 %indices.1 = (s32[4,36]{1,0:T(4,128)}, s32[1,4]{1,0:T(1,128)}, s32[16,128]{1,0:T(8,128)S(1)}) custom-call(s32[16,16,128]{2,1,0:T(8,128)S(1)} %all_to_all.11.tab_ref), custom_call_target="tpu_custom_call" | custom-call | tf_op jit(solution)/shard_map/indices/pallas_call | solution.py:226
  84.4 0.0 collective-permute-done.2.down_ref
  84.4 0.0 collective-permute-done.1.over_ref
  84.4 0.0 collective-permute-done.up_ref
  84.4 0.0 collective-permute-done.5.swap_ref
  84.4 0.0 collective-permute-done.7.last_ref
  84.4 6.6 %square.1 = bf16[4,36,128,128]{3,2,1,0:T(8,128)(2,1)} custom-call(s32[16,128]{1,0:T(8,128)S(1)} %get-tuple-element.6.map_ref, bf16[4,3,128,128]{3,2,1,0:T(8,128)(2,1)} %collective-permute-done.up_ref, bf16[4,3,128,128]{3,2,1,0:T(8,128)(2,1)} %collective-permute-done.1.over_ref, bf16[4,3,128,128]{3,2,1,0:T(8,128)(2,1)S(1)} %collective-permute-done.2.down_ref, ...), custom_call_target="tpu_custom_call" | custom-call | tf_op jit(solution)/shard_map/square/pallas_call | solution.py:242
Async XLA Ops:
  0.6 10.3 %collective-permute-start.3 = (bf16[4,3,128,128]{3,2,1,0:T(8,128)(2,1)}, bf16[4,3,128,128]{3,2,1,0:T(8,128)(2,1)S(1)}, u32[]{:S(2)}, u32[]{:S(2)}) collective-permute-start(bf16[4,3,128,128]{3,2,1,0:T(8,128)(2,1)} %bitcast.15), channel_id=1, source_target_pairs={{0,4},{4,0},{1,5},{5,1},{2,6},{6,2},{3,7},{7,3},{8,12},{12,8},{9,1... | collective-permute-start | bytes 1179656 | tf_op jit(solution)/shard_map/ppermute | solution.py:268
  12.0 17.1 %collective-permute-start.4 = (bf16[2,4,3,128,128]{4,3,2,1,0:T(8,128)(2,1)S(1)}, bf16[2,4,3,128,128]{4,3,2,1,0:T(8,128)(2,1)S(1)}, u32[]{:S(2)}, u32[]{:S(2)}) collective-permute-start(bf16[2,4,3,128,128]{4,3,2,1,0:T(8,128)(2,1)S(1)} %pad_maximum_fusion.pair_ref), channel_id=1, source_target_pairs={{0,8},{4,508},{8,16},{12,4},{16,24},{20,12},{24,32},{28,20},{32,40... | collective-permute-start | bytes 2359304 | tf_op jit(solution)/shard_map/ppermute | solution.py:281
  29.1 19.6 %collective-permute-start.6 = (bf16[2,4,3,128,128]{4,3,2,1,0:T(8,128)(2,1)S(1)}, bf16[2,4,3,128,128]{4,3,2,1,0:T(8,128)(2,1)S(1)}, u32[]{:S(2)}, u32[]{:S(2)}) collective-permute-start(bf16[2,4,3,128,128]{4,3,2,1,0:T(8,128)(2,1)S(1)} %collective-permute-done.4.next_ref), channel_id=1, source_target_pairs={{0,8},{4,508},{8,16},{12,4},{16,24},{20,12},{24,32},{28,20},{32,40... | collective-permute-start | bytes 2359304 | tf_op jit(solution)/shard_map/ppermute | solution.py:281
  36.3 48.1 %collective-permute-start.5 = (bf16[2,4,3,128,128]{4,3,2,1,0:T(8,128)(2,1)S(1)}, bf16[2,4,3,128,128]{4,3,2,1,0:T(8,128)(2,1)S(1)}, u32[]{:S(2)}, u32[]{:S(2)}) collective-permute-start(bf16[2,4,3,128,128]{4,3,2,1,0:T(8,128)(2,1)S(1)} %collective-permute-done.4.next_ref), channel_id=1, source_target_pairs={{0,4},{4,0},{1,5},{5,1},{2,6},{6,2},{3,7},{7,3},{8,12},{12,8},{9,1... | collective-permute-start | bytes 2359304 | tf_op jit(solution)/shard_map/ppermute | solution.py:268
  38.2 46.2 %collective-permute-start.2 = (bf16[4,3,128,128]{3,2,1,0:T(8,128)(2,1)}, bf16[4,3,128,128]{3,2,1,0:T(8,128)(2,1)S(1)}, u32[]{:S(2)}, u32[]{:S(2)}) collective-permute-start(bf16[4,3,128,128]{3,2,1,0:T(8,128)(2,1)} %bitcast.17), channel_id=1, source_target_pairs={{3,0},{0,1},{1,2},{2,3},{7,4},{4,5},{5,6},{6,7},{11,8},{8,9},{9,10... | collective-permute-start | bytes 1179656 | tf_op jit(solution)/shard_map/ppermute | solution.py:272
  41.3 43.1 %collective-permute-start.1 = (bf16[4,3,128,128]{3,2,1,0:T(8,128)(2,1)}, bf16[4,3,128,128]{3,2,1,0:T(8,128)(2,1)}, u32[]{:S(2)}, u32[]{:S(2)}) collective-permute-start(bf16[4,3,128,128]{3,2,1,0:T(8,128)(2,1)} %bitcast.18), channel_id=1, source_target_pairs={{2,0},{3,1},{0,2},{1,3},{6,4},{7,5},{4,6},{5,7},{10,8},{11,9},{8,1... | collective-permute-start | bytes 1179656 | tf_op jit(solution)/shard_map/ppermute | solution.py:272
  45.7 38.7 %collective-permute-start = (bf16[4,3,128,128]{3,2,1,0:T(8,128)(2,1)}, bf16[4,3,128,128]{3,2,1,0:T(8,128)(2,1)}, u32[]{:S(2)}, u32[]{:S(2)}) collective-permute-start(bf16[4,3,128,128]{3,2,1,0:T(8,128)(2,1)} %bitcast.19), channel_id=1, source_target_pairs={{1,0},{2,1},{3,2},{0,3},{5,4},{6,5},{7,6},{4,7},{9,8},{10,9},{11,1... | collective-permute-start | bytes 1179656 | tf_op jit(solution)/shard_map/ppermute | solution.py:272
  49.6 34.9 %collective-permute-start.7 = (bf16[4,3,128,128]{3,2,1,0:T(8,128)(2,1)}, bf16[4,3,128,128]{3,2,1,0:T(8,128)(2,1)}, u32[]{:S(2)}, u32[]{:S(2)}) collective-permute-start(bf16[4,3,128,128]{3,2,1,0:T(8,128)(2,1)} %slice_bitcast_fusion), channel_id=1, source_target_pairs={{0,4},{1,5},{2,6},{3,7},{8,12},{9,13},{10,14},{11,15},{16,20},{17,... | collective-permute-start | bytes 1179656 | tf_op jit(solution)/shard_map/ppermute | solution.py:297

commit v7 on v5

--- a/solution.py
+++ b/solution.py
@@ -17,6 +17,8 @@
 WIN = 2 * HP
 ROWS = ("rows_0", "rows_1", "rows_2")
 ROOM = 16
+FLOOR = 512
+ALL_AXES = (*ROWS, "cols")
 
 
 def place():
@@ -24,19 +26,12 @@
 
 
 def spread_kernel(cols_ref, out_ref):
-    lane = lax.broadcasted_iota(jnp.int32, (1, BS), 1)
-    row = jnp.zeros((1, BS), jnp.int32)
+    lane = lax.broadcasted_iota(jnp.int32, (1, FLOOR), 1)
+    row = jnp.zeros((1, FLOOR), jnp.int32)
     for r in range(PB):
         for s in range(KG):
             row = jnp.where(lane == KG * r + s, cols_ref[r, s] >> 2, row)
-    out_ref[...] = jnp.broadcast_to(row[None], out_ref.shape)
-
-
-def turn_kernel(in_ref, out_ref, table_ref):
-    for n in range(NP):
-        table_ref[n : n + 1, :] = in_ref[n]
-    turned = jnp.transpose(table_ref[...])
-    out_ref[...] = jnp.broadcast_to(turned[None, :ROOM], out_ref.shape)
+    out_ref[0] = row
 
 
 def bits_set(x):
@@ -46,10 +41,16 @@
     return (x + (x >> 8)) & 0x1F
 
 
-def index_kernel(tab_ref, cols_ref, starts_ref, map_ref, turned_ref):
+def index_kernel(tab_ref, cols_ref, starts_ref, map_ref, table_ref, turned_ref):
     p0, c = place()
     spot = lax.broadcasted_iota(jnp.int32, (GROUPS * ROOM, NP), 1)
-    turned = (tab_ref[...].reshape(GROUPS * ROOM, NP) - spot + HP) & (NP - 1)
+    for n in range(GROUPS * NP):
+        table_ref[n : n + 1, :] = tab_ref[n, :, :BS]
+    parts = []
+    for g in range(GROUPS):
+        parts.append(jnp.transpose(table_ref[pl.ds(g, NP, stride=GROUPS), :])[:ROOM])
+    turned = jnp.concatenate(parts, axis=0)
+    turned = (turned - spot + HP) & (NP - 1)
     turned_ref[...] = turned
     panel = lax.broadcasted_iota(jnp.int32, (1, NP), 1)
     wants = []
@@ -193,24 +194,12 @@
 def spread(cols):
     return pl.pallas_call(
         spread_kernel,
-        out_shape=jax.ShapeDtypeStruct((NP, 1, BS), jnp.int32),
+        out_shape=jax.ShapeDtypeStruct((1, 1, FLOOR), jnp.int32),
         in_specs=[SMEM],
         out_specs=VMEM,
         compiler_params=pltpu.CompilerParams(vmem_limit_bytes=8 << 20),
         name="spread",
     )(cols)
-
-
-def turned_table(parts):
-    return pl.pallas_call(
-        turn_kernel,
-        out_shape=jax.ShapeDtypeStruct((GROUPS, ROOM, BS), jnp.int32),
-        in_specs=[VMEM],
-        out_specs=VMEM,
-        scratch_shapes=[pltpu.VMEM((NP, BS), jnp.int32)],
-        compiler_params=pltpu.CompilerParams(vmem_limit_bytes=8 << 20),
-        name="turned_table",
-    )(parts)
 
 
 def indices(table):
@@ -223,7 +212,10 @@
         ),
         in_specs=[VMEM],
         out_specs=(VMEM, VMEM, VMEM),
-        scratch_shapes=[pltpu.VMEM((GROUPS * ROOM, NP), jnp.int32)],
+        scratch_shapes=[
+            pltpu.VMEM((GROUPS * NP, BS), jnp.int32),
+            pltpu.VMEM((GROUPS * ROOM, NP), jnp.int32),
+        ],
         compiler_params=pltpu.CompilerParams(vmem_limit_bytes=8 << 20),
         name="indices",
     )(table)
@@ -251,10 +243,6 @@
     )(where, *[near_core(piece) for piece in (*lefts, *pieces)])
 
 
-def exchange(array, axes):
-    return lax.all_to_all(array, axes, 0, 0, tiled=True)
-
-
 def swapped(block):
     return lax.ppermute(block, "rows_2", [(0, 1), (1, 0)])
 
@@ -274,8 +262,7 @@
 
 def on_device(blocks, block_cols):
     own = blocks[:, 0]
-    parts = exchange(spread(block_cols[:, 0]), ROWS)
-    table = exchange(turned_table(parts), "cols")
+    table = lax.all_gather(spread(block_cols[:, 0]), ALL_AXES, axis=0, tiled=True)
     columns, starts, where = indices(table)
     partner = swapped(own)
     pair = jnp.stack([own, partner])

time: 93.2 us -> 209 us (2.24)
  waiting for transfers between devices: 10.5 us -> 144 us
  blocking collectives: 32.6 us -> 0 us
  between operations: 0.74 us -> 14.1 us
    all_gather x0 -> x1, waiting for transfers between devices: none -> 135 us  [on_device(): lax.all_gather(spread(block_cols[:, 0]), ALL_AXES, axis=0, tiled=True)]
    all_to_all x2 -> x0, blocking collectives: 32.6 us -> none  [exchange(): return lax.all_to_all(array, axes, 0, 0, tiled=True)]
  transfers between devices with their start and end apart: 8 -> 9, of which waited for: 2 -> 3; matrix products, arithmetic and copies ran while one was open for 2% -> 1% of each run, Pallas kernels for 2% -> 1%
where the time goes in v7:
time: 209 us
  waiting for transfers between devices  144 us (69%)
  starting transfers between devices  37.9 us (18%)
  between operations  14.1 us (7%)
  Pallas kernels  9.12 us (4%)
  local copies, waits for them, and re-layouts  2.77 us (1%)
    all_gather x1, waiting for transfers between devices, on_device(): lax.all_gather(spread(block_cols[:, 0]), ALL_AXES, axis=0, tiled=True)  135 us
    ppermute x2, starting transfers between devices, outward(): return lax.ppermute(pair, ROWS, route)  15.3 us
    ppermute x2, starting transfers between devices, swapped(): return lax.ppermute(block, 'rows_2', [(0, 1), (1, 0)])  10.7 us
    ppermute x3, starting transfers between devices, turned(): lax.ppermute(block, 'cols', [((c + distance) % GROUPS, c) for c in range(...  10.5 us
    ppermute x2, waiting for transfers between devices, outward(): return lax.ppermute(pair, ROWS, route)  6.96 us
    pallas_call x1, Pallas kernels, square(): pl.pallas_call(square_kernel, out_shape=jax.ShapeDtypeStruct((PB, WIDTH,...  6.64 us
  transfers between devices with their start and end apart: 9, of which 3 were waited for; matrix products, arithmetic and copies ran while one was open for 1% of the time, Pallas kernels for 1%

profile of v7, /device:TPU:1, one launch (start us, length us, event | category | flops | bytes accessed | tf_op | source)
XLA Modules:
  0.0 208.7 jit_solution(13177037804086096757)
XLA Ops:
  7.2 0.0 all-gather.2.cloned.1.call-start
  7.2 8.7 %collective-permute-start.3 = (bf16[4,3,128,128]{3,2,1,0:T(8,128)(2,1)}, bf16[4,3,128,128]{3,2,1,0:T(8,128)(2,1)S(1)}, u32[]{:S(2)}, u32[]{:S(2)}) collective-permute-start(bf16[4,3,128,128]{3,2,1,0:T(8,128)(2,1)} %bitcast.15), channel_id=1, source_target_pairs={{0,4},{4,0},{1,5},{5,1},{2,6},{6,2},{3,7},{7,3},{8,12},{12,8},{9,1... | collective-permute-start | bytes 1179656 | tf_op jit(solution)/shard_map/ppermute | solution.py:247
  16.0 1.5 collective-permute-done.3
  17.5 1.1 pad_maximum_fusion.pair_ref
  18.6 8.2 %collective-permute-start.4 = (bf16[2,4,3,128,128]{4,3,2,1,0:T(8,128)(2,1)S(1)}, bf16[2,4,3,128,128]{4,3,2,1,0:T(8,128)(2,1)S(1)}, u32[]{:S(2)}, u32[]{:S(2)}) collective-permute-start(bf16[2,4,3,128,128]{4,3,2,1,0:T(8,128)(2,1)S(1)} %pad_maximum_fusion.pair_ref), channel_id=1, source_target_pairs={{0,8},{4,508},{8,16},{12,4},{16,24},{20,12},{24,32},{28,20},{32,40... | collective-permute-start | bytes 2359304 | tf_op jit(solution)/shard_map/ppermute | solution.py:260
  26.8 0.8 copy.8
  27.6 1.2 spread.1
  28.7 0.0 all-gather.2.cloned.1.call-update
  28.8 7.0 %collective-permute-done.4.next_ref = bf16[2,4,3,128,128]{4,3,2,1,0:T(8,128)(2,1)S(1)} collective-permute-done((bf16[2,4,3,128,128]{4,3,2,1,0:T(8,128)(2,1)S(1)}, bf16[2,4,3,128,128]{4,3,2,1,0:T(8,128)(2,1)S(1)}, u32[]{:S(2)}, u32[]{:S(2)}) %collective-permute-start.4) | collective-permute-done | bytes 786464 | tf_op jit(solution)/shard_map/ppermute | solution.py:260
  35.7 7.1 %collective-permute-start.6 = (bf16[2,4,3,128,128]{4,3,2,1,0:T(8,128)(2,1)S(1)}, bf16[2,4,3,128,128]{4,3,2,1,0:T(8,128)(2,1)S(1)}, u32[]{:S(2)}, u32[]{:S(2)}) collective-permute-start(bf16[2,4,3,128,128]{4,3,2,1,0:T(8,128)(2,1)S(1)} %collective-permute-done.4.next_ref), channel_id=1, source_target_pairs={{0,8},{4,508},{8,16},{12,4},{16,24},{20,12},{24,32},{28,20},{32,40... | collective-permute-start | bytes 2359304 | tf_op jit(solution)/shard_map/ppermute | solution.py:260
  42.9 1.9 collective-permute-start.5
  44.8 3.1 %collective-permute-start.2 = (bf16[4,3,128,128]{3,2,1,0:T(8,128)(2,1)}, bf16[4,3,128,128]{3,2,1,0:T(8,128)(2,1)S(1)}, u32[]{:S(2)}, u32[]{:S(2)}) collective-permute-start(bf16[4,3,128,128]{3,2,1,0:T(8,128)(2,1)} %bitcast.17), channel_id=1, source_target_pairs={{3,0},{0,1},{1,2},{2,3},{7,4},{4,5},{5,6},{6,7},{11,8},{8,9},{9,10... | collective-permute-start | bytes 1179656 | tf_op jit(solution)/shard_map/ppermute | solution.py:251
  47.9 4.4 %collective-permute-start.1 = (bf16[4,3,128,128]{3,2,1,0:T(8,128)(2,1)}, bf16[4,3,128,128]{3,2,1,0:T(8,128)(2,1)}, u32[]{:S(2)}, u32[]{:S(2)}) collective-permute-start(bf16[4,3,128,128]{3,2,1,0:T(8,128)(2,1)} %bitcast.18), channel_id=1, source_target_pairs={{2,0},{3,1},{0,2},{1,3},{6,4},{7,5},{4,6},{5,7},{10,8},{11,9},{8,1... | collective-permute-start | bytes 1179656 | tf_op jit(solution)/shard_map/ppermute | solution.py:251
  52.3 3.1 %collective-permute-start = (bf16[4,3,128,128]{3,2,1,0:T(8,128)(2,1)}, bf16[4,3,128,128]{3,2,1,0:T(8,128)(2,1)}, u32[]{:S(2)}, u32[]{:S(2)}) collective-permute-start(bf16[4,3,128,128]{3,2,1,0:T(8,128)(2,1)} %bitcast.19), channel_id=1, source_target_pairs={{1,0},{2,1},{3,2},{0,3},{5,4},{6,5},{7,6},{4,7},{9,8},{10,9},{11,1... | collective-permute-start | bytes 1179656 | tf_op jit(solution)/shard_map/ppermute | solution.py:251
  55.4 0.0 collective-permute-done.6.far_ref
  55.4 0.8 slice_bitcast_fusion
  56.1 1.3 collective-permute-start.7
  57.4 135.2 %all-gather.2.cloned.1.call-done.tab_ref = s32[512,1,512]{2,1,0:T(1,128)} async-done(((s32[1,1,512]{2,1,0:T(1,128)}), s32[512,1,512]{2,1,0:T(1,128)}) %all-gather.2.cloned.1.call-update) | async-done | bytes 1048592 | tf_op jit(solution)/shard_map/all_gather | solution.py:265
  192.6 0.0 copy-start
  192.6 1.2 copy-done
  193.8 1.3 indices.1
  195.1 0.0 collective-permute-done.2.down_ref
  195.1 0.0 collective-permute-done.1.over_ref
  195.2 0.0 collective-permute-done.up_ref
  195.2 0.0 collective-permute-done.5.swap_ref
  195.2 0.0 collective-permute-done.7.last_ref
  195.2 6.6 %square.1 = bf16[4,36,128,128]{3,2,1,0:T(8,128)(2,1)} custom-call(s32[16,128]{1,0:T(8,128)S(1)} %get-tuple-element.6.map_ref, bf16[4,3,128,128]{3,2,1,0:T(8,128)(2,1)} %collective-permute-done.up_ref, bf16[4,3,128,128]{3,2,1,0:T(8,128)(2,1)} %collective-permute-done.1.over_ref, bf16[4,3,128,128]{3,2,1,0:T(8,128)(2,1)S(1)} %collective-permute-done.2.down_ref, ...), custom_call_target="tpu_custom_call" | custom-call | tf_op jit(solution)/shard_map/square/pallas_call | solution.py:225
Async XLA Ops:
  7.2 185.4 %all-gather.2.cloned.1.call-start = ((), (), s32[]{:S(2)}) async-start(), calls=%async_computation | async-start | bytes 1050624 | tf_op jit(solution)/shard_map/all_gather | solution.py:265
  7.2 10.3 %collective-permute-start.3 = (bf16[4,3,128,128]{3,2,1,0:T(8,128)(2,1)}, bf16[4,3,128,128]{3,2,1,0:T(8,128)(2,1)S(1)}, u32[]{:S(2)}, u32[]{:S(2)}) collective-permute-start(bf16[4,3,128,128]{3,2,1,0:T(8,128)(2,1)} %bitcast.15), channel_id=1, source_target_pairs={{0,4},{4,0},{1,5},{5,1},{2,6},{6,2},{3,7},{7,3},{8,12},{12,8},{9,1... | collective-permute-start | bytes 1179656 | tf_op jit(solution)/shard_map/ppermute | solution.py:247
  18.6 17.1 %collective-permute-start.4 = (bf16[2,4,3,128,128]{4,3,2,1,0:T(8,128)(2,1)S(1)}, bf16[2,4,3,128,128]{4,3,2,1,0:T(8,128)(2,1)S(1)}, u32[]{:S(2)}, u32[]{:S(2)}) collective-permute-start(bf16[2,4,3,128,128]{4,3,2,1,0:T(8,128)(2,1)S(1)} %pad_maximum_fusion.pair_ref), channel_id=1, source_target_pairs={{0,8},{4,508},{8,16},{12,4},{16,24},{20,12},{24,32},{28,20},{32,40... | collective-permute-start | bytes 2359304 | tf_op jit(solution)/shard_map/ppermute | solution.py:260
  35.7 19.6 %collective-permute-start.6 = (bf16[2,4,3,128,128]{4,3,2,1,0:T(8,128)(2,1)S(1)}, bf16[2,4,3,128,128]{4,3,2,1,0:T(8,128)(2,1)S(1)}, u32[]{:S(2)}, u32[]{:S(2)}) collective-permute-start(bf16[2,4,3,128,128]{4,3,2,1,0:T(8,128)(2,1)S(1)} %collective-permute-done.4.next_ref), channel_id=1, source_target_pairs={{0,8},{4,508},{8,16},{12,4},{16,24},{20,12},{24,32},{28,20},{32,40... | collective-permute-start | bytes 2359304 | tf_op jit(solution)/shard_map/ppermute | solution.py:260
  42.9 152.3 %collective-permute-start.5 = (bf16[2,4,3,128,128]{4,3,2,1,0:T(8,128)(2,1)S(1)}, bf16[2,4,3,128,128]{4,3,2,1,0:T(8,128)(2,1)S(1)}, u32[]{:S(2)}, u32[]{:S(2)}) collective-permute-start(bf16[2,4,3,128,128]{4,3,2,1,0:T(8,128)(2,1)S(1)} %collective-permute-done.4.next_ref), channel_id=1, source_target_pairs={{0,4},{4,0},{1,5},{5,1},{2,6},{6,2},{3,7},{7,3},{8,12},{12,8},{9,1... | collective-permute-start | bytes 2359304 | tf_op jit(solution)/shard_map/ppermute | solution.py:247
  44.8 150.4 %collective-permute-start.2 = (bf16[4,3,128,128]{3,2,1,0:T(8,128)(2,1)}, bf16[4,3,128,128]{3,2,1,0:T(8,128)(2,1)S(1)}, u32[]{:S(2)}, u32[]{:S(2)}) collective-permute-start(bf16[4,3,128,128]{3,2,1,0:T(8,128)(2,1)} %bitcast.17), channel_id=1, source_target_pairs={{3,0},{0,1},{1,2},{2,3},{7,4},{4,5},{5,6},{6,7},{11,8},{8,9},{9,10... | collective-permute-start | bytes 1179656 | tf_op jit(solution)/shard_map/ppermute | solution.py:251
  47.9 147.2 %collective-permute-start.1 = (bf16[4,3,128,128]{3,2,1,0:T(8,128)(2,1)}, bf16[4,3,128,128]{3,2,1,0:T(8,128)(2,1)}, u32[]{:S(2)}, u32[]{:S(2)}) collective-permute-start(bf16[4,3,128,128]{3,2,1,0:T(8,128)(2,1)} %bitcast.18), channel_id=1, source_target_pairs={{2,0},{3,1},{0,2},{1,3},{6,4},{7,5},{4,6},{5,7},{10,8},{11,9},{8,1... | collective-permute-start | bytes 1179656 | tf_op jit(solution)/shard_map/ppermute | solution.py:251
  52.3 142.9 %collective-permute-start = (bf16[4,3,128,128]{3,2,1,0:T(8,128)(2,1)}, bf16[4,3,128,128]{3,2,1,0:T(8,128)(2,1)}, u32[]{:S(2)}, u32[]{:S(2)}) collective-permute-start(bf16[4,3,128,128]{3,2,1,0:T(8,128)(2,1)} %bitcast.19), channel_id=1, source_target_pairs={{1,0},{2,1},{3,2},{0,3},{5,4},{6,5},{7,6},{4,7},{9,8},{10,9},{11,1... | collective-permute-start | bytes 1179656 | tf_op jit(solution)/shard_map/ppermute | solution.py:251
  56.1 139.0 %collective-permute-start.7 = (bf16[4,3,128,128]{3,2,1,0:T(8,128)(2,1)}, bf16[4,3,128,128]{3,2,1,0:T(8,128)(2,1)}, u32[]{:S(2)}, u32[]{:S(2)}) collective-permute-start(bf16[4,3,128,128]{3,2,1,0:T(8,128)(2,1)} %slice_bitcast_fusion), channel_id=1, source_target_pairs={{0,4},{1,5},{2,6},{3,7},{8,12},{9,13},{10,14},{11,15},{16,20},{17,... | collective-permute-start | bytes 1179656 | tf_op jit(solution)/shard_map/ppermute | solution.py:275
  192.6 1.2 copy-start
Sparse Core Ops, SparseCore 0:
  28.9 163.6 all-gather.1
